TPU v7x, 128 devices: a whole 4x4x4 slice. The times are simulated.
128 devices in a mesh: row: 16 (over z, x), col: 8 (over y, core).
Axes of the slice: x: 4, y: 4, z: 4, core: 2. Of those that a mesh axis runs over, the one named last changes fastest.
Arguments:
- pole_values: float32 [65536], P('row'), may hold values from -32768 to 32768, as said below
- weights: float32 [65536], P('row'), may hold values from 0.15 to 0.5
- centers: float32 [65536], P('col'), as said below
- offsets: float32 [65536], P('col'), may hold values from -0.1 to 0.1
- chosen: int32 [2048], replicated, may hold values from 0 to 65535
- column_pole: int32 [2, 32768], P(None, 'row'), may hold values from 0 to 65535, as said below
- eigen_blocks: bfloat16 [6144, 2, 32768], P('col', None, 'row'), may hold values from -6 to 6
Outputs:
- roots_offset: float32 [65536], P('col')
- panel: float32 [6144, 2, 2048], P(('col', 'row'))
Inputs may be any that keep to these rules, and one draw needn't show every extreme that they name: `pole_values`: ascending; consecutive poles differ by 1/4 to 7/4; every pole is a multiple of 1/128. centers[i] is the midpoint of pole_values[i] and pole_values[i + 1]; the last one is the last pole plus 1/2. `chosen`: indices of roots. `column_pole`: each of 0 to 65535 stands once.
All inputs are finite; a program needn't handle non-finite values.
Results may differ from a plain program's by a relative error of at most 0.0021.
Values may be sent and summed in bfloat16 or wider, within the bound.
No kernel may reach another device: no remote copies, remote signals or barrier semaphores. Data moves between devices by JAX's collectives and lax.ppermute only.
A program may use at most 128 MiB of HBM per device.

v0:
```python
import jax
import jax.numpy as jnp
from jax import lax
from jax.sharding import Mesh
from jax.sharding import PartitionSpec as P

ITERS = 3
ROW = ("row_0", "row_1")
COL_ROW = ("col", "row_0", "row_1")


def gather_turned(arrays, axis, dims):
    turned = [jnp.moveaxis(a, dim, 0) for a, dim in zip(arrays, dims)]
    widths = [t[0].size for t in turned]
    both = jnp.concatenate([t.reshape(-1, w) for t, w in zip(turned, widths)], axis=1)
    filled = lax.all_gather(both, axis, axis=0, tiled=True)
    blocks = jnp.split(filled, [sum(widths[:k]) for k in range(1, len(widths))], axis=1)
    return tuple(
        (
            jnp.moveaxis(b.reshape(-1, *t.shape[1:]), 0, dim)
            for b, t, dim in zip(blocks, turned, dims)
        )
    )


def copy_for_each(shard, axis):
    size = lax.axis_size(axis)
    return lax.all_to_all(
        jnp.broadcast_to(shard[None], (size, *shard.shape)), axis, 0, 0, tiled=True
    )


def joined_along(blocks, dim):
    blocks = jnp.moveaxis(blocks, 0, dim)
    lengths = blocks.shape
    return blocks.reshape(*lengths[:dim], lengths[dim] * lengths[dim + 1], *lengths[dim + 2 :])


def gather_directly(shard, axis, dim):
    blocks = copy_for_each(shard, axis)
    return joined_along(blocks, dim)


def by_axis(shard, axes):
    for axis in axes:
        shard = lax.psum(shard, axis)
    return shard


def block_sums(pole_vals, weight_sq, center_vals, offset_vals, block_rows):
    root_count = center_vals.shape[0]
    block_rows = min(block_rows, root_count)
    center_blocks = center_vals.reshape(root_count // block_rows, block_rows)
    offset_blocks = offset_vals.reshape(root_count // block_rows, block_rows)

    def per_block(blocks):
        distance = pole_vals[None, :] - blocks[0][:, None] - blocks[1][:, None]
        inverse = 1.0 / distance
        weighted = weight_sq[None, :] * inverse
        return (
            jnp.sum(weighted, axis=1),
            jnp.sum(weighted * inverse, axis=1),
            jnp.min(jnp.abs(distance), axis=1),
        )

    sums = lax.map(per_block, (center_blocks, offset_blocks))
    return tuple((item.reshape(root_count) for item in sums))


def newton_update(offset_now, sum_inverse, sum_square, nearest):
    limit = 0.5 * nearest
    return offset_now - jnp.clip((1.0 + sum_inverse) / sum_square, -limit, limit)


def cauchy_block(pole_picked, weight_picked, panel_center, panel_offset, inv_norm):
    distance = pole_picked[:, None] - panel_center[None, :] - panel_offset[None, :]
    return (weight_picked[:, None] * (1.0 / distance) * inv_norm[None, :]).astype(jnp.bfloat16)


def on_device(pole_values, weights, centers, offsets, chosen, column_pole, eigen_blocks):
    all_poles, all_weights = gather_turned((pole_values, weights), ROW, (0, 0))
    weight_sq = weights * weights
    per_device = offsets.shape[0] // lax.axis_size(ROW)
    first_root = lax.axis_index(ROW) * per_device
    my_centers = lax.dynamic_slice_in_dim(centers, first_root, per_device)
    my_offsets = lax.dynamic_slice_in_dim(offsets, first_root, per_device)
    all_sq = all_weights * all_weights
    for iteration in range(ITERS):
        sum_inverse, sum_square, nearest = block_sums(all_poles, all_sq, my_centers, my_offsets, 32)
        my_offsets = newton_update(my_offsets, sum_inverse, sum_square, nearest)
    offset_now = gather_directly(my_offsets, ROW, 0)
    full_centers, full_offsets = gather_turned((centers, offset_now), "col", (0, 0))
    panel_center = full_centers[chosen]
    panel_offset = full_offsets[chosen]
    partial_sq = block_sums(pole_values, weight_sq, panel_center, panel_offset, 64)[1]
    norm_sq = by_axis(partial_sq, ROW)
    inv_norm = lax.rsqrt(norm_sq)
    cauchy_halves = []
    for half_index in range(2):
        pole_index = column_pole[half_index]
        cauchy_halves.append(
            cauchy_block(
                all_poles[pole_index], all_weights[pole_index], panel_center, panel_offset, inv_norm
            )
        )
    panel = lax.psum_scatter(
        jnp.stack(
            [
                jnp.dot(
                    eigen_blocks[:, half_index, :],
                    cauchy_halves[half_index],
                    preferred_element_type=jnp.float32,
                )
                for half_index in range(2)
            ],
            axis=1,
        ),
        ROW,
        scatter_dimension=0,
        tiled=True,
    )
    return (offset_now, panel)


def solution(mesh):
    torus = Mesh(mesh.devices.reshape(4, 4, mesh.shape["col"]), ("row_0", "row_1", "col"))
    placed = (P(ROW), P(ROW), P("col"), P("col"), P(), P(None, ROW), P("col", None, ROW))
    return jax.shard_map(
        on_device,
        mesh=torus,
        in_specs=placed,
        out_specs=(P("col"), P(COL_ROW, None, None)),
        check_vma=False,
    )
```

profile of v0, /device:TPU:1, one launch (start us, length us, event | category | flops | bytes accessed | tf_op | source)
XLA Modules:
  0.0 557.3 jit_solution(9556216317746386524)
XLA Ops:
  9.6 21.0 %all_gather.6 = f32[65536,2]{0,1:T(2,128)S(1)} all-gather(f32[4096,2]{0,1:T(2,128)S(1)} %pad_maximum_fusion.2), channel_id=1, replica_groups=mesh['row_0'=4,'row_1'=4,'col'=8] {'row_0','row_1'}, dimensions={0}, use_global_device_ids=true | all-gather | bytes 557056 | tf_op jit(solution)/shard_map/all_gather | solution.py:16
  31.1 46.1 %while.52 = (s32[]{:T(128)}, f32[16,32]{1,0:T(8,128)S(1)}, f32[16,32]{1,0:T(8,128)S(1)}, f32[16,32]{1,0:T(8,128)S(1)}, f32[65536]{0:T(1024)S(1)}, /*index=5*/f32...) while((s32[]{:T(128)}, f32[16,32]{1,0:T(8,128)S(1)}, ...), condition=%wide.region_4.5_spmd, body=%wide.region_0.4_spmd.sunk | while | flops 18874272 | bytes 526325 | solution.py:66
  31.1 2.7 fusion.33
  34.0 2.7 fusion.33
  36.9 2.7 fusion.33
  39.8 2.7 fusion.33
  42.7 2.7 fusion.33
  45.5 2.7 fusion.33
  48.4 2.7 fusion.33
  51.3 2.7 fusion.33
  62.8 2.7 fusion.33
  78.2 46.1 %while.53 = (s32[]{:T(128)}, f32[16,32]{1,0:T(8,128)S(1)}, f32[16,32]{1,0:T(8,128)S(1)}, f32[16,32]{1,0:T(8,128)S(1)}, f32[65536]{0:T(1024)S(1)}, /*index=5*/f32...) while((s32[]{:T(128)}, f32[16,32]{1,0:T(8,128)S(1)}, ...), condition=%wide.region_9.10_spmd, body=%wide.region_5.9_spmd.sunk | while | flops 18874272 | bytes 526325 | solution.py:66
  118.5 2.7 fusion.34
  124.5 46.1 %while.54 = (s32[]{:T(128)}, f32[16,32]{1,0:T(8,128)S(1)}, f32[16,32]{1,0:T(8,128)S(1)}, f32[16,32]{1,0:T(8,128)S(1)}, f32[65536]{0:T(1024)S(1)}, /*index=5*/f32...) while((s32[]{:T(128)}, f32[16,32]{1,0:T(8,128)S(1)}, ...), condition=%wide.region_14.15_spmd, body=%wide.region_10.14_spmd.sunk | while | flops 18874272 | bytes 526325 | solution.py:66
  144.7 2.7 fusion.35
  171.4 4.7 all-to-all-start
  176.2 13.8 %fusion.26 = (bf16[768,1,2048]{2,1,0:T(2,128)(2,1)}, bf16[768,1,2048]{2,1,0:T(2,128)(2,1)}) fusion(bf16[768,2,2048]{2,1,0:T(2,128)(2,1)} %param.21), kind=kLoop, calls=%fused_computation.75 | loop fusion | bytes 12582912 | tf_op jit(solution)/shard_map/slice | solution.py:110
  190.1 11.8 %gather_fusion = f32[2048]{0:T(1024)S(1)} fusion(f32[65536]{0:T(1024)S(1)} %bitcast.100, s32[2048]{0:T(1024)S(1)} %broadcast_clamp_fusion.1), kind=kCustom, calls=%fused_computation | custom fusion | bytes 24576 | tf_op jit(solution)/shard_map/gather | solution.py:103
  201.9 11.8 %gather_fusion.1 = f32[2048]{0:T(1024)S(1)} fusion(f32[65536]{0:T(1024)S(1)} %bitcast.96, s32[2048]{0:T(1024)S(1)} %broadcast_clamp_fusion.1), kind=kCustom, calls=%fused_computation.1 | custom fusion | bytes 24576 | tf_op jit(solution)/shard_map/gather | solution.py:103
  213.7 11.8 %gather_fusion.5 = f32[2048]{0:T(1024)S(1)} fusion(f32[65536]{0:T(1024)S(1)} %bitcast.97, s32[2048]{0:T(1024)S(1)} %broadcast_clamp_fusion), kind=kCustom, calls=%fused_computation.5 | custom fusion | bytes 24576 | tf_op jit(solution)/shard_map/gather | solution.py:103
  225.5 11.8 %gather_fusion.4 = f32[2048]{0:T(1024)S(1)} fusion(f32[65536]{0:T(1024)S(1)} %bitcast.101, s32[2048]{0:T(1024)S(1)} %broadcast_clamp_fusion), kind=kCustom, calls=%fused_computation.4 | custom fusion | bytes 24576 | tf_op jit(solution)/shard_map/gather | solution.py:103
  237.4 19.6 %all_gather.7 = f32[65536,2]{0,1:T(2,128)S(1)} all-gather(f32[8192,2]{0,1:T(2,128)S(1)} %pad_maximum_fusion.1), channel_id=1, replica_groups=mesh['row_0'=4,'row_1'=4,'col'=8] {'col'}, dimensions={0}, use_global_device_ids=true | all-gather | bytes 589824 | tf_op jit(solution)/shard_map/all_gather | solution.py:16
  257.4 11.8 %gather_fusion.2 = f32[2048]{0:T(1024)S(1)} fusion(f32[65536]{0:T(1024)S(1)} %bitcast.103, s32[2048]{0:T(1024)S(1)} %fusion.23), kind=kCustom, calls=%fused_computation.2 | custom fusion | bytes 24576 | tf_op jit(solution)/shard_map/gather | solution.py:93
  269.3 11.8 %gather_fusion.3 = f32[2048]{0:T(1024)S(1)} fusion(f32[65536]{0:T(1024)S(1)} %bitcast.102, s32[2048]{0:T(1024)S(1)} %fusion.23), kind=kCustom, calls=%fused_computation.3 | custom fusion | bytes 24576 | tf_op jit(solution)/shard_map/gather | solution.py:94
  281.1 14.2 %while.55 = (s32[]{:T(128)}, f32[32,64]{1,0:T(8,128)S(1)}, f32[4096]{0:T(1024)S(1)}, f32[4096]{0:T(1024)S(1)}, f32[32,64]{1,0:T(8,128)S(1)}, /*index=5*/f32[32,64]{1,0:T(8,128)S(1)}, s32[]{:T(128)}, s32[]{:T(128)}) while((s32[]{:T(128)}, f32[32,64]{1,0:T(8,128)S(1)}, f32[4096]{0:T(1024)S(1)}, f32[4096]{0:T(1024)S(1)}, ...), condition=%wide.region_17.18_spmd, body=%wide.region_15.17_spmd.sunk | while | flops 1572802 | bytes 35165 | solution.py:66
  295.4 8.9 %psum.14 = f32[2048]{0:T(1024)S(1)} all-reduce(f32[2048]{0:T(1024)S(1)} %reshape.184), channel_id=1, replica_groups=mesh['row_0'=4,'row_1'=4,'col'=8] {'row_0'}, use_global_device_ids=true, to_apply=%region_18.19 | all-reduce | flops 2048 | bytes 16384 | tf_op jit(solution)/shard_map/psum | solution.py:46
  304.3 8.7 %psum.15 = f32[2048]{0:T(1024)S(1)} all-reduce(f32[2048]{0:T(1024)S(1)} %psum.14), channel_id=1, replica_groups=mesh['row_0'=4,'row_1'=4,'col'=8] {'row_1'}, use_global_device_ids=true, to_apply=%region_19.20 | all-reduce | flops 2048 | bytes 16384 | tf_op jit(solution)/shard_map/psum | solution.py:46
  313.0 14.9 %fusion.22 = f32[768,1,2048]{0,2,1:T(8,128)} fusion(f32[2048]{0:T(1024)S(1)} %rsqrt.3, f32[2048]{0:T(1024)S(1)} %gather_fusion.3, f32[2048]{0:T(1024)S(1)} %gather_fusion.2, f32[2048]{0:T(1024)S(1)} %gather_fusion.1, f32[2048]{0:T(1024)S(1)} %gather_fusion, bf16[768,1,2048]{2,1,0:T(2,128)(2,1)} %get-tuple-element.257), kind=kOutput, calls=%fused_computation.52 | convolution fusion | flops 6467616768 | bytes 9478144 | tf_op jit(solution)/shard_map/dot_general | solution.py:109
  327.9 12.2 %fusion.21 = f32[768,1,2048]{0,2,1:T(8,128)} fusion(f32[2048]{0:T(1024)S(1)} %gather_fusion.5, f32[2048]{0:T(1024)S(1)} %gather_fusion.4, f32[2048]{0:T(1024)S(1)} %rsqrt.3, f32[2048]{0:T(1024)S(1)} %gather_fusion.3, f32[2048]{0:T(1024)S(1)} %gather_fusion.2, bf16[768,1,2048]{2,1,0:T(2,128)(2,1)S(1)} %bitcast.105), kind=kOutput, calls=%fused_computation.51 | convolution fusion | flops 6467616768 | bytes 9478144 | tf_op jit(solution)/shard_map/dot_general | solution.py:109
  340.1 10.0 %pad_maximum_fusion = f32[768,2,2048]{0,2,1:T(8,128)} fusion(f32[768,1,2048]{0,2,1:T(8,128)} %fusion.21, f32[768,1,2048]{0,2,1:T(8,128)} %fusion.22), kind=kLoop, calls=%fused_computation.36 | loop fusion | flops 3145728 | bytes 25165824 | tf_op jit(solution)/shard_map/stack | solution.py:107
  350.1 19.4 %copy.18 = f32[768,2,2048]{2,1,0:T(2,128)} copy(f32[768,2,2048]{0,2,1:T(8,128)} %pad_maximum_fusion) | data formatting | bytes 25165824 | tf_op jit(solution)/shard_map/stack | solution.py:107
  371.4 176.4 %all-reduce.3.cloned.1.call-done = f32[768,2,2048]{2,1,0:T(2,128)} async-done(((f32[768,2,2048]{2,1,0:T(2,128)}), f32[768,2,2048]{2,1,0:T(2,128)}) %all-reduce.3.cloned.1.call-update) | async-done | bytes 12582928
  (393 shorter events, 130.1 us)
Async XLA Ops:
  7.2 169.0 %copy-start.4 = (s32[2048]{0:T(1024)S(1)}, s32[2048]{0:T(1024)}, u32[]{:S(2)}) copy-start(s32[2048]{0:T(1024)} %param.19) | copy-start | bytes 24580
  7.2 169.0 %copy-start.3 = (s32[2,2048]{1,0:T(2,128)S(1)}, s32[2,2048]{1,0:T(2,128)}, u32[]{:S(2)}) copy-start(s32[2,2048]{1,0:T(2,128)} %param.20) | copy-start | bytes 49156
  171.4 65.9 %all-to-all-start = ((f32[16,1,512]{2,1,0:T(1,128)}), f32[16,1,512]{2,1,0:T(1,128)S(1)}, u32[]{:S(2)}, u32[]{:S(2)}) async-start(f32[16,1,512]{2,1,0:T(1,128)} %broadcast_in_dim.72), calls=%async_computation | async-start | bytes 65536 | tf_op jit(solution)/shard_map/all_to_all | solution.py:28
  176.1 371.7 %all-reduce.3.cloned.1.call-start = ((), (), s32[]{:S(2)}) async-start(), calls=%async_computation.1 | async-start | bytes 25165824
  176.2 13.9 %copy-start.1 = (f32[4096]{0:T(1024)S(1)}, f32[4096]{0:T(1024)}, u32[]{:S(2)}) copy-start(f32[4096]{0:T(1024)} %param.16) | copy-start | bytes 49156
  213.7 23.6 %copy-start.2 = (f32[8192]{0:T(1024)S(1)}, f32[8192]{0:T(1024)}, u32[]{:S(2)}) copy-start(f32[8192]{0:T(1024)} %param.17) | copy-start | bytes 98308
  257.4 23.7 %copy-start = (f32[4096]{0:T(1024)S(1)}, f32[4096]{0:T(1024)}, u32[]{:S(2)}) copy-start(f32[4096]{0:T(1024)} %param.15) | copy-start | bytes 49156
  269.3 58.6 %slice-start = ((s8[6291456]{0:T(1024)(128)(4,1)}), s8[2097152]{0:T(1024)(128)(4,1)S(1)}, s32[]{:S(2)}) async-start(s8[6291456]{0:T(1024)(128)(4,1)} %bitcast.104), calls=%async_computation.2 | async-start | bytes 4194304
  313.0 14.9 %slice-start.1 = ((s8[6291456]{0:T(1024)(128)(4,1)}), s8[4194304]{0:T(1024)(128)(4,1)S(1)}, s32[]{:S(2)}) async-start(s8[6291456]{0:T(1024)(128)(4,1)} %bitcast.104), calls=%async_computation.3 | async-start | bytes 8388608
  369.5 0.7 copy-start.5
Sparse Core Ops, SparseCore 0:
  369.6 178.0 all-reduce.2
where the time goes:
time: 558 us; the launch traced here: 557 us
  waiting for transfers between devices  176 us (32%)
  other arithmetic  155 us (28%)
  local copies, waits for them, and re-layouts  119 us (21%)
  blocking collectives  58.2 us (10%)
  matrix products  27 us (5%)
  between operations  15 us (3%)
    unnamed x2, waiting for transfers between devices  176 us
    reduce_sum x80, other arithmetic, per_block(): jnp.sum(weighted * inverse, axis=1)  143 us
    all_gather x2, blocking collectives, gather_turned(): filled = lax.all_gather(both, axis, axis=0, tiled=True)  40.6 us
    dot_general x2, matrix products, on_device(): jnp.dot(eigen_blocks[:, half_index, :], cauchy_halves[half_index], prefer...  27 us
    gather x2, local copies, waits for them, and re-layouts, on_device(): all_weights[pole_index]  23.6 us
    gather x2, local copies, waits for them, and re-layouts, on_device(): all_poles[pole_index]  23.6 us
    another operation x1, local copies, waits for them, and re-layouts, on_device(): jnp.stack([jnp.dot(eigen_blocks[:, half_index, :], cauchy_halves[half_ind...  19.4 us
    psum x2, blocking collectives, by_axis(): shard = lax.psum(shard, axis)  17.6 us
  transfers between devices with their start and end apart: 2, of which 1 were waited for; matrix products, arithmetic and copies ran while one was open for 11% of the time, Pallas kernels for 0%

commit v1 on v0

v1 whole, which is shorter than its diff:
```python
import jax
import jax.numpy as jnp
from jax import lax
from jax.experimental import pallas as pl
from jax.experimental.pallas import tpu as pltpu
from jax.sharding import Mesh
from jax.sharding import PartitionSpec as P

ITERS = 3
ROW = ("z", "x")
COL = ("y", "core")
ALL = ("z", "x", "y", "core")
F32 = jnp.float32
BF16 = jnp.bfloat16
LANES = 128
GROUP = 64
UNROLL = 32
SPLIT = 3


def cost(flops):
    return pl.CostEstimate(flops=int(flops), bytes_accessed=1 << 20, transcendentals=0)


def column(row):
    return jnp.broadcast_to(row, (LANES, LANES)).T


def load_tables(pw_ref, w2_ref):
    parts, _, rows, _ = pw_ref.shape
    for part in range(parts):
        w = pw_ref[part, 1]
        w2_ref[part * rows : (part + 1) * rows, :] = w * w


def shift_poles(pw_ref, ps_ref, base):
    parts, _, rows, _ = pw_ref.shape
    for part in range(parts):
        ps_ref[part * rows : (part + 1) * rows, :] = pw_ref[part, 0] - base


def root_kernel(pw_ref, root_ref, out_ref, w2_ref, ps_ref, c_ref, t_ref, lo_ref, hi_ref):
    load_tables(pw_ref, w2_ref)
    n_rows = root_ref.shape[1]
    for k in range(n_rows):
        here = pl.ds(k * LANES, LANES)
        c_ref[here, :] = column(root_ref[0, k : k + 1, :])
        t_ref[here, :] = column(root_ref[1, k : k + 1, :])
        lo_ref[here, :] = column(root_ref[2, k : k + 1, :])
        hi_ref[here, :] = column(root_ref[3, k : k + 1, :])

    def group_body(g, carry):
        here = pl.ds(g * GROUP, GROUP)
        c = c_ref[here, :]
        base = c_ref[pl.ds(g * GROUP + GROUP // 2, 1), :]
        shift_poles(pw_ref, ps_ref, base)
        near = c - base

        def step(_, carry):
            t = t_ref[here, :]
            s = near + t

            def body(r, sums):
                first, second = sums
                for u in range(UNROLL):
                    row = pl.ds(r * UNROLL + u, 1)
                    inverse = 1.0 / (ps_ref[row, :] - s)
                    weighted = w2_ref[row, :] * inverse
                    first = first + weighted
                    second = second + weighted * inverse
                return first, second

            zero = jnp.zeros((GROUP, LANES), F32)
            first, second = lax.fori_loop(0, ps_ref.shape[0] // UNROLL, body, (zero, zero))
            sum_inverse = jnp.sum(first, axis=1, keepdims=True)
            sum_square = jnp.sum(second, axis=1, keepdims=True)
            nearest = jnp.minimum(jnp.abs(lo_ref[here, :] - t), jnp.abs(hi_ref[here, :] - t))
            limit = 0.5 * nearest
            t_ref[here, :] = t - jnp.clip((1.0 + sum_inverse) / sum_square, -limit, limit)
            return carry

        lax.fori_loop(0, ITERS, step, 0)
        return carry

    lax.fori_loop(0, n_rows * LANES // GROUP, group_body, 0)
    for k in range(n_rows):
        out_ref[k : k + 1, :] = t_ref[pl.ds(k * LANES, LANES), :].T[0:1, :]


def find_roots(pw, root):
    n_rows = root.shape[1]
    n_pole_rows = pw.shape[0] * pw.shape[2]
    roots = n_rows * LANES
    return pl.pallas_call(
        root_kernel,
        out_shape=jax.ShapeDtypeStruct((n_rows, LANES), F32),
        scratch_shapes=[pltpu.VMEM((n_pole_rows, LANES), F32)] * 2
        + [pltpu.VMEM((roots, LANES), F32)] * 4,
        cost_estimate=cost(ITERS * roots * n_pole_rows * LANES * 10),
        name="find_roots",
    )(pw, root)


def panel_kernel(pw_ref, root_ref, out_ref, w2_ref):
    load_tables(pw_ref, w2_ref)
    parts, _, rows, _ = pw_ref.shape
    count = 16
    c = column(root_ref[0:1, :])[:count]
    t = column(root_ref[1:2, :])[:count]
    unroll = 16
    per_part = rows // unroll

    def sums_at(t):
        def body(r, sums):
            first, second, nearest = sums
            part = r // per_part
            start = (r % per_part) * unroll
            for u in range(unroll):
                distance = (pw_ref[part, 0, pl.ds(start + u, 1), :] - c) - t
                inverse = 1.0 / distance
                weighted = w2_ref[pl.ds(r * unroll + u, 1), :] * inverse
                first = first + weighted
                second = second + weighted * inverse
                nearest = jnp.minimum(nearest, jnp.abs(distance))
            return first, second, nearest

        zero = jnp.zeros((count, LANES), F32)
        first, second, nearest = lax.fori_loop(
            0, parts * per_part, body, (zero, zero, jnp.full((count, LANES), 3e38, F32))
        )
        return (
            jnp.sum(first, axis=1, keepdims=True),
            jnp.sum(second, axis=1, keepdims=True),
            jnp.min(nearest, axis=1, keepdims=True),
        )

    for _ in range(ITERS):
        sum_inverse, sum_square, nearest = sums_at(t)
        limit = 0.5 * nearest
        t = t - jnp.clip((1.0 + sum_inverse) / sum_square, -limit, limit)
    norm = lax.rsqrt(sums_at(t)[1])
    pad = jnp.zeros((LANES - count, LANES), F32)
    out_ref[0:1, :] = jnp.concatenate([t, pad], axis=0).T[0:1, :]
    out_ref[1:2, :] = jnp.concatenate([jnp.broadcast_to(norm, (count, LANES)), pad], axis=0).T[0:1, :]


def panel_roots(pw, root):
    n_pole_rows = pw.shape[0] * pw.shape[2]
    return pl.pallas_call(
        panel_kernel,
        out_shape=jax.ShapeDtypeStruct((2, LANES), F32),
        scratch_shapes=[pltpu.VMEM((n_pole_rows, LANES), F32)],
        cost_estimate=cost(4 * 20 * n_pole_rows * LANES * 10),
        name="panel_roots",
    )(pw, root)


def pick_kernel(index_ref, pw_ref, out_ref):
    parts, _, rows, _ = pw_ref.shape
    index = jnp.concatenate([index_ref[...], index_ref[...]], axis=0)
    row = index // LANES
    lane = index % LANES
    unroll = 16
    per_part = rows // unroll

    def body(r, carry):
        p, w = carry
        part = r // per_part
        start = (r % per_part) * unroll
        for u in range(unroll):
            hit = row == r * unroll + u
            p_row = jnp.broadcast_to(pw_ref[part, 0, pl.ds(start + u, 1), :], (8, LANES))
            w_row = jnp.broadcast_to(pw_ref[part, 1, pl.ds(start + u, 1), :], (8, LANES))
            p = jnp.where(hit, jnp.take_along_axis(p_row, lane, axis=1), p)
            w = jnp.where(hit, jnp.take_along_axis(w_row, lane, axis=1), w)
        return p, w

    zero = jnp.zeros((8, LANES), F32)
    p, w = lax.fori_loop(0, parts * per_part, body, (zero, zero))
    out_ref[0] = p[:4]
    out_ref[1] = w[:4]


def pick_columns(index, pw):
    return pl.pallas_call(
        pick_kernel,
        out_shape=jax.ShapeDtypeStruct((2, 4, LANES), F32),
        cost_estimate=cost(5e7),
        name="pick_columns",
    )(index, pw)


def matmul_kernel(
    col_ref, root_ref, e0, e1, e2, e3, own_ref, send_ref, p_ref, w_ref, tile_a, tile_b, acc_ref
):
    blocks = (e0, e1, e2, e3)
    halves, rows, depth = e0.shape
    chunk = tile_a.shape[1]
    chunks = root_ref.shape[1] // chunk
    pieces = depth // LANES
    for piece in range(p_ref.shape[0] // LANES):
        here = pl.ds(piece * LANES, LANES)
        p_ref[here, :] = column(col_ref[0, piece : piece + 1, :])
        w_ref[here, :] = column(col_ref[1, piece : piece + 1, :])

    def fill(tile, src, half, k):
        for part in range(chunk // LANES):
            lanes = pl.ds(k * chunk + part * LANES, LANES)
            c = root_ref[0:1, lanes]
            t = root_ref[1:2, lanes]
            n = root_ref[2:3, lanes]
            for piece in range(pieces):
                here = pl.ds((src * halves + half) * depth + piece * LANES, LANES)
                distance = (p_ref[here, :] - c) - t
                value = w_ref[here, :] * (1.0 / distance) * n
                tile[piece * LANES : (piece + 1) * LANES, part * LANES : (part + 1) * LANES] = (
                    value.astype(BF16)
                )

    def product(src, half, tile):
        return jnp.dot(blocks[src][half], tile[...], preferred_element_type=F32)

    steps = halves * chunks
    fill(tile_a, 0, 0, 0)

    def body(i, carry):
        half = i // chunks
        k = i % chunks
        following = jnp.minimum(i + 1, steps - 1)
        fill(tile_b, 1, half, k)
        acc_ref[...] = product(0, half, tile_a)
        fill(tile_a, 2, half, k)
        acc_ref[...] += product(1, half, tile_b)
        fill(tile_b, 3, half, k)
        acc_ref[...] += product(2, half, tile_a)
        fill(tile_a, 0, following // chunks, following % chunks)
        acc = acc_ref[...] + product(3, half, tile_b)
        quarter = rows // 4
        for part in range(4):
            piece = acc[part * quarter : (part + 1) * quarter]
            own_ref[part, half, :, pl.ds(k * chunk, chunk)] = piece
            send_ref[part, half, :, pl.ds(k * chunk, chunk)] = piece.astype(BF16)
        return carry

    lax.fori_loop(0, steps, body, 0)


def panel_product(columns, root, blocks):
    halves, rows, depth = blocks[0].shape
    n_roots = root.shape[1]
    chunk = 256
    shape = (4, halves, rows // 4, n_roots)
    return pl.pallas_call(
        matmul_kernel,
        out_shape=(jax.ShapeDtypeStruct(shape, F32), jax.ShapeDtypeStruct(shape, BF16)),
        scratch_shapes=[pltpu.VMEM((4 * halves * depth, LANES), F32)] * 2
        + [pltpu.VMEM((depth, chunk), BF16)] * 2
        + [pltpu.VMEM((rows, chunk), F32)],
        cost_estimate=cost(2 * 4 * halves * rows * depth * n_roots),
        name="panel_product",
    )(columns, root, *blocks)


def copies(value, axis):
    size = lax.axis_size(axis)
    return lax.all_to_all(
        jnp.broadcast_to(value[None], (size, *value.shape)), axis, 0, 0, tiled=True
    )


def ring(shift):
    return [(i, (i + shift) % 4) for i in range(4)]


def on_device(pole_values, weights, centers, offsets, chosen, column_pole, eigen_blocks):
    z = lax.axis_index("z")
    x = lax.axis_index("x")
    row = z * 4 + x
    col = lax.axis_index("y") * 2 + lax.axis_index("core")
    n_col = centers.shape[0]
    n_own = n_col // 16

    parted = jnp.stack([pole_values.reshape(-1, LANES), weights.reshape(-1, LANES)])
    pw = copies(parted, ROW)

    turned = jnp.moveaxis(eigen_blocks.reshape(4, -1, 2, eigen_blocks.shape[2]), 2, 1)
    blocks = [lax.dynamic_index_in_dim(turned, z, 0, keepdims=False)]
    for shift in (1, 2, 3):
        block = lax.dynamic_index_in_dim(turned, (z + shift) % 4, 0, keepdims=False)
        blocks.append(lax.ppermute(block, "z", ring(shift)))

    wanted = lax.dynamic_slice_in_dim(chosen, row * LANES, LANES)
    local = wanted - col * n_col
    hit = local[:, None] == lax.broadcasted_iota(jnp.int32, (1, n_col), 1)
    first = jnp.stack(
        [
            jnp.sum(jnp.where(hit, centers[None, :], 0.0), axis=1),
            jnp.sum(jnp.where(hit, offsets[None, :], 0.0), axis=1),
        ]
    )
    spread = jnp.moveaxis(first.reshape(2, 8, 16), 1, 0)
    mine = jnp.sum(lax.all_to_all(spread, COL, 0, 0, tiled=True), axis=0)
    panel_start = jnp.pad(mine, ((0, 0), (0, LANES - 16)), constant_values=0.25)
    panel_end = panel_roots(pw, panel_start)

    index = lax.dynamic_slice_in_dim(column_pole.reshape(-1, LANES), col * 4, 4)
    picked = pick_columns(index, pw)

    note = jnp.concatenate([picked.reshape(8, LANES), panel_start[:1], panel_end], axis=0)
    notes = copies(note, ALL)
    columns = lax.dynamic_index_in_dim(
        notes[:, :8].reshape(4, 4, 8, 2, 4, LANES), x, 1, keepdims=False
    )
    columns = jnp.concatenate(
        [lax.dynamic_slice_in_dim(jnp.concatenate([columns, columns]), (z - s) % 4, 1) for s in range(4)]
    )
    columns = jnp.moveaxis(columns, 2, 0).reshape(2, -1, LANES)
    panel_root = jnp.moveaxis(notes[:, 8:, :16], 1, 0).reshape(3, -1)

    start = col * n_col + row * n_own
    my_centers = lax.dynamic_slice_in_dim(centers, row * n_own, n_own)
    my_offsets = lax.dynamic_slice_in_dim(offsets, row * n_own, n_own)
    part = start // pole_values.shape[0]
    own_poles = lax.dynamic_slice(
        pw.reshape(16, 2, -1), (part, 0, start - part * pole_values.shape[0]), (1, 1, n_own)
    ).reshape(n_own)
    low = own_poles - my_centers
    last = start + jnp.arange(n_own) == pole_values.shape[0] * 16 - 1
    high = jnp.where(last, 3e38, -low)
    mine = jnp.stack([my_centers, my_offsets, low, high]).reshape(4, -1, LANES)
    roots_a = find_roots(pw, mine[:, :SPLIT])

    own, send = panel_product(columns, panel_root, blocks)
    pieces = [lax.dynamic_index_in_dim(own, x, 0, keepdims=False)]
    for shift in (1, 2, 3):
        piece = lax.dynamic_index_in_dim(send, (x + shift) % 4, 0, keepdims=False)
        pieces.append(lax.ppermute(piece, "x", ring(shift)))

    roots_b = find_roots(pw, mine[:, SPLIT:])
    panel = pieces[0] + pieces[1] + pieces[2] + pieces[3]
    panel = jnp.moveaxis(panel, 0, 1)
    roots = copies(jnp.concatenate([roots_a, roots_b]), ROW)
    return roots.reshape(-1), panel


def solution(mesh):
    torus = Mesh(mesh.devices.reshape(4, 4, 4, 2), ALL)
    placed = (P(ROW), P(ROW), P(COL), P(COL), P(), P(None, ROW), P(COL, None, ROW))
    return jax.shard_map(
        on_device,
        mesh=torus,
        in_specs=placed,
        out_specs=(P(COL), P(COL + ROW, None, None)),
        check_vma=False,
    )
```

time: 558 us -> 281 us (0.50)
  Pallas kernels: 0 us -> 152 us
  other arithmetic: 155 us -> 9.03 us
  waiting for transfers between devices: 176 us -> 52.8 us
  local copies, waits for them, and re-layouts: 119 us -> 24.1 us
  blocking collectives: 58.2 us -> 12 us
  matrix products: 27 us -> 0 us
  starting transfers between devices: 4.71 us -> 28.8 us
  between operations: 15 us -> 0.92 us
    unnamed x2 -> x0, waiting for transfers between devices: 176 us -> none
    pallas_call x0 -> x5, Pallas kernels: none -> 152 us  [the longest x2 87.9 us: find_roots(): pl.pallas_call(root_kernel, out_shape=jax.ShapeDtypeStruct((n_rows, LANES...]
    reduce_sum x80 -> x2, other arithmetic: 143 us -> 2.16 us  [the longest x1 2.14 us: on_device(): jnp.sum(jnp.where(hit, centers[None, :], 0.0), axis=1)]
    gather x6 -> x0, local copies, waits for them, and re-layouts: 70.7 us -> none  [the longest x2 23.6 us: on_device(): all_weights[pole_index]]
    all_to_all x1 -> x3, waiting for transfers between devices: 0.01 us -> 52.8 us  [the longest x2 48.9 us: copies(): lax.all_to_all(jnp.broadcast_to(value[None], (size, *value.shape)), axis,...]
    all_gather x2 -> x0, blocking collectives: 40.6 us -> none  [gather_turned(): filled = lax.all_gather(both, axis, axis=0, tiled=True)]
    dot_general x2 -> x0, matrix products: 27 us -> none  [on_device(): jnp.dot(eigen_blocks[:, half_index, :], cauchy_halves[half_index], prefer...]
    psum x2 -> x0, blocking collectives: 17.6 us -> none  [by_axis(): shard = lax.psum(shard, axis)]
  transfers between devices with their start and end apart: 2 -> 9, of which waited for: 1 -> 2; matrix products, arithmetic and copies ran while one was open for 11% -> 8% of each run, Pallas kernels for 0% -> 36%
where the time goes in v1:
time: 281 us; the launch traced here: 279 us
  Pallas kernels  152 us (54%)
  waiting for transfers between devices  52.8 us (19%)
  starting transfers between devices  28.8 us (10%)
  local copies, waits for them, and re-layouts  24.1 us (9%)
  blocking collectives  12 us (4%)
  other arithmetic  9.03 us (3%)
    pallas_call x2, Pallas kernels, find_roots(): pl.pallas_call(root_kernel, out_shape=jax.ShapeDtypeStruct((n_rows, LANES...  87.9 us
    pallas_call x1, Pallas kernels, panel_product(): pl.pallas_call(matmul_kernel, out_shape=(jax.ShapeDtypeStruct(shape, F32)...  50.3 us
    all_to_all x2, waiting for transfers between devices, copies(): lax.all_to_all(jnp.broadcast_to(value[None], (size, *value.shape)), axis,...  48.9 us
    all_to_all x2, starting transfers between devices, copies(): lax.all_to_all(jnp.broadcast_to(value[None], (size, *value.shape)), axis,...  14.1 us
    all_to_all x1, blocking collectives, copies(): lax.all_to_all(jnp.broadcast_to(value[None], (size, *value.shape)), axis,...  12 us
    unnamed x14, local copies, waits for them, and re-layouts  10.1 us
    pallas_call x1, Pallas kernels, panel_roots(): pl.pallas_call(panel_kernel, out_shape=jax.ShapeDtypeStruct((2, LANES), F...  8.48 us
    another operation x1, local copies, waits for them, and re-layouts  6.89 us
  transfers between devices with their start and end apart: 9, of which 2 were waited for; matrix products, arithmetic and copies ran while one was open for 8% of the time, Pallas kernels for 36%

profile of v1, /device:TPU:1, one launch (start us, length us, event | category | flops | bytes accessed | tf_op | source)
XLA Modules:
  0.0 279.4 jit_solution(10850269130480037672)
XLA Ops:
  0.6 0.8 dynamic-slice_subtract_fusion.1
  1.4 2.1 select_reduce_fusion.1
  4.3 6.0 %all-to-all-start.2 = ((f32[8,2,16]{2,1,0:T(2,128)}), f32[8,2,16]{2,1,0:T(2,128)S(1)}, u32[]{:S(2)}, u32[]{:S(2)}) async-start(f32[8,2,16]{2,1,0:T(2,128)} %copy.26), calls=%async_computation.2 | async-start | bytes 16384 | tf_op jit(solution)/shard_map/all_to_all | solution.py:302
  10.3 0.7 pad_maximum_fusion.1
  11.0 3.9 %all-to-all-done.2 = f32[8,2,16]{2,1,0:T(2,128)S(1)} async-done(((f32[8,2,16]{2,1,0:T(2,128)}), f32[8,2,16]{2,1,0:T(2,128)S(1)}, u32[]{:S(2)}, u32[]{:S(2)}) %all-to-all-start.2) | async-done | bytes 1056 | tf_op jit(solution)/shard_map/all_to_all | solution.py:302
  14.9 0.9 broadcast_in_dim.43
  15.8 7.6 %all-to-all-start = ((f32[16,2,32,128]{3,2,1,0:T(8,128)}), f32[16,2,32,128]{3,2,1,0:T(8,128)S(1)}, u32[]{:S(2)}, u32[]{:S(2)}) async-start(f32[16,2,32,128]{3,2,1,0:T(8,128)} %broadcast_in_dim.43), calls=%async_computation | async-start | bytes 1048576 | tf_op jit(solution)/shard_map/all_to_all | solution.py:266
  23.4 6.9 %constant_dynamic-slice_fusion = (bf16[1,192,2,2048]{3,2,1,0:T(2,128)(2,1)S(1)}, bf16[1,192,2,2048]{3,2,1,0:T(2,128)(2,1)S(1)}, bf16[1,192,2,2048]{3,2,1,0:T(2,128)(2,1)S(1)}, bf16[1,192,2,2048]{3,2,1,0:T(2,128)(2,1)S(1)}) fusion(bf16[4,192,2,2048]{3,2,1,0:T(2,128)(2,1)} %bitcast.63, s32[]{:T(128)S(6)} %select_n.139, s32[]{:T(128)S(6)} %select_n.137, ...), kind=kLoop, calls=%fused_computation.33 | loop fusion | bytes 12582928 | tf_op jit(solution)/shard_map/dynamic-slice.3
  30.3 1.8 copy.48
  32.0 1.4 collective-permute-start
  33.4 1.8 copy.47
  35.2 2.4 collective-permute-start.1
  37.6 1.9 copy.46
  39.4 1.2 collective-permute-start.2
  41.8 0.8 copy-done
  42.6 5.0 %pick_columns.1 = f32[2,4,128]{2,1,0:T(4,128)} custom-call(s32[4,128]{1,0:T(4,128)} %constant_dynamic-slice_fusion.5.index_ref, f32[16,2,32,128]{3,2,1,0:T(8,128)} %copy-done), custom_call_target="tpu_custom_call" | custom-call | flops 50000000 | bytes 1048576 | tf_op jit(solution)/shard_map/pick_columns/pallas_call | solution.py:185
  47.6 8.5 %panel_roots.1 = f32[2,128]{1,0:T(2,128)} custom-call(f32[16,2,32,128]{3,2,1,0:T(8,128)} %copy-done, f32[2,128]{1,0:T(2,128)} %pad.4.root_ref), custom_call_target="tpu_custom_call" | custom-call | flops 52428800 | bytes 1048576 | tf_op jit(solution)/shard_map/panel_roots/pallas_call | solution.py:149
  56.8 1.0 broadcast_in_dim.49
  57.8 6.5 %all-to-all-start.3 = ((f32[128,11,128]{2,1,0:T(8,128)}), f32[128,11,128]{2,1,0:T(8,128)S(1)}, u32[]{:S(2)}, u32[]{:S(2)}) async-start(f32[128,11,128]{2,1,0:T(8,128)} %broadcast_in_dim.49), calls=%async_computation.3 | async-start | bytes 2097152 | tf_op jit(solution)/shard_map/all_to_all | solution.py:266
  64.6 1.8 copy.49
  66.3 0.8 dynamic-slice_bitcast_fusion.3
  67.4 0.8 fusion.7
  68.2 48.9 %all-to-all-done.3 = f32[128,11,128]{2,1,0:T(8,128)S(1)} async-done(((f32[128,11,128]{2,1,0:T(8,128)}), f32[128,11,128]{2,1,0:T(8,128)S(1)}, u32[]{:S(2)}, u32[]{:S(2)}) %all-to-all-start.3) | async-done | bytes 720928 | tf_op jit(solution)/shard_map/all_to_all | solution.py:266
  117.1 0.8 reshape.58.root_ref
  118.7 50.3 %panel_product.1 = (f32[4,2,48,2048]{3,2,1,0:T(8,128)}, bf16[4,2,48,2048]{3,2,1,0:T(8,128)(2,1)}) custom-call(f32[2,128,128]{2,1,0:T(8,128)} %bitcast.66, f32[3,2048]{1,0:T(4,128)} %reshape.58.root_ref, bf16[2,192,2048]{2,1,0:T(8,128)(2,1)} %bitcast.64, bf16[2,192,2048]{2,1,0:T(8,128)(2,1)} %collective-permute-done.e1, ...), custom_call_target="tpu_custom_call" | custom-call | flops 12884901888 | bytes 1048576 | tf_op jit(solution)/shard_map/panel_product/pallas_call | solution.py:253
  169.0 1.3 dynamic-slice_bitcast_fusion.2
  170.3 2.6 collective-permute-start.5
  174.7 22.9 %find_roots.3 = f32[1,128]{1,0:T(1,128)} custom-call(f32[16,2,32,128]{3,2,1,0:T(8,128)} %copy-done, f32[4,1,128]{2,1,0:T(1,128)} %pad_maximum_fusion.4.root_ref), custom_call_target="tpu_custom_call" | custom-call | flops 251658240 | bytes 1048576 | tf_op jit(solution)/shard_map/find_roots/pallas_call | solution.py:94
  198.2 65.1 %find_roots.2 = f32[3,128]{1,0:T(4,128)} custom-call(f32[16,2,32,128]{3,2,1,0:T(8,128)} %copy-done, f32[4,3,128]{2,1,0:T(4,128)} %bitcast.71), custom_call_target="tpu_custom_call" | custom-call | flops 754974720 | bytes 1048576 | tf_op jit(solution)/shard_map/find_roots/pallas_call | solution.py:94
  263.9 12.0 %all_to_all.20 = f32[16,4,128]{2,1,0:T(4,128)S(1)} all-to-all(f32[16,4,128]{2,1,0:T(4,128)S(1)} %broadcast_in_dim.45), channel_id=1, replica_groups=mesh['z'=4,'x'=4,'y'=4,'core'=2] {'z','x'}, dimensions={0} | all-to-all | bytes 65536 | tf_op jit(solution)/shard_map/all_to_all | solution.py:266
  276.0 1.3 fusion.2
  277.3 1.5 copy.34
  (39 shorter events, 7.4 us)
Async XLA Ops:
  4.3 10.6 %all-to-all-start.2 = ((f32[8,2,16]{2,1,0:T(2,128)}), f32[8,2,16]{2,1,0:T(2,128)S(1)}, u32[]{:S(2)}, u32[]{:S(2)}) async-start(f32[8,2,16]{2,1,0:T(2,128)} %copy.26), calls=%async_computation.2 | async-start | bytes 16384 | tf_op jit(solution)/shard_map/all_to_all | solution.py:302
  15.8 26.0 %all-to-all-start = ((f32[16,2,32,128]{3,2,1,0:T(8,128)}), f32[16,2,32,128]{3,2,1,0:T(8,128)S(1)}, u32[]{:S(2)}, u32[]{:S(2)}) async-start(f32[16,2,32,128]{3,2,1,0:T(8,128)} %broadcast_in_dim.43), calls=%async_computation | async-start | bytes 1048576 | tf_op jit(solution)/shard_map/all_to_all | solution.py:266
  32.0 86.7 %collective-permute-start = (bf16[2,192,2048]{2,1,0:T(8,128)(2,1)}, bf16[2,192,2048]{2,1,0:T(8,128)(2,1)}, u32[]{:S(2)}, u32[]{:S(2)}) collective-permute-start(bf16[2,192,2048]{2,1,0:T(8,128)(2,1)} %bitcast.60), channel_id=1, source_target_pairs={{0,32},{32,64},{64,96},{96,0},{1,33},{33,65},{65,97},{97,1},{2,34}... | collective-permute-start | bytes 4718600 | tf_op jit(solution)/shard_map/ppermute | solution.py:290
  35.2 83.5 %collective-permute-start.1 = (bf16[2,192,2048]{2,1,0:T(8,128)(2,1)}, bf16[2,192,2048]{2,1,0:T(8,128)(2,1)}, u32[]{:S(2)}, u32[]{:S(2)}) collective-permute-start(bf16[2,192,2048]{2,1,0:T(8,128)(2,1)} %bitcast.59), channel_id=1, source_target_pairs={{0,64},{32,96},{64,0},{96,32},{1,65},{33,97},{65,1},{97,33},{2,66}... | collective-permute-start | bytes 4718600 | tf_op jit(solution)/shard_map/ppermute | solution.py:290
  37.6 3.1 %copy-start.2 = (s32[2,2048]{1,0:T(2,128)S(1)}, s32[2,2048]{1,0:T(2,128)}, u32[]{:S(2)}) copy-start(s32[2,2048]{1,0:T(2,128)} %param.12) | copy-start | bytes 49156
  39.4 79.3 %collective-permute-start.2 = (bf16[2,192,2048]{2,1,0:T(8,128)(2,1)}, bf16[2,192,2048]{2,1,0:T(8,128)(2,1)}, u32[]{:S(2)}, u32[]{:S(2)}) collective-permute-start(bf16[2,192,2048]{2,1,0:T(8,128)(2,1)} %bitcast.58), channel_id=1, source_target_pairs={{0,96},{32,0},{64,32},{96,64},{1,97},{33,1},{65,33},{97,65},{2,98}... | collective-permute-start | bytes 4718600 | tf_op jit(solution)/shard_map/ppermute | solution.py:290
  41.8 0.8 copy-start
  57.8 59.2 %all-to-all-start.3 = ((f32[128,11,128]{2,1,0:T(8,128)}), f32[128,11,128]{2,1,0:T(8,128)S(1)}, u32[]{:S(2)}, u32[]{:S(2)}) async-start(f32[128,11,128]{2,1,0:T(8,128)} %broadcast_in_dim.49), calls=%async_computation.3 | async-start | bytes 2097152 | tf_op jit(solution)/shard_map/all_to_all | solution.py:266
  64.5 2.5 copy-start.1
  170.3 105.6 %collective-permute-start.5 = (bf16[2,48,2048]{2,1,0:T(8,128)(2,1)S(1)}, bf16[2,48,2048]{2,1,0:T(8,128)(2,1)S(1)}, u32[]{:S(2)}, u32[]{:S(2)}) collective-permute-start(bf16[2,48,2048]{2,1,0:T(8,128)(2,1)S(1)} %get-tuple-element.19), channel_id=1, source_target_pairs={{0,24},{8,0},{16,8},{24,16},{1,25},{9,1},{17,9},{25,17},{2,26},{10... | collective-permute-start | bytes 1179656 | tf_op jit(solution)/shard_map/ppermute | solution.py:337
  173.0 103.0 %collective-permute-start.4 = (bf16[2,48,2048]{2,1,0:T(8,128)(2,1)S(1)}, bf16[2,48,2048]{2,1,0:T(8,128)(2,1)S(1)}, u32[]{:S(2)}, u32[]{:S(2)}) collective-permute-start(bf16[2,48,2048]{2,1,0:T(8,128)(2,1)S(1)} %get-tuple-element.20), channel_id=1, source_target_pairs={{0,16},{8,24},{16,0},{24,8},{1,17},{9,25},{17,1},{25,9},{2,18},{10... | collective-permute-start | bytes 1179656 | tf_op jit(solution)/shard_map/ppermute | solution.py:337
  173.5 102.4 %collective-permute-start.3 = (bf16[2,48,2048]{2,1,0:T(8,128)(2,1)S(1)}, bf16[2,48,2048]{2,1,0:T(8,128)(2,1)S(1)}, u32[]{:S(2)}, u32[]{:S(2)}) collective-permute-start(bf16[2,48,2048]{2,1,0:T(8,128)(2,1)S(1)} %get-tuple-element.18), channel_id=1, source_target_pairs={{0,8},{8,16},{16,24},{24,0},{1,9},{9,17},{17,25},{25,1},{2,10},{10... | collective-permute-start | bytes 1179656 | tf_op jit(solution)/shard_map/ppermute | solution.py:337
  197.6 65.7 %copy-start.3 = (f32[1,128]{1,0:T(1,128)S(1)}, f32[1,128]{1,0:T(1,128)}, u32[]{:S(2)}) copy-start(f32[1,128]{1,0:T(1,128)} %find_roots.3) | copy-start | bytes 1540

commit v2 on v1

--- a/solution.py
+++ b/solution.py
@@ -15,7 +15,8 @@
 LANES = 128
 GROUP = 64
 UNROLL = 32
-SPLIT = 3
+CUT_A = 5
+CUT_B = 6
 
 
 def cost(flops):
@@ -41,20 +42,19 @@
 
 def root_kernel(pw_ref, root_ref, out_ref, w2_ref, ps_ref, c_ref, t_ref, lo_ref, hi_ref):
     load_tables(pw_ref, w2_ref)
-    n_rows = root_ref.shape[1]
-    for k in range(n_rows):
-        here = pl.ds(k * LANES, LANES)
-        c_ref[here, :] = column(root_ref[0, k : k + 1, :])
-        t_ref[here, :] = column(root_ref[1, k : k + 1, :])
-        lo_ref[here, :] = column(root_ref[2, k : k + 1, :])
-        hi_ref[here, :] = column(root_ref[3, k : k + 1, :])
+    groups = root_ref.shape[1]
+    for k in range(groups):
+        here = pl.ds(k * GROUP, GROUP)
+        c_ref[here, :] = column(root_ref[0, k : k + 1, :])[:GROUP]
+        t_ref[here, :] = column(root_ref[1, k : k + 1, :])[:GROUP]
+        lo_ref[here, :] = column(root_ref[2, k : k + 1, :])[:GROUP]
+        hi_ref[here, :] = column(root_ref[3, k : k + 1, :])[:GROUP]
 
     def group_body(g, carry):
         here = pl.ds(g * GROUP, GROUP)
-        c = c_ref[here, :]
         base = c_ref[pl.ds(g * GROUP + GROUP // 2, 1), :]
         shift_poles(pw_ref, ps_ref, base)
-        near = c - base
+        near = c_ref[here, :] - base
 
         def step(_, carry):
             t = t_ref[here, :]
@@ -82,23 +82,27 @@
         lax.fori_loop(0, ITERS, step, 0)
         return carry
 
-    lax.fori_loop(0, n_rows * LANES // GROUP, group_body, 0)
-    for k in range(n_rows):
-        out_ref[k : k + 1, :] = t_ref[pl.ds(k * LANES, LANES), :].T[0:1, :]
+    lax.fori_loop(0, groups, group_body, 0)
+    pad = jnp.zeros((LANES - GROUP, LANES), F32)
+    for k in range(groups):
+        t = jnp.concatenate([t_ref[pl.ds(k * GROUP, GROUP), :], pad], axis=0)
+        out_ref[k : k + 1, :] = t.T[0:1, :]
 
 
 def find_roots(pw, root):
-    n_rows = root.shape[1]
+    groups = root.shape[1]
     n_pole_rows = pw.shape[0] * pw.shape[2]
-    roots = n_rows * LANES
-    return pl.pallas_call(
+    roots = groups * GROUP
+    root = jnp.pad(root, ((0, 0), (0, 0), (0, LANES - GROUP)))
+    found = pl.pallas_call(
         root_kernel,
-        out_shape=jax.ShapeDtypeStruct((n_rows, LANES), F32),
+        out_shape=jax.ShapeDtypeStruct((groups, LANES), F32),
         scratch_shapes=[pltpu.VMEM((n_pole_rows, LANES), F32)] * 2
         + [pltpu.VMEM((roots, LANES), F32)] * 4,
         cost_estimate=cost(ITERS * roots * n_pole_rows * LANES * 10),
         name="find_roots",
     )(pw, root)
+    return found[:, :GROUP]
 
 
 def panel_kernel(pw_ref, root_ref, out_ref, w2_ref):
@@ -190,75 +194,78 @@
     )(index, pw)
 
 
-def matmul_kernel(
-    col_ref, root_ref, e0, e1, e2, e3, own_ref, send_ref, p_ref, w_ref, tile_a, tile_b, acc_ref
-):
-    blocks = (e0, e1, e2, e3)
-    halves, rows, depth = e0.shape
-    chunk = tile_a.shape[1]
+def matmul_kernel(col_ref, root_ref, *refs):
+    blocks = refs[:8]
+    own_ref, send_ref, p_ref, w_ref = refs[8:]
+    sources = 4
+    _, rows, depth = blocks[0].shape
+    chunk = 256
     chunks = root_ref.shape[1] // chunk
     pieces = depth // LANES
-    for piece in range(p_ref.shape[0] // LANES):
-        here = pl.ds(piece * LANES, LANES)
-        p_ref[here, :] = column(col_ref[0, piece : piece + 1, :])
-        w_ref[here, :] = column(col_ref[1, piece : piece + 1, :])
-
-    def fill(tile, src, half, k):
-        for part in range(chunk // LANES):
-            lanes = pl.ds(k * chunk + part * LANES, LANES)
-            c = root_ref[0:1, lanes]
-            t = root_ref[1:2, lanes]
-            n = root_ref[2:3, lanes]
-            for piece in range(pieces):
-                here = pl.ds((src * halves + half) * depth + piece * LANES, LANES)
-                distance = (p_ref[here, :] - c) - t
-                value = w_ref[here, :] * (1.0 / distance) * n
-                tile[piece * LANES : (piece + 1) * LANES, part * LANES : (part + 1) * LANES] = (
-                    value.astype(BF16)
-                )
-
-    def product(src, half, tile):
-        return jnp.dot(blocks[src][half], tile[...], preferred_element_type=F32)
-
-    steps = halves * chunks
-    fill(tile_a, 0, 0, 0)
-
-    def body(i, carry):
-        half = i // chunks
-        k = i % chunks
-        following = jnp.minimum(i + 1, steps - 1)
-        fill(tile_b, 1, half, k)
-        acc_ref[...] = product(0, half, tile_a)
-        fill(tile_a, 2, half, k)
-        acc_ref[...] += product(1, half, tile_b)
-        fill(tile_b, 3, half, k)
-        acc_ref[...] += product(2, half, tile_a)
-        fill(tile_a, 0, following // chunks, following % chunks)
-        acc = acc_ref[...] + product(3, half, tile_b)
+    for src in range(sources):
+        p = jnp.concatenate([col_ref[0, src, 0]] * (LANES // pieces), axis=0).T
+        w = jnp.concatenate([col_ref[1, src, 0]] * (LANES // pieces), axis=0).T
+        for piece in range(pieces):
+            here = pl.ds(src * depth + piece * LANES, LANES)
+            p_ref[here, :] = jnp.broadcast_to(p[:, piece : piece + 1], (LANES, LANES))
+            w_ref[here, :] = jnp.broadcast_to(w[:, piece : piece + 1], (LANES, LANES))
+
+    def cauchy(src, k):
+        down = []
+        for piece in range(pieces):
+            here = pl.ds(src * depth + piece * LANES, LANES)
+            p = p_ref[here, :]
+            w = w_ref[here, :]
+            across = []
+            for part in range(chunk // LANES):
+                lanes = pl.ds(k * chunk + part * LANES, LANES)
+                distance = (p - root_ref[0:1, lanes]) - root_ref[1:2, lanes]
+                value = w * (1.0 / distance) * root_ref[2:3, lanes]
+                across.append(value.astype(BF16))
+            down.append(jnp.concatenate(across, axis=1))
+        return jnp.concatenate(down, axis=0)
+
+    def body(k, carry):
+        acc = None
+        for src in range(sources):
+            left = jnp.concatenate([blocks[src][0], blocks[sources + src][0]], axis=0)
+            product = jnp.dot(left, cauchy(src, k), preferred_element_type=F32)
+            acc = product if acc is None else acc + product
         quarter = rows // 4
         for part in range(4):
-            piece = acc[part * quarter : (part + 1) * quarter]
-            own_ref[part, half, :, pl.ds(k * chunk, chunk)] = piece
-            send_ref[part, half, :, pl.ds(k * chunk, chunk)] = piece.astype(BF16)
+            for side in range(2):
+                first = side * rows + part * quarter
+                piece = acc[first : first + quarter]
+                own_ref[part, 0, side, :, pl.ds(k * chunk, chunk)] = piece
+                send_ref[part, 0, side, :, pl.ds(k * chunk, chunk)] = piece.astype(BF16)
         return carry
 
-    lax.fori_loop(0, steps, body, 0)
+    lax.fori_loop(0, chunks, body, 0)
 
 
 def panel_product(columns, root, blocks):
+    sources = 4
     halves, rows, depth = blocks[0].shape
     n_roots = root.shape[1]
-    chunk = 256
-    shape = (4, halves, rows // 4, n_roots)
+    pieces = depth // LANES
+    shape = (4, halves, 2, rows // 4, n_roots)
+    out = pl.BlockSpec((4, 1, 2, rows // 4, n_roots), lambda h: (0, h, 0, 0, 0))
+    block = pl.BlockSpec((1, rows, depth), lambda h: (h, 0, 0))
     return pl.pallas_call(
         matmul_kernel,
+        grid=(halves,),
+        in_specs=[
+            pl.BlockSpec((2, sources, 1, pieces, LANES), lambda h: (0, 0, h, 0, 0)),
+            pl.BlockSpec((3, n_roots), lambda h: (0, 0)),
+        ]
+        + [block] * 8,
+        out_specs=(out, out),
         out_shape=(jax.ShapeDtypeStruct(shape, F32), jax.ShapeDtypeStruct(shape, BF16)),
-        scratch_shapes=[pltpu.VMEM((4 * halves * depth, LANES), F32)] * 2
-        + [pltpu.VMEM((depth, chunk), BF16)] * 2
-        + [pltpu.VMEM((rows, chunk), F32)],
-        cost_estimate=cost(2 * 4 * halves * rows * depth * n_roots),
+        scratch_shapes=[pltpu.VMEM((sources * depth, LANES), F32)] * 2,
+        compiler_params=pltpu.CompilerParams(vmem_limit_bytes=56 << 20),
+        cost_estimate=cost(2 * 2 * sources * halves * rows * depth * n_roots),
         name="panel_product",
-    )(columns, root, *blocks)
+    )(columns.reshape(2, sources, halves, pieces, LANES), root, *blocks)
 
 
 def copies(value, axis):
@@ -272,22 +279,20 @@
     return [(i, (i + shift) % 4) for i in range(4)]
 
 
-def on_device(pole_values, weights, centers, offsets, chosen, column_pole, eigen_blocks):
+def merge(pole_values, weights, centers, offsets, chosen, column_pole, eigen_blocks):
     z = lax.axis_index("z")
     x = lax.axis_index("x")
+    core = lax.axis_index("core")
     row = z * 4 + x
-    col = lax.axis_index("y") * 2 + lax.axis_index("core")
+    col = lax.axis_index("y") * 2 + core
     n_col = centers.shape[0]
     n_own = n_col // 16
+    swap = [(0, 1), (1, 0)]
 
     parted = jnp.stack([pole_values.reshape(-1, LANES), weights.reshape(-1, LANES)])
     pw = copies(parted, ROW)
 
     turned = jnp.moveaxis(eigen_blocks.reshape(4, -1, 2, eigen_blocks.shape[2]), 2, 1)
-    blocks = [lax.dynamic_index_in_dim(turned, z, 0, keepdims=False)]
-    for shift in (1, 2, 3):
-        block = lax.dynamic_index_in_dim(turned, (z + shift) % 4, 0, keepdims=False)
-        blocks.append(lax.ppermute(block, "z", ring(shift)))
 
     wanted = lax.dynamic_slice_in_dim(chosen, row * LANES, LANES)
     local = wanted - col * n_col
@@ -299,23 +304,22 @@
         ]
     )
     spread = jnp.moveaxis(first.reshape(2, 8, 16), 1, 0)
-    mine = jnp.sum(lax.all_to_all(spread, COL, 0, 0, tiled=True), axis=0)
-    panel_start = jnp.pad(mine, ((0, 0), (0, LANES - 16)), constant_values=0.25)
+    arrived = lax.all_to_all(spread, COL, 0, 0, tiled=True)
+    pw, turned, arrived = lax.optimization_barrier((pw, turned, arrived))
+    eigen = [lax.dynamic_index_in_dim(turned, z, 0, keepdims=False)]
+    for shift in (1, 2, 3):
+        block = lax.dynamic_index_in_dim(turned, (z + shift) % 4, 0, keepdims=False)
+        eigen.append(lax.ppermute(block, "z", ring(shift)))
+    peer = [lax.ppermute(eigen[0], "core", swap)]
+
+    panel_start = jnp.pad(
+        jnp.sum(arrived, axis=0), ((0, 0), (0, LANES - 16)), constant_values=0.25
+    )
     panel_end = panel_roots(pw, panel_start)
-
     index = lax.dynamic_slice_in_dim(column_pole.reshape(-1, LANES), col * 4, 4)
     picked = pick_columns(index, pw)
-
     note = jnp.concatenate([picked.reshape(8, LANES), panel_start[:1], panel_end], axis=0)
     notes = copies(note, ALL)
-    columns = lax.dynamic_index_in_dim(
-        notes[:, :8].reshape(4, 4, 8, 2, 4, LANES), x, 1, keepdims=False
-    )
-    columns = jnp.concatenate(
-        [lax.dynamic_slice_in_dim(jnp.concatenate([columns, columns]), (z - s) % 4, 1) for s in range(4)]
-    )
-    columns = jnp.moveaxis(columns, 2, 0).reshape(2, -1, LANES)
-    panel_root = jnp.moveaxis(notes[:, 8:, :16], 1, 0).reshape(3, -1)
 
     start = col * n_col + row * n_own
     my_centers = lax.dynamic_slice_in_dim(centers, row * n_own, n_own)
@@ -327,27 +331,45 @@
     low = own_poles - my_centers
     last = start + jnp.arange(n_own) == pole_values.shape[0] * 16 - 1
     high = jnp.where(last, 3e38, -low)
-    mine = jnp.stack([my_centers, my_offsets, low, high]).reshape(4, -1, LANES)
-    roots_a = find_roots(pw, mine[:, :SPLIT])
-
-    own, send = panel_product(columns, panel_root, blocks)
+    state = jnp.stack([my_centers, my_offsets, low, high]).reshape(4, -1, GROUP)
+    roots_a = find_roots(pw, state[:, :CUT_A])
+    eigen, notes, roots_a = lax.optimization_barrier((eigen, notes, roots_a))
+
+    peer += [lax.ppermute(block, "core", swap) for block in eigen[1:]]
+    roots_b = find_roots(pw, state[:, CUT_A:CUT_B])
+
+    columns = lax.dynamic_index_in_dim(
+        notes[:, :8].reshape(4, 4, 8, 2, 4, LANES), x, 1, keepdims=False
+    )
+    columns = jnp.concatenate(
+        [lax.dynamic_slice_in_dim(columns, (z - s) % 4, 1) for s in range(4)]
+    )
+    columns = jnp.moveaxis(columns, 2, 0)
+    panel_root = jnp.moveaxis(notes[:, 8:, :16], 1, 0).reshape(3, 2, -1)
+    panel_root = lax.dynamic_index_in_dim(panel_root, core, 1, keepdims=False)
+    panel_root, peer, roots_b = lax.optimization_barrier((panel_root, peer, roots_b))
+    own, send = panel_product(columns, panel_root, eigen + peer)
+
     pieces = [lax.dynamic_index_in_dim(own, x, 0, keepdims=False)]
     for shift in (1, 2, 3):
         piece = lax.dynamic_index_in_dim(send, (x + shift) % 4, 0, keepdims=False)
         pieces.append(lax.ppermute(piece, "x", ring(shift)))
-
-    roots_b = find_roots(pw, mine[:, SPLIT:])
-    panel = pieces[0] + pieces[1] + pieces[2] + pieces[3]
-    panel = jnp.moveaxis(panel, 0, 1)
-    roots = copies(jnp.concatenate([roots_a, roots_b]), ROW)
-    return roots.reshape(-1), panel
+    roots_c = find_roots(pw, state[:, CUT_B:])
+    total = pieces[0] + pieces[1] + pieces[2] + pieces[3]
+    keep = total[:, 0]
+    got = lax.ppermute(total[:, 1], "core", swap)
+    roots = copies(jnp.concatenate([roots_a, roots_b, roots_c]), ROW)
+    panel = jnp.where(
+        core == 0, jnp.concatenate([keep, got], axis=2), jnp.concatenate([got, keep], axis=2)
+    )
+    return roots.reshape(-1), jnp.moveaxis(panel, 0, 1)
 
 
 def solution(mesh):
     torus = Mesh(mesh.devices.reshape(4, 4, 4, 2), ALL)
     placed = (P(ROW), P(ROW), P(COL), P(COL), P(), P(None, ROW), P(COL, None, ROW))
     return jax.shard_map(
-        on_device,
+        merge,
         mesh=torus,
         in_specs=placed,
         out_specs=(P(COL), P(COL + ROW, None, None)),

time: 281 us -> 232 us (0.83)
  waiting for transfers between devices: 52.8 us -> 29 us
  Pallas kernels: 152 us -> 129 us
  blocking collectives: 12 us -> 0 us
  starting transfers between devices: 28.8 us -> 36.4 us
  local copies, waits for them, and re-layouts: 24.1 us -> 27.7 us
    all_to_all x2 -> x3, waiting for transfers between devices: 48.9 us -> 8.44 us  [copies(): lax.all_to_all(jnp.broadcast_to(value[None], (size, *value.shape)), axis,...]
    pallas_call x3 -> x4, Pallas kernels: 138 us -> 115 us  [the longest x3 90.1 us: find_roots(): pl.pallas_call(root_kernel, out_shape=jax.ShapeDtypeStruct((groups, LANES...]
    ppermute x6 -> x11, waiting for transfers between devices: 0.02 us -> 16.7 us  [the longest x3 16.7 us: merge(): pieces.append(lax.ppermute(piece, 'x', ring(shift)))]
    all_to_all x1 -> x0, blocking collectives: 12 us -> none  [copies(): lax.all_to_all(jnp.broadcast_to(value[None], (size, *value.shape)), axis,...]
    reshape x3 -> x5, local copies, waits for them, and re-layouts: 1.04 us -> 9.49 us  [the longest x1 8.37 us: merge(): eigen_blocks.reshape(4, -1, 2, eigen_blocks.shape[2])]
    all_to_all x2 -> x3, starting transfers between devices: 14.1 us -> 21.6 us  [copies(): lax.all_to_all(jnp.broadcast_to(value[None], (size, *value.shape)), axis,...]
    another operation x4 -> x7, local copies, waits for them, and re-layouts: 7.8 us -> 0.46 us  [the longest x5 0.31 us: merge(): state = jnp.stack([my_centers, my_offsets, low, high]).reshape(4, -1, GROUP)]
    unnamed x14 -> x17, local copies, waits for them, and re-layouts: 10.1 us -> 2.92 us
  transfers between devices with their start and end apart: 9 -> 15, of which waited for: 2 -> 5; matrix products, arithmetic and copies ran while one was open for 8% -> 9% of each run, Pallas kernels for 36% -> 45%
where the time goes in v2:
time: 232 us; the launch traced here: 231 us
  Pallas kernels  129 us (56%)
  starting transfers between devices  36.4 us (16%)
  waiting for transfers between devices  29 us (12%)
  local copies, waits for them, and re-layouts  27.7 us (12%)
  other arithmetic  7.97 us (3%)
    pallas_call x3, Pallas kernels, find_roots(): pl.pallas_call(root_kernel, out_shape=jax.ShapeDtypeStruct((groups, LANES...  90.1 us
    pallas_call x1, Pallas kernels, panel_product(): pl.pallas_call(matmul_kernel, grid=(halves,), in_specs=[pl.BlockSpec((2,...  25.1 us
    all_to_all x3, starting transfers between devices, copies(): lax.all_to_all(jnp.broadcast_to(value[None], (size, *value.shape)), axis,...  21.6 us
    ppermute x3, waiting for transfers between devices, merge(): pieces.append(lax.ppermute(piece, 'x', ring(shift)))  16.7 us
    pallas_call x1, Pallas kernels, panel_roots(): pl.pallas_call(panel_kernel, out_shape=jax.ShapeDtypeStruct((2, LANES), F...  8.5 us
    all_to_all x3, waiting for transfers between devices, copies(): lax.all_to_all(jnp.broadcast_to(value[None], (size, *value.shape)), axis,...  8.44 us
    reshape x1, local copies, waits for them, and re-layouts, merge(): eigen_blocks.reshape(4, -1, 2, eigen_blocks.shape[2])  8.37 us
    all_to_all x1, starting transfers between devices, merge(): arrived = lax.all_to_all(spread, COL, 0, 0, tiled=True)  5.96 us
  transfers between devices with their start and end apart: 15, of which 5 were waited for; matrix products, arithmetic and copies ran while one was open for 9% of the time, Pallas kernels for 45%

profile of v2, /device:TPU:1, one launch (start us, length us, event | category | flops | bytes accessed | tf_op | source)
XLA Modules:
  0.0 230.6 jit_solution(8513470170285040695)
XLA Ops:
  0.6 0.8 dynamic-slice_subtract_fusion
  1.4 2.1 select_reduce_fusion.1
  4.3 6.0 %all-to-all-start.1 = ((f32[8,2,16]{2,1,0:T(2,128)}), f32[8,2,16]{2,1,0:T(2,128)S(1)}, u32[]{:S(2)}, u32[]{:S(2)}) async-start(f32[8,2,16]{2,1,0:T(2,128)} %copy.25), calls=%async_computation.1 | async-start | bytes 16384 | tf_op jit(solution)/shard_map/all_to_all | solution.py:307
  11.0 3.9 %all-to-all-done.1 = f32[8,2,16]{2,1,0:T(2,128)S(1)} async-done(((f32[8,2,16]{2,1,0:T(2,128)}), f32[8,2,16]{2,1,0:T(2,128)S(1)}, u32[]{:S(2)}, u32[]{:S(2)}) %all-to-all-start.1) | async-done | bytes 1056 | tf_op jit(solution)/shard_map/all_to_all | solution.py:307
  14.9 0.9 broadcast_in_dim.43
  15.8 7.6 %all-to-all-start = ((f32[16,2,32,128]{3,2,1,0:T(8,128)}), f32[16,2,32,128]{3,2,1,0:T(8,128)S(1)}, u32[]{:S(2)}, u32[]{:S(2)}) async-start(f32[16,2,32,128]{3,2,1,0:T(8,128)} %broadcast_in_dim.43), calls=%async_computation | async-start | bytes 1048576 | tf_op jit(solution)/shard_map/all_to_all | solution.py:273
  23.4 8.4 %copy.35 = bf16[4,192,2,2048]{3,1,2,0:T(8,128)(2,1)} copy(bf16[4,192,2,2048]{3,2,1,0:T(2,128)(2,1)} %bitcast.62) | data formatting | bytes 12582912 | tf_op jit(solution)/shard_map/reshape | solution.py:295
  31.8 2.0 all-to-all-done.pw_ref
  33.8 5.5 %dynamic-slice_bitcast_fusion = (bf16[2,192,2048]{2,1,0:T(8,128)(2,1)}, bf16[2,192,2048]{2,1,0:T(8,128)(2,1)}, bf16[2,192,2048]{2,1,0:T(8,128)(2,1)}, bf16[2,192,2048]{2,1,0:T(8,128)(2,1)S(1)}) fusion(bf16[4,2,192,2048]{3,2,1,0:T(8,128)(2,1)} %bitcast.61, s32[]{:T(128)S(6)} %select_n.146, s32[]{:T(128)S(6)} %select_n.144, s32[]{:T(128)S(6)} %select_n.142, ...), kind=kLoop, calls=%fused_computation.4 | loop fusion | bytes 12582928 | tf_op jit(solution)/shard_map/jit(dynamic_index_in_dim)/squeeze | solution.py:311
  39.3 0.9 collective-permute-start.2
  41.3 0.8 dynamic_slice.75
  43.7 5.0 %pick_columns.1 = f32[2,4,128]{2,1,0:T(4,128)} custom-call(s32[4,128]{1,0:T(4,128)} %constant_dynamic-slice_fusion.2.index_ref, f32[16,2,32,128]{3,2,1,0:T(8,128)} %copy-done), custom_call_target="tpu_custom_call" | custom-call | flops 50000000 | bytes 1048576 | tf_op jit(solution)/shard_map/pick_columns/pallas_call | solution.py:189
  48.8 8.5 %panel_roots.1 = f32[2,128]{1,0:T(2,128)} custom-call(f32[16,2,32,128]{3,2,1,0:T(8,128)} %copy-done, f32[2,128]{1,0:T(2,128)} %pad.16.root_ref), custom_call_target="tpu_custom_call" | custom-call | flops 52428800 | bytes 1048576 | tf_op jit(solution)/shard_map/panel_roots/pallas_call | solution.py:153
  58.0 1.0 broadcast_in_dim.47
  59.0 8.0 %all-to-all-start.2 = ((f32[128,11,128]{2,1,0:T(8,128)}), f32[128,11,128]{2,1,0:T(8,128)S(1)}, u32[]{:S(2)}, u32[]{:S(2)}) async-start(f32[128,11,128]{2,1,0:T(8,128)} %broadcast_in_dim.47), calls=%async_computation.2 | async-start | bytes 2097152 | tf_op jit(solution)/shard_map/all_to_all | solution.py:273
  67.0 0.8 negate_select_fusion
  68.7 1.1 collective-permute-start.3
  69.7 54.7 %find_roots.3 = f32[5,128]{1,0:T(8,128)} custom-call(f32[16,2,32,128]{3,2,1,0:T(8,128)} %copy-done, f32[4,5,128]{2,1,0:T(8,128)} %pad.17.root_ref), custom_call_target="tpu_custom_call" | custom-call | flops 629145600 | bytes 1048576 | tf_op jit(solution)/shard_map/find_roots/pallas_call | solution.py:97
  125.8 12.3 %find_roots.4 = f32[1,128]{1,0:T(1,128)} custom-call(f32[16,2,32,128]{3,2,1,0:T(8,128)} %copy-done, f32[4,1,128]{2,1,0:T(1,128)} %pad.18.root_ref), custom_call_target="tpu_custom_call" | custom-call | flops 125829120 | bytes 1048576 | tf_op jit(solution)/shard_map/find_roots/pallas_call | solution.py:97
  140.0 25.1 %panel_product.1 = (f32[4,2,2,48,1024]{4,3,2,1,0:T(8,128)}, bf16[4,2,2,48,1024]{4,3,2,1,0:T(8,128)(2,1)}) custom-call(f32[2,4,2,16,128]{4,3,2,1,0:T(8,128)} %bitcast.64, f32[3,1024]{1,0:T(4,128)} %bitcast.67, bf16[2,192,2048]{2,1,0:T(8,128)(2,1)} %copy-done.1, bf16[2,192,2048]{2,1,0:T(8,128)(2,1)} %collective-permute-done.refs_1_, ...), custom_call_target="tpu_custom_call" | custom-call | flops 12884901888 | bytes 1048576 | tf_op jit(solution)/shard_map/panel_product/pallas_call | solution.py:254
  165.0 1.4 dynamic-slice_bitcast_fusion.6
  166.4 0.8 collective-permute-start.7
  167.2 2.0 collective-permute-start.9
  169.1 1.0 collective-permute-start.8
  170.1 7.8 %collective-permute-done.7 = bf16[2,2,48,1024]{3,2,1,0:T(8,128)(2,1)S(1)} collective-permute-done((bf16[2,2,48,1024]{3,2,1,0:T(8,128)(2,1)S(1)}, bf16[2,2,48,1024]{3,2,1,0:T(8,128)(2,1)S(1)}, u32[]{:S(2)}, u32[]{:S(2)}) %collective-permute-start.7) | collective-permute-done | bytes 393248 | tf_op jit(solution)/shard_map/ppermute | solution.py:356
  177.9 8.9 %collective-permute-done.8 = bf16[2,2,48,1024]{3,2,1,0:T(8,128)(2,1)S(1)} collective-permute-done((bf16[2,2,48,1024]{3,2,1,0:T(8,128)(2,1)S(1)}, bf16[2,2,48,1024]{3,2,1,0:T(8,128)(2,1)S(1)}, u32[]{:S(2)}, u32[]{:S(2)}) %collective-permute-start.8) | collective-permute-done | bytes 393248 | tf_op jit(solution)/shard_map/ppermute | solution.py:356
  186.8 1.3 fusion.2
  188.2 1.3 collective-permute-start.10
  190.2 23.0 %find_roots.5 = f32[2,128]{1,0:T(2,128)} custom-call(f32[16,2,32,128]{3,2,1,0:T(8,128)} %copy-done, f32[4,2,128]{2,1,0:T(2,128)} %pad.19.root_ref), custom_call_target="tpu_custom_call" | custom-call | flops 251658240 | bytes 1048576 | tf_op jit(solution)/shard_map/find_roots/pallas_call | solution.py:97
  214.6 6.0 %all-to-all-start.3 = ((f32[16,1,512]{2,1,0:T(1,128)}), f32[16,1,512]{2,1,0:T(1,128)S(1)}, u32[]{:S(2)}, u32[]{:S(2)}) async-start(f32[16,1,512]{2,1,0:T(1,128)} %reshape.64), calls=%async_computation.3 | async-start | bytes 65536 | tf_op jit(solution)/shard_map/all_to_all | solution.py:273
  220.6 6.4 %all-to-all-done.3 = f32[16,1,512]{2,1,0:T(1,128)S(1)} async-done(((f32[16,1,512]{2,1,0:T(1,128)}), f32[16,1,512]{2,1,0:T(1,128)S(1)}, u32[]{:S(2)}, u32[]{:S(2)}) %all-to-all-start.3) | async-done | bytes 32800 | tf_op jit(solution)/shard_map/all_to_all | solution.py:273
  229.1 1.5 copy.30
  (70 shorter events, 13.1 us)
Async XLA Ops:
  4.3 10.6 %all-to-all-start.1 = ((f32[8,2,16]{2,1,0:T(2,128)}), f32[8,2,16]{2,1,0:T(2,128)S(1)}, u32[]{:S(2)}, u32[]{:S(2)}) async-start(f32[8,2,16]{2,1,0:T(2,128)} %copy.25), calls=%async_computation.1 | async-start | bytes 16384 | tf_op jit(solution)/shard_map/all_to_all | solution.py:307
  15.8 18.0 %all-to-all-start = ((f32[16,2,32,128]{3,2,1,0:T(8,128)}), f32[16,2,32,128]{3,2,1,0:T(8,128)S(1)}, u32[]{:S(2)}, u32[]{:S(2)}) async-start(f32[16,2,32,128]{3,2,1,0:T(8,128)} %broadcast_in_dim.43), calls=%async_computation | async-start | bytes 1048576 | tf_op jit(solution)/shard_map/all_to_all | solution.py:273
  33.8 9.0 %copy-start = (f32[16,2,32,128]{3,2,1,0:T(8,128)}, f32[16,2,32,128]{3,2,1,0:T(8,128)S(1)}, u32[]{:S(2)}) copy-start(f32[16,2,32,128]{3,2,1,0:T(8,128)S(1)} %all-to-all-done.pw_ref) | copy-start | bytes 1572868
  33.8 8.4 %copy-start.2 = (s32[2,2048]{1,0:T(2,128)S(1)}, s32[2,2048]{1,0:T(2,128)}, u32[]{:S(2)}) copy-start(s32[2,2048]{1,0:T(2,128)} %param.12) | copy-start | bytes 49156
  39.3 29.4 %copy-start.1 = (bf16[2,192,2048]{2,1,0:T(8,128)(2,1)}, bf16[2,192,2048]{2,1,0:T(8,128)(2,1)S(1)}, u32[]{:S(2)}) copy-start(bf16[2,192,2048]{2,1,0:T(8,128)(2,1)S(1)} %get-tuple-element.29.refs_0_) | copy-start | bytes 4718596
  39.3 85.2 %collective-permute-start.2 = (bf16[2,192,2048]{2,1,0:T(8,128)(2,1)}, bf16[2,192,2048]{2,1,0:T(8,128)(2,1)}, u32[]{:S(2)}, u32[]{:S(2)}) collective-permute-start(bf16[2,192,2048]{2,1,0:T(8,128)(2,1)} %get-tuple-element.49), channel_id=1, source_target_pairs={{0,96},{32,0},{64,32},{96,64},{1,97},{33,1},{65,33},{97,65},{2,98}... | collective-permute-start | bytes 4718600 | tf_op jit(solution)/shard_map/ppermute | solution.py:312
  40.2 84.3 %collective-permute-start.1 = (bf16[2,192,2048]{2,1,0:T(8,128)(2,1)}, bf16[2,192,2048]{2,1,0:T(8,128)(2,1)}, u32[]{:S(2)}, u32[]{:S(2)}) collective-permute-start(bf16[2,192,2048]{2,1,0:T(8,128)(2,1)} %get-tuple-element.50), channel_id=1, source_target_pairs={{0,64},{32,96},{64,0},{96,32},{1,65},{33,97},{65,1},{97,33},{2,66}... | collective-permute-start | bytes 4718600 | tf_op jit(solution)/shard_map/ppermute | solution.py:312
  40.8 83.7 %collective-permute-start = (bf16[2,192,2048]{2,1,0:T(8,128)(2,1)}, bf16[2,192,2048]{2,1,0:T(8,128)(2,1)}, u32[]{:S(2)}, u32[]{:S(2)}) collective-permute-start(bf16[2,192,2048]{2,1,0:T(8,128)(2,1)} %get-tuple-element.51), channel_id=1, source_target_pairs={{0,32},{32,64},{64,96},{96,0},{1,33},{33,65},{65,97},{97,1},{2,34}... | collective-permute-start | bytes 4718600 | tf_op jit(solution)/shard_map/ppermute | solution.py:312
  59.0 65.4 %all-to-all-start.2 = ((f32[128,11,128]{2,1,0:T(8,128)}), f32[128,11,128]{2,1,0:T(8,128)S(1)}, u32[]{:S(2)}, u32[]{:S(2)}) async-start(f32[128,11,128]{2,1,0:T(8,128)} %broadcast_in_dim.47), calls=%async_computation.2 | async-start | bytes 2097152 | tf_op jit(solution)/shard_map/all_to_all | solution.py:273
  68.7 71.3 %collective-permute-start.3 = (bf16[2,192,2048]{2,1,0:T(8,128)(2,1)S(1)}, bf16[2,192,2048]{2,1,0:T(8,128)(2,1)}, u32[]{:S(2)}, u32[]{:S(2)}) collective-permute-start(bf16[2,192,2048]{2,1,0:T(8,128)(2,1)S(1)} %get-tuple-element.29.refs_0_), channel_id=1, source_target_pairs={{0,1},{1,0},{2,3},{3,2},{4,5},{5,4},{6,7},{7,6},{8,9},{9,8},{10,11... | collective-permute-start | bytes 4718600 | tf_op jit(solution)/shard_map/ppermute | solution.py:313
  124.5 15.5 %collective-permute-start.4 = (bf16[2,192,2048]{2,1,0:T(8,128)(2,1)}, bf16[2,192,2048]{2,1,0:T(8,128)(2,1)}, u32[]{:S(2)}, u32[]{:S(2)}) collective-permute-start(bf16[2,192,2048]{2,1,0:T(8,128)(2,1)} %collective-permute-done.refs_1_), channel_id=1, source_target_pairs={{0,1},{1,0},{2,3},{3,2},{4,5},{5,4},{6,7},{7,6},{8,9},{9,8},{10,11... | collective-permute-start | bytes 4718600 | tf_op jit(solution)/shard_map/ppermute | solution.py:338
  124.6 15.4 %collective-permute-start.5 = (bf16[2,192,2048]{2,1,0:T(8,128)(2,1)}, bf16[2,192,2048]{2,1,0:T(8,128)(2,1)}, u32[]{:S(2)}, u32[]{:S(2)}) collective-permute-start(bf16[2,192,2048]{2,1,0:T(8,128)(2,1)} %collective-permute-done.1.refs_2_), channel_id=1, source_target_pairs={{0,1},{1,0},{2,3},{3,2},{4,5},{5,4},{6,7},{7,6},{8,9},{9,8},{10,11... | collective-permute-start | bytes 4718600 | tf_op jit(solution)/shard_map/ppermute | solution.py:338
  125.1 14.9 %collective-permute-start.6 = (bf16[2,192,2048]{2,1,0:T(8,128)(2,1)}, bf16[2,192,2048]{2,1,0:T(8,128)(2,1)}, u32[]{:S(2)}, u32[]{:S(2)}) collective-permute-start(bf16[2,192,2048]{2,1,0:T(8,128)(2,1)} %collective-permute-done.2.refs_3_), channel_id=1, source_target_pairs={{0,1},{1,0},{2,3},{3,2},{4,5},{5,4},{6,7},{7,6},{8,9},{9,8},{10,11... | collective-permute-start | bytes 4718600 | tf_op jit(solution)/shard_map/ppermute | solution.py:338
  166.4 11.5 %collective-permute-start.7 = (bf16[2,2,48,1024]{3,2,1,0:T(8,128)(2,1)S(1)}, bf16[2,2,48,1024]{3,2,1,0:T(8,128)(2,1)S(1)}, u32[]{:S(2)}, u32[]{:S(2)}) collective-permute-start(bf16[2,2,48,1024]{3,2,1,0:T(8,128)(2,1)S(1)} %get-tuple-element.53), channel_id=1, source_target_pairs={{0,8},{8,16},{16,24},{24,0},{1,9},{9,17},{17,25},{25,1},{2,10},{10... | collective-permute-start | bytes 1179656 | tf_op jit(solution)/shard_map/ppermute | solution.py:356
  167.2 10.8 %collective-permute-start.9 = (bf16[2,2,48,1024]{3,2,1,0:T(8,128)(2,1)S(1)}, bf16[2,2,48,1024]{3,2,1,0:T(8,128)(2,1)S(1)}, u32[]{:S(2)}, u32[]{:S(2)}) collective-permute-start(bf16[2,2,48,1024]{3,2,1,0:T(8,128)(2,1)S(1)} %get-tuple-element.54), channel_id=1, source_target_pairs={{0,24},{8,0},{16,8},{24,16},{1,25},{9,1},{17,9},{25,17},{2,26},{10... | collective-permute-start | bytes 1179656 | tf_op jit(solution)/shard_map/ppermute | solution.py:356
  169.1 17.7 %collective-permute-start.8 = (bf16[2,2,48,1024]{3,2,1,0:T(8,128)(2,1)S(1)}, bf16[2,2,48,1024]{3,2,1,0:T(8,128)(2,1)S(1)}, u32[]{:S(2)}, u32[]{:S(2)}) collective-permute-start(bf16[2,2,48,1024]{3,2,1,0:T(8,128)(2,1)S(1)} %get-tuple-element.55), channel_id=1, source_target_pairs={{0,16},{8,24},{16,0},{24,8},{1,17},{9,25},{17,1},{25,9},{2,18},{10... | collective-permute-start | bytes 1179656 | tf_op jit(solution)/shard_map/ppermute | solution.py:356
  188.1 25.1 %copy-start.3 = (f32[5,128]{1,0:T(8,128)S(1)}, f32[5,128]{1,0:T(8,128)}, u32[]{:S(2)}) copy-start(f32[5,128]{1,0:T(8,128)} %find_roots.3) | copy-start | bytes 7684
  188.2 25.1 %copy-start.4 = (f32[1,128]{1,0:T(1,128)S(1)}, f32[1,128]{1,0:T(1,128)}, u32[]{:S(2)}) copy-start(f32[1,128]{1,0:T(1,128)} %find_roots.4) | copy-start | bytes 1540
  188.2 40.8 %collective-permute-start.10 = (f32[2,48,1024]{2,1,0:T(8,128)S(1)}, f32[2,48,1024]{2,1,0:T(8,128)S(1)}, u32[]{:S(2)}, u32[]{:S(2)}) collective-permute-start(f32[2,48,1024]{2,1,0:T(8,128)S(1)} %get-tuple-element.57), channel_id=1, source_target_pairs={{0,1},{1,0},{2,3},{3,2},{4,5},{5,4},{6,7},{7,6},{8,9},{9,8},{10,11... | collective-permute-start | bytes 1179656 | tf_op jit(solution)/shard_map/ppermute | solution.py:360
  214.6 12.4 %all-to-all-start.3 = ((f32[16,1,512]{2,1,0:T(1,128)}), f32[16,1,512]{2,1,0:T(1,128)S(1)}, u32[]{:S(2)}, u32[]{:S(2)}) async-start(f32[16,1,512]{2,1,0:T(1,128)} %reshape.64), calls=%async_computation.3 | async-start | bytes 65536 | tf_op jit(solution)/shard_map/all_to_all | solution.py:273

commit v3 on v2

--- a/solution.py
+++ b/solution.py
@@ -13,10 +13,10 @@
 F32 = jnp.float32
 BF16 = jnp.bfloat16
 LANES = 128
-GROUP = 64
-UNROLL = 32
-CUT_A = 5
-CUT_B = 6
+GROUP = 128
+BLOCK = 16
+CUT_A = 2
+CUT_B = 3
 
 
 def cost(flops):
@@ -40,38 +40,58 @@
         ps_ref[part * rows : (part + 1) * rows, :] = pw_ref[part, 0] - base
 
 
-def root_kernel(pw_ref, root_ref, out_ref, w2_ref, ps_ref, c_ref, t_ref, lo_ref, hi_ref):
+def root_kernel(rank_ref, pw_ref, root_ref, out_ref, w2_ref, ps_ref, c_ref, t_ref, lo_ref, hi_ref):
     load_tables(pw_ref, w2_ref)
     groups = root_ref.shape[1]
+    blocks = ps_ref.shape[0] // BLOCK
     for k in range(groups):
         here = pl.ds(k * GROUP, GROUP)
-        c_ref[here, :] = column(root_ref[0, k : k + 1, :])[:GROUP]
-        t_ref[here, :] = column(root_ref[1, k : k + 1, :])[:GROUP]
-        lo_ref[here, :] = column(root_ref[2, k : k + 1, :])[:GROUP]
-        hi_ref[here, :] = column(root_ref[3, k : k + 1, :])[:GROUP]
+        c_ref[here, :] = column(root_ref[0, k : k + 1, :])
+        t_ref[here, :] = column(root_ref[1, k : k + 1, :])
+        lo_ref[here, :] = column(root_ref[2, k : k + 1, :])
+        hi_ref[here, :] = column(root_ref[3, k : k + 1, :])
 
     def group_body(g, carry):
         here = pl.ds(g * GROUP, GROUP)
         base = c_ref[pl.ds(g * GROUP + GROUP // 2, 1), :]
         shift_poles(pw_ref, ps_ref, base)
-        near = c_ref[here, :] - base
+        offset = c_ref[here, :] - base
+        near_block = jnp.clip((rank_ref[0] // LANES + g - BLOCK // 2) // BLOCK, 0, blocks - 2)
 
         def step(_, carry):
             t = t_ref[here, :]
-            s = near + t
-
-            def body(r, sums):
+            s = offset + t
+
+            def near(r, sums):
                 first, second = sums
-                for u in range(UNROLL):
-                    row = pl.ds(r * UNROLL + u, 1)
+                for u in range(BLOCK):
+                    row = pl.ds((near_block + r) * BLOCK + u, 1)
                     inverse = 1.0 / (ps_ref[row, :] - s)
                     weighted = w2_ref[row, :] * inverse
                     first = first + weighted
                     second = second + weighted * inverse
                 return first, second
 
+            def far(i, sums):
+                first, second = sums
+                for half in range(2):
+                    block = 2 * i + half
+                    block = jnp.where(block >= near_block, block + 2, block)
+                    some = None
+                    for u in range(BLOCK):
+                        row = pl.ds(block * BLOCK + u, 1)
+                        distance = (ps_ref[row, :] - s).astype(BF16)
+                        weight = jnp.broadcast_to(w2_ref[row, :], (GROUP, LANES)).astype(BF16)
+                        weighted = weight / distance
+                        square = weighted / distance
+                        some = (weighted, square) if some is None else (some[0] + weighted, some[1] + square)
+                    first = first + some[0].astype(F32)
+                    second = second + some[1].astype(F32)
+                return first, second
+
             zero = jnp.zeros((GROUP, LANES), F32)
-            first, second = lax.fori_loop(0, ps_ref.shape[0] // UNROLL, body, (zero, zero))
+            sums = lax.fori_loop(0, 2, near, (zero, zero))
+            first, second = lax.fori_loop(0, (blocks - 2) // 2, far, sums)
             sum_inverse = jnp.sum(first, axis=1, keepdims=True)
             sum_square = jnp.sum(second, axis=1, keepdims=True)
             nearest = jnp.minimum(jnp.abs(lo_ref[here, :] - t), jnp.abs(hi_ref[here, :] - t))
@@ -83,26 +103,24 @@
         return carry
 
     lax.fori_loop(0, groups, group_body, 0)
-    pad = jnp.zeros((LANES - GROUP, LANES), F32)
     for k in range(groups):
-        t = jnp.concatenate([t_ref[pl.ds(k * GROUP, GROUP), :], pad], axis=0)
-        out_ref[k : k + 1, :] = t.T[0:1, :]
-
-
-def find_roots(pw, root):
+        out_ref[k : k + 1, :] = t_ref[pl.ds(k * GROUP, GROUP), :].T[0:1, :]
+
+
+def find_roots(rank, pw, root):
     groups = root.shape[1]
     n_pole_rows = pw.shape[0] * pw.shape[2]
     roots = groups * GROUP
-    root = jnp.pad(root, ((0, 0), (0, 0), (0, LANES - GROUP)))
-    found = pl.pallas_call(
+    vmem = pl.BlockSpec(memory_space=pltpu.VMEM)
+    return pl.pallas_call(
         root_kernel,
+        in_specs=[pl.BlockSpec(memory_space=pltpu.SMEM), vmem, vmem],
         out_shape=jax.ShapeDtypeStruct((groups, LANES), F32),
         scratch_shapes=[pltpu.VMEM((n_pole_rows, LANES), F32)] * 2
         + [pltpu.VMEM((roots, LANES), F32)] * 4,
         cost_estimate=cost(ITERS * roots * n_pole_rows * LANES * 10),
         name="find_roots",
-    )(pw, root)
-    return found[:, :GROUP]
+    )(rank, pw, root)
 
 
 def panel_kernel(pw_ref, root_ref, out_ref, w2_ref):
@@ -198,13 +216,13 @@
     blocks = refs[:8]
     own_ref, send_ref, p_ref, w_ref = refs[8:]
     sources = 4
-    _, rows, depth = blocks[0].shape
+    rows, depth = blocks[0].shape
     chunk = 256
     chunks = root_ref.shape[1] // chunk
     pieces = depth // LANES
     for src in range(sources):
-        p = jnp.concatenate([col_ref[0, src, 0]] * (LANES // pieces), axis=0).T
-        w = jnp.concatenate([col_ref[1, src, 0]] * (LANES // pieces), axis=0).T
+        p = jnp.concatenate([col_ref[0, src]] * (LANES // pieces), axis=0).T
+        w = jnp.concatenate([col_ref[1, src]] * (LANES // pieces), axis=0).T
         for piece in range(pieces):
             here = pl.ds(src * depth + piece * LANES, LANES)
             p_ref[here, :] = jnp.broadcast_to(p[:, piece : piece + 1], (LANES, LANES))
@@ -228,7 +246,7 @@
     def body(k, carry):
         acc = None
         for src in range(sources):
-            left = jnp.concatenate([blocks[src][0], blocks[sources + src][0]], axis=0)
+            left = jnp.concatenate([blocks[src][...], blocks[sources + src][...]], axis=0)
             product = jnp.dot(left, cauchy(src, k), preferred_element_type=F32)
             acc = product if acc is None else acc + product
         quarter = rows // 4
@@ -236,8 +254,8 @@
             for side in range(2):
                 first = side * rows + part * quarter
                 piece = acc[first : first + quarter]
-                own_ref[part, 0, side, :, pl.ds(k * chunk, chunk)] = piece
-                send_ref[part, 0, side, :, pl.ds(k * chunk, chunk)] = piece.astype(BF16)
+                own_ref[part, side, :, pl.ds(k * chunk, chunk)] = piece
+                send_ref[part, side, :, pl.ds(k * chunk, chunk)] = piece.astype(BF16)
         return carry
 
     lax.fori_loop(0, chunks, body, 0)
@@ -245,27 +263,18 @@
 
 def panel_product(columns, root, blocks):
     sources = 4
-    halves, rows, depth = blocks[0].shape
+    rows, depth = blocks[0].shape
     n_roots = root.shape[1]
     pieces = depth // LANES
-    shape = (4, halves, 2, rows // 4, n_roots)
-    out = pl.BlockSpec((4, 1, 2, rows // 4, n_roots), lambda h: (0, h, 0, 0, 0))
-    block = pl.BlockSpec((1, rows, depth), lambda h: (h, 0, 0))
+    shape = (4, 2, rows // 4, n_roots)
     return pl.pallas_call(
         matmul_kernel,
-        grid=(halves,),
-        in_specs=[
-            pl.BlockSpec((2, sources, 1, pieces, LANES), lambda h: (0, 0, h, 0, 0)),
-            pl.BlockSpec((3, n_roots), lambda h: (0, 0)),
-        ]
-        + [block] * 8,
-        out_specs=(out, out),
         out_shape=(jax.ShapeDtypeStruct(shape, F32), jax.ShapeDtypeStruct(shape, BF16)),
         scratch_shapes=[pltpu.VMEM((sources * depth, LANES), F32)] * 2,
         compiler_params=pltpu.CompilerParams(vmem_limit_bytes=56 << 20),
-        cost_estimate=cost(2 * 2 * sources * halves * rows * depth * n_roots),
+        cost_estimate=cost(2 * 2 * sources * rows * depth * n_roots),
         name="panel_product",
-    )(columns.reshape(2, sources, halves, pieces, LANES), root, *blocks)
+    )(columns.reshape(2, sources, pieces, LANES), root, *blocks)
 
 
 def copies(value, axis):
@@ -292,7 +301,20 @@
     parted = jnp.stack([pole_values.reshape(-1, LANES), weights.reshape(-1, LANES)])
     pw = copies(parted, ROW)
 
-    turned = jnp.moveaxis(eigen_blocks.reshape(4, -1, 2, eigen_blocks.shape[2]), 2, 1)
+    axes = ("z", "x")
+    places = (z, x)
+    wide = eigen_blocks.reshape(4, 4, -1, 2, eigen_blocks.shape[2])
+    turned = (
+        wide[:, :, :, 0].reshape(4, -1, eigen_blocks.shape[2]),
+        jnp.swapaxes(wide[:, :, :, 1], 0, 1).reshape(4, -1, eigen_blocks.shape[2]),
+    )
+    cut = [
+        [
+            lax.dynamic_index_in_dim(turned[half], (places[half] + shift) % 4, 0, keepdims=False)
+            for shift in range(4)
+        ]
+        for half in range(2)
+    ]
 
     wanted = lax.dynamic_slice_in_dim(chosen, row * LANES, LANES)
     local = wanted - col * n_col
@@ -304,20 +326,22 @@
         ]
     )
     spread = jnp.moveaxis(first.reshape(2, 8, 16), 1, 0)
+    pw, spread = lax.optimization_barrier((pw, spread))
     arrived = lax.all_to_all(spread, COL, 0, 0, tiled=True)
-    pw, turned, arrived = lax.optimization_barrier((pw, turned, arrived))
-    eigen = [lax.dynamic_index_in_dim(turned, z, 0, keepdims=False)]
+    index = lax.dynamic_slice_in_dim(column_pole.reshape(-1, LANES), col * 4, 4)
+    picked = pick_columns(index, pw)
+    cut, arrived = lax.optimization_barrier((cut, arrived))
+
+    eigen = [[cut[0][0]], [cut[1][0]]]
     for shift in (1, 2, 3):
-        block = lax.dynamic_index_in_dim(turned, (z + shift) % 4, 0, keepdims=False)
-        eigen.append(lax.ppermute(block, "z", ring(shift)))
-    peer = [lax.ppermute(eigen[0], "core", swap)]
+        for half in range(2):
+            eigen[half].append(lax.ppermute(cut[half][shift], axes[half], ring(shift)))
+    peer = [[lax.ppermute(eigen[half][0], "core", swap)] for half in range(2)]
 
     panel_start = jnp.pad(
         jnp.sum(arrived, axis=0), ((0, 0), (0, LANES - 16)), constant_values=0.25
     )
     panel_end = panel_roots(pw, panel_start)
-    index = lax.dynamic_slice_in_dim(column_pole.reshape(-1, LANES), col * 4, 4)
-    picked = pick_columns(index, pw)
     note = jnp.concatenate([picked.reshape(8, LANES), panel_start[:1], panel_end], axis=0)
     notes = copies(note, ALL)
 
@@ -332,30 +356,44 @@
     last = start + jnp.arange(n_own) == pole_values.shape[0] * 16 - 1
     high = jnp.where(last, 3e38, -low)
     state = jnp.stack([my_centers, my_offsets, low, high]).reshape(4, -1, GROUP)
-    roots_a = find_roots(pw, state[:, :CUT_A])
+    rank = start.reshape(1)
+    roots_a = find_roots(rank, pw, state[:, :CUT_A])
     eigen, notes, roots_a = lax.optimization_barrier((eigen, notes, roots_a))
 
-    peer += [lax.ppermute(block, "core", swap) for block in eigen[1:]]
-    roots_b = find_roots(pw, state[:, CUT_A:CUT_B])
-
-    columns = lax.dynamic_index_in_dim(
-        notes[:, :8].reshape(4, 4, 8, 2, 4, LANES), x, 1, keepdims=False
-    )
-    columns = jnp.concatenate(
-        [lax.dynamic_slice_in_dim(columns, (z - s) % 4, 1) for s in range(4)]
-    )
-    columns = jnp.moveaxis(columns, 2, 0)
+    for half in range(2):
+        peer[half] += [lax.ppermute(block, "core", swap) for block in eigen[half][1:]]
+    roots_b = find_roots(rank + CUT_A * GROUP, pw, state[:, CUT_A:CUT_B])
+
+    table = notes[:, :8].reshape(4, 4, 2, 4, 2, 4, LANES)
+    columns = (
+        lax.dynamic_index_in_dim(table[:, :, 0], x, 1, keepdims=False),
+        lax.dynamic_index_in_dim(table[:, :, 1], z, 0, keepdims=False),
+    )
+    columns = [
+        jnp.moveaxis(
+            jnp.concatenate(
+                [lax.dynamic_slice_in_dim(c, (place - s) % 4, 1) for s in range(4)]
+            ),
+            2,
+            0,
+        ).reshape(2, -1, LANES)
+        for c, place in zip(columns, places)
+    ]
     panel_root = jnp.moveaxis(notes[:, 8:, :16], 1, 0).reshape(3, 2, -1)
     panel_root = lax.dynamic_index_in_dim(panel_root, core, 1, keepdims=False)
-    panel_root, peer, roots_b = lax.optimization_barrier((panel_root, peer, roots_b))
-    own, send = panel_product(columns, panel_root, eigen + peer)
-
-    pieces = [lax.dynamic_index_in_dim(own, x, 0, keepdims=False)]
-    for shift in (1, 2, 3):
-        piece = lax.dynamic_index_in_dim(send, (x + shift) % 4, 0, keepdims=False)
-        pieces.append(lax.ppermute(piece, "x", ring(shift)))
-    roots_c = find_roots(pw, state[:, CUT_B:])
-    total = pieces[0] + pieces[1] + pieces[2] + pieces[3]
+    panel_root, columns, peer, roots_b = lax.optimization_barrier(
+        (panel_root, columns, peer, roots_b)
+    )
+    pieces = []
+    for half in range(2):
+        own, send = panel_product(columns[half], panel_root, eigen[half] + peer[half])
+        other = places[1 - half]
+        pieces.append([lax.dynamic_index_in_dim(own, other, 0, keepdims=False)])
+        for shift in (1, 2, 3):
+            piece = lax.dynamic_index_in_dim(send, (other + shift) % 4, 0, keepdims=False)
+            pieces[half].append(lax.ppermute(piece, axes[1 - half], ring(shift)))
+    roots_c = find_roots(rank + CUT_B * GROUP, pw, state[:, CUT_B:])
+    total = jnp.stack([p[0] + p[1] + p[2] + p[3] for p in pieces])
     keep = total[:, 0]
     got = lax.ppermute(total[:, 1], "core", swap)
     roots = copies(jnp.concatenate([roots_a, roots_b, roots_c]), ROW)

time: 232 us -> 217 us (0.935)
  Pallas kernels: 129 us -> 115 us
  waiting for transfers between devices: 29 us -> 16.7 us
  starting transfers between devices: 36.4 us -> 47.5 us
  other arithmetic: 7.97 us -> 10.9 us
  local copies, waits for them, and re-layouts: 27.7 us -> 25.1 us
    pallas_call x4 -> x5, Pallas kernels: 115 us -> 101 us  [the longest x3 71.5 us: find_roots(): pl.pallas_call(root_kernel, in_specs=[pl.BlockSpec(memory_space=pltpu.SME...]
    ppermute x10 -> x20, starting transfers between devices: 7.53 us -> 21.4 us  [the longest x6 9.87 us: merge(): eigen[half].append(lax.ppermute(cut[half][shift], axes[half], ring(shift)))]
    reshape x2 -> x0, local copies, waits for them, and re-layouts: 9.06 us -> none  [the longest x1 8.37 us: merge(): eigen_blocks.reshape(4, -1, 2, eigen_blocks.shape[2])]
    ppermute x10 -> x20, waiting for transfers between devices: 16.7 us -> 10.3 us  [the longest x6 6.49 us: merge(): pieces[half].append(lax.ppermute(piece, axes[1 - half], ring(shift)))]
    unnamed x17 -> x25, local copies, waits for them, and re-layouts: 2.92 us -> 6.96 us
    all_to_all x1, waiting for transfers between devices: 3.88 us -> 0.01 us  [merge(): arrived = lax.all_to_all(spread, COL, 0, 0, tiled=True)]
    all_to_all x3, starting transfers between devices: 21.6 us -> 18.8 us  [copies(): lax.all_to_all(jnp.broadcast_to(value[None], (size, *value.shape)), axis,...]
    transpose x2 -> x4, local copies, waits for them, and re-layouts: 1.3 us -> 3.9 us  [the longest x2 2.62 us: merge(): jnp.swapaxes(wide[:, :, :, 1], 0, 1).reshape(4, -1, eigen_blocks.shape[2])]
  transfers between devices with their start and end apart: 15 -> 25, of which waited for: 5 -> 7; matrix products, arithmetic and copies ran while one was open for 9% -> 13% of each run, Pallas kernels for 45% -> 46%
where the time goes in v3:
time: 217 us; the launch traced here: 216 us
  Pallas kernels  115 us (53%)
  starting transfers between devices  47.5 us (22%)
  local copies, waits for them, and re-layouts  25.1 us (12%)
  waiting for transfers between devices  16.7 us (8%)
  other arithmetic  10.9 us (5%)
    pallas_call x3, Pallas kernels, find_roots(): pl.pallas_call(root_kernel, in_specs=[pl.BlockSpec(memory_space=pltpu.SME...  71.5 us
    pallas_call x2, Pallas kernels, panel_product(): pl.pallas_call(matmul_kernel, out_shape=(jax.ShapeDtypeStruct(shape, F32)...  29.5 us
    all_to_all x3, starting transfers between devices, copies(): lax.all_to_all(jnp.broadcast_to(value[None], (size, *value.shape)), axis,...  18.8 us
    ppermute x6, starting transfers between devices, merge(): eigen[half].append(lax.ppermute(cut[half][shift], axes[half], ring(shift)))  9.87 us
    pallas_call x1, Pallas kernels, panel_roots(): pl.pallas_call(panel_kernel, out_shape=jax.ShapeDtypeStruct((2, LANES), F...  8.5 us
    ppermute x6, starting transfers between devices, merge(): pieces[half].append(lax.ppermute(piece, axes[1 - half], ring(shift)))  8.37 us
    unnamed x25, local copies, waits for them, and re-layouts  6.96 us
    ppermute x6, waiting for transfers between devices, merge(): pieces[half].append(lax.ppermute(piece, axes[1 - half], ring(shift)))  6.49 us
  transfers between devices with their start and end apart: 25, of which 7 were waited for; matrix products, arithmetic and copies ran while one was open for 13% of the time, Pallas kernels for 46%

profile of v3, /device:TPU:1, one launch (start us, length us, event | category | flops | bytes accessed | tf_op | source)
XLA Modules:
  0.0 215.9 jit_solution(15205217839227131318)
XLA Ops:
  2.2 8.5 %all-to-all-start = ((f32[16,2,32,128]{3,2,1,0:T(8,128)}), f32[16,2,32,128]{3,2,1,0:T(8,128)}, u32[]{:S(2)}, u32[]{:S(2)}) async-start(f32[16,2,32,128]{3,2,1,0:T(8,128)} %broadcast_in_dim.43), calls=%async_computation | async-start | bytes 1048576 | tf_op jit(solution)/shard_map/all_to_all | solution.py:282
  11.6 2.1 select_reduce_fusion.1
  13.9 5.7 %copy.26 = bf16[768,2,2048]{2,0,1:T(8,128)(2,1)S(1)} copy(bf16[768,2,2048]{2,1,0:T(2,128)(2,1)} %param.13) | data formatting | bytes 12582912 | tf_op args[6]
  19.6 2.2 %slice_bitcast_fusion = (bf16[4,4,48,2048]{3,2,0,1:T(8,128)(2,1)S(1)}, bf16[4,4,48,1,2048]{4,2,1,0,3:T(8,128)(2,1)}) fusion(bf16[4,4,48,2,2048]{4,2,1,0,3:T(8,128)(2,1)S(1)} %bitcast.101), kind=kLoop, calls=%fused_computation.3 | loop fusion | bytes 12582912 | tf_op jit(solution)/shard_map/transpose | solution.py:309
  22.9 5.4 %all-to-all-start.1 = ((f32[8,2,16]{2,1,0:T(2,128)}), f32[8,2,16]{2,1,0:T(2,128)S(1)}, u32[]{:S(2)}, u32[]{:S(2)}) async-start(f32[8,2,16]{2,1,0:T(2,128)} %copy.28), calls=%async_computation.1 | async-start | bytes 16384 | tf_op jit(solution)/shard_map/all_to_all | solution.py:330
  28.3 4.6 %dynamic-slice_bitcast_fusion = (bf16[192,2048]{1,0:T(8,128)(2,1)}, bf16[192,2048]{1,0:T(8,128)(2,1)}, bf16[192,2048]{1,0:T(8,128)(2,1)}, bf16[192,2048]{1,0:T(8...) fusion(bf16[4,192,2048]{2,1,0:T(8,128)(2,1)S(1)} %bitcast.102, ...), kind=kLoop, calls=%fused_computation.8 | loop fusion | bytes 12582944 | tf_op jit(solution)/shard_map/jit(dynamic_index_in_dim)/squeeze | solution.py:313
  32.9 1.5 collective-permute-start
  35.0 5.0 %pick_columns.1 = f32[2,4,128]{2,1,0:T(4,128)} custom-call(s32[4,128]{1,0:T(4,128)} %constant_dynamic-slice_fusion.2.index_ref, f32[16,2,32,128]{3,2,1,0:T(8,128)} %all-to-all-done.pw_ref), custom_call_target="tpu_custom_call" | custom-call | flops 50000000 | bytes 1048576 | tf_op jit(solution)/shard_map/pick_columns/pallas_call | solution.py:207
  40.1 2.4 %collective-permute-start.1 = (bf16[192,2048]{1,0:T(8,128)(2,1)}, bf16[192,2048]{1,0:T(8,128)(2,1)}, u32[]{:S(2)}, u32[]{:S(2)}) collective-permute-start(bf16[192,2048]{1,0:T(8,128)(2,1)} %get-tuple-element.42), channel_id=1, source_target_pairs={{0,64},{32,96},{64,0},{96,32},{1,65},{33,97},{65,1},{97,33},{2,66}... | collective-permute-start | bytes 2359304 | tf_op jit(solution)/shard_map/ppermute | solution.py:338
  42.5 1.2 collective-permute-start.2
  43.7 1.2 collective-permute-start.3
  44.8 2.4 %collective-permute-start.4 = (bf16[192,2048]{1,0:T(8,128)(2,1)}, bf16[192,2048]{1,0:T(8,128)(2,1)}, u32[]{:S(2)}, u32[]{:S(2)}) collective-permute-start(bf16[192,2048]{1,0:T(8,128)(2,1)} %get-tuple-element.46), channel_id=1, source_target_pairs={{0,16},{8,24},{16,0},{24,8},{1,17},{9,25},{17,1},{25,9},{2,18},{10... | collective-permute-start | bytes 2359304 | tf_op jit(solution)/shard_map/ppermute | solution.py:338
  47.9 8.5 %panel_roots.1 = f32[2,128]{1,0:T(2,128)} custom-call(f32[16,2,32,128]{3,2,1,0:T(8,128)} %all-to-all-done.pw_ref, f32[2,128]{1,0:T(2,128)} %pad.4.root_ref), custom_call_target="tpu_custom_call" | custom-call | flops 52428800 | bytes 1048576 | tf_op jit(solution)/shard_map/panel_roots/pallas_call | solution.py:171
  56.4 1.3 collective-permute-start.5
  59.4 6.2 %all-to-all-start.2 = ((f32[128,11,128]{2,1,0:T(8,128)}), f32[128,11,128]{2,1,0:T(8,128)S(1)}, u32[]{:S(2)}, u32[]{:S(2)}) async-start(f32[128,11,128]{2,1,0:T(8,128)} %broadcast_in_dim.47), calls=%async_computation.2 | async-start | bytes 2097152 | tf_op jit(solution)/shard_map/all_to_all | solution.py:282
  65.6 1.3 reshape.83
  68.3 34.9 %find_roots.3 = f32[2,128]{1,0:T(2,128)} custom-call(s32[1]{0:T(128)} %bitcast.17.rank_ref, f32[16,2,32,128]{3,2,1,0:T(8,128)} %all-to-all-done.pw_ref, f32[4,2,128]{2,1,0:T(2,128)} %slice.50.root_ref), custom_call_target="tpu_custom_call" | custom-call | flops 503316480 | bytes 1048576 | tf_op jit(solution)/shard_map/find_roots/pallas_call | solution.py:115
  105.7 18.3 %find_roots.4 = f32[1,128]{1,0:T(1,128)} custom-call(s32[1]{0:T(128)S(6)} %add.309.rank_ref, f32[16,2,32,128]{3,2,1,0:T(8,128)} %all-to-all-done.pw_ref, f32[4,1,128]{2,1,0:T(1,128)} %get-tuple-element.109.root_ref), custom_call_target="tpu_custom_call" | custom-call | flops 251658240 | bytes 1048576 | tf_op jit(solution)/shard_map/find_roots/pallas_call | solution.py:115
  131.3 14.9 %panel_product.2 = (f32[4,2,48,1024]{3,2,1,0:T(8,128)}, bf16[4,2,48,1024]{3,2,1,0:T(8,128)(2,1)}) custom-call(f32[2,4,16,128]{3,2,1,0:T(8,128)} %bitcast.107, f32[3,1024]{1,0:T(4,128)} %bitcast.109, bf16[192,2048]{1,0:T(8,128)(2,1)} %get-tuple-element.61.refs_0_, bf16[192,2048]{1,0:T(8,128)(2,1)} %copy-done.5, ...), custom_call_target="tpu_custom_call" | custom-call | flops 6442450944 | bytes 1048576 | tf_op jit(solution)/shard_map/panel_product/pallas_call | solution.py:270
  146.3 1.2 dynamic-slice_bitcast_fusion.13
  148.2 2.0 collective-permute-start.16
  151.2 14.6 %panel_product.3 = (f32[4,2,48,1024]{3,2,1,0:T(8,128)}, bf16[4,2,48,1024]{3,2,1,0:T(8,128)(2,1)}) custom-call(f32[2,4,16,128]{3,2,1,0:T(8,128)} %bitcast.106, f32[3,1024]{1,0:T(4,128)} %bitcast.110, bf16[192,2048]{1,0:T(8,128)(2,1)} %get-tuple-element.69.refs_0_, bf16[192,2048]{1,0:T(8,128)(2,1)} %collective-permute-done.3.refs_1_, ...), custom_call_target="tpu_custom_call" | custom-call | flops 6442450944 | bytes 1048576 | tf_op jit(solution)/shard_map/panel_product/pallas_call | solution.py:270
  166.9 1.4 collective-permute-start.17
  168.3 1.8 collective-permute-start.19
  170.1 1.4 collective-permute-start.18
  172.9 1.4 collective-permute-done.17
  174.3 5.1 %collective-permute-done.18 = bf16[2,48,1024]{2,1,0:T(8,128)(2,1)S(1)} collective-permute-done((bf16[2,48,1024]{2,1,0:T(8,128)(2,1)S(1)}, bf16[2,48,1024]{2,1,0:T(8,128)(2,1)S(1)}, u32[]{:S(2)}, u32[]{:S(2)}) %collective-permute-start.18) | collective-permute-done | bytes 196640 | tf_op jit(solution)/shard_map/ppermute | solution.py:394
  181.5 1.9 collective-permute-start.20
  183.5 18.3 %find_roots.5 = f32[1,128]{1,0:T(1,128)} custom-call(s32[1]{0:T(128)S(6)} %add.310.rank_ref, f32[16,2,32,128]{3,2,1,0:T(8,128)} %all-to-all-done.pw_ref, f32[4,1,128]{2,1,0:T(1,128)} %get-tuple-element.110.root_ref), custom_call_target="tpu_custom_call" | custom-call | flops 251658240 | bytes 1048576 | tf_op jit(solution)/shard_map/find_roots/pallas_call | solution.py:115
  203.0 4.2 %all-to-all-start.3 = ((f32[16,4,128]{2,1,0:T(4,128)}), f32[16,4,128]{2,1,0:T(4,128)S(1)}, u32[]{:S(2)}, u32[]{:S(2)}) async-start(f32[16,4,128]{2,1,0:T(4,128)} %broadcast_in_dim.49), calls=%async_computation.3 | async-start | bytes 65536 | tf_op jit(solution)/shard_map/all_to_all | solution.py:282
  207.2 6.4 %all-to-all-done.3 = f32[16,4,128]{2,1,0:T(4,128)S(1)} async-done(((f32[16,4,128]{2,1,0:T(4,128)}), f32[16,4,128]{2,1,0:T(4,128)S(1)}, u32[]{:S(2)}, u32[]{:S(2)}) %all-to-all-start.3) | async-done | bytes 32800 | tf_op jit(solution)/shard_map/all_to_all | solution.py:282
  213.7 1.6 fusion
  (96 shorter events, 25.9 us)
Async XLA Ops:
  2.2 20.0 %all-to-all-start = ((f32[16,2,32,128]{3,2,1,0:T(8,128)}), f32[16,2,32,128]{3,2,1,0:T(8,128)}, u32[]{:S(2)}, u32[]{:S(2)}) async-start(f32[16,2,32,128]{3,2,1,0:T(8,128)} %broadcast_in_dim.43), calls=%async_computation | async-start | bytes 1048576 | tf_op jit(solution)/shard_map/all_to_all | solution.py:282
  22.9 10.1 %all-to-all-start.1 = ((f32[8,2,16]{2,1,0:T(2,128)}), f32[8,2,16]{2,1,0:T(2,128)S(1)}, u32[]{:S(2)}, u32[]{:S(2)}) async-start(f32[8,2,16]{2,1,0:T(2,128)} %copy.28), calls=%async_computation.1 | async-start | bytes 16384 | tf_op jit(solution)/shard_map/all_to_all | solution.py:330
  32.9 23.4 %collective-permute-start = (bf16[192,2048]{1,0:T(8,128)(2,1)}, bf16[192,2048]{1,0:T(8,128)(2,1)S(1)}, u32[]{:S(2)}, u32[]{:S(2)}) collective-permute-start(bf16[192,2048]{1,0:T(8,128)(2,1)} %get-tuple-element.41), channel_id=1, source_target_pairs={{0,32},{32,64},{64,96},{96,0},{1,33},{33,65},{65,97},{97,1},{2,34}... | collective-permute-start | bytes 2359304 | tf_op jit(solution)/shard_map/ppermute | solution.py:338
  40.1 63.2 %collective-permute-start.1 = (bf16[192,2048]{1,0:T(8,128)(2,1)}, bf16[192,2048]{1,0:T(8,128)(2,1)}, u32[]{:S(2)}, u32[]{:S(2)}) collective-permute-start(bf16[192,2048]{1,0:T(8,128)(2,1)} %get-tuple-element.42), channel_id=1, source_target_pairs={{0,64},{32,96},{64,0},{96,32},{1,65},{33,97},{65,1},{97,33},{2,66}... | collective-permute-start | bytes 2359304 | tf_op jit(solution)/shard_map/ppermute | solution.py:338
  42.5 61.9 %collective-permute-start.2 = (bf16[192,2048]{1,0:T(8,128)(2,1)}, bf16[192,2048]{1,0:T(8,128)(2,1)}, u32[]{:S(2)}, u32[]{:S(2)}) collective-permute-start(bf16[192,2048]{1,0:T(8,128)(2,1)} %get-tuple-element.43), channel_id=1, source_target_pairs={{0,96},{32,0},{64,32},{96,64},{1,97},{33,1},{65,33},{97,65},{2,98}... | collective-permute-start | bytes 2359304 | tf_op jit(solution)/shard_map/ppermute | solution.py:338
  43.7 60.8 %collective-permute-start.3 = (bf16[192,2048]{1,0:T(8,128)(2,1)}, bf16[192,2048]{1,0:T(8,128)(2,1)}, u32[]{:S(2)}, u32[]{:S(2)}) collective-permute-start(bf16[192,2048]{1,0:T(8,128)(2,1)} %get-tuple-element.45), channel_id=1, source_target_pairs={{0,8},{8,16},{16,24},{24,0},{1,9},{9,17},{17,25},{25,1},{2,10},{10... | collective-permute-start | bytes 2359304 | tf_op jit(solution)/shard_map/ppermute | solution.py:338
  44.8 59.6 %collective-permute-start.4 = (bf16[192,2048]{1,0:T(8,128)(2,1)}, bf16[192,2048]{1,0:T(8,128)(2,1)}, u32[]{:S(2)}, u32[]{:S(2)}) collective-permute-start(bf16[192,2048]{1,0:T(8,128)(2,1)} %get-tuple-element.46), channel_id=1, source_target_pairs={{0,16},{8,24},{16,0},{24,8},{1,17},{9,25},{17,1},{25,9},{2,18},{10... | collective-permute-start | bytes 2359304 | tf_op jit(solution)/shard_map/ppermute | solution.py:338
  56.4 46.9 %copy-start.1 = (bf16[192,2048]{1,0:T(8,128)(2,1)S(1)}, bf16[192,2048]{1,0:T(8,128)(2,1)}, u32[]{:S(2)}) copy-start(bf16[192,2048]{1,0:T(8,128)(2,1)} %get-tuple-element.61.refs_0_) | copy-start | bytes 2359300
  56.4 48.0 %copy-start = (bf16[192,2048]{1,0:T(8,128)(2,1)S(1)}, bf16[192,2048]{1,0:T(8,128)(2,1)}, u32[]{:S(2)}) copy-start(bf16[192,2048]{1,0:T(8,128)(2,1)} %get-tuple-element.69.refs_0_) | copy-start | bytes 2359300
  56.4 48.1 %collective-permute-start.5 = (bf16[192,2048]{1,0:T(8,128)(2,1)}, bf16[192,2048]{1,0:T(8,128)(2,1)}, u32[]{:S(2)}, u32[]{:S(2)}) collective-permute-start(bf16[192,2048]{1,0:T(8,128)(2,1)} %get-tuple-element.47), channel_id=1, source_target_pairs={{0,24},{8,0},{16,8},{24,16},{1,25},{9,1},{17,9},{25,17},{2,26},{10... | collective-permute-start | bytes 2359304 | tf_op jit(solution)/shard_map/ppermute | solution.py:338
  59.4 45.1 %all-to-all-start.2 = ((f32[128,11,128]{2,1,0:T(8,128)}), f32[128,11,128]{2,1,0:T(8,128)S(1)}, u32[]{:S(2)}, u32[]{:S(2)}) async-start(f32[128,11,128]{2,1,0:T(8,128)} %broadcast_in_dim.47), calls=%async_computation.2 | async-start | bytes 2097152 | tf_op jit(solution)/shard_map/all_to_all | solution.py:282
  103.3 21.6 %collective-permute-start.6 = (bf16[192,2048]{1,0:T(8,128)(2,1)S(1)}, bf16[192,2048]{1,0:T(8,128)(2,1)}, u32[]{:S(2)}, u32[]{:S(2)}) collective-permute-start(bf16[192,2048]{1,0:T(8,128)(2,1)S(1)} %copy-done.1), channel_id=1, source_target_pairs={{0,1},{1,0},{2,3},{3,2},{4,5},{5,4},{6,7},{7,6},{8,9},{9,8},{10,11... | collective-permute-start | bytes 2359304 | tf_op jit(solution)/shard_map/ppermute | solution.py:339
  104.3 20.7 %collective-permute-start.10 = (bf16[192,2048]{1,0:T(8,128)(2,1)S(1)}, bf16[192,2048]{1,0:T(8,128)(2,1)}, u32[]{:S(2)}, u32[]{:S(2)}) collective-permute-start(bf16[192,2048]{1,0:T(8,128)(2,1)S(1)} %copy-done), channel_id=1, source_target_pairs={{0,1},{1,0},{2,3},{3,2},{4,5},{5,4},{6,7},{7,6},{8,9},{9,8},{10,11... | collective-permute-start | bytes 2359304 | tf_op jit(solution)/shard_map/ppermute | solution.py:339
  104.5 20.9 %collective-permute-start.7 = (bf16[192,2048]{1,0:T(8,128)(2,1)}, bf16[192,2048]{1,0:T(8,128)(2,1)}, u32[]{:S(2)}, u32[]{:S(2)}) collective-permute-start(bf16[192,2048]{1,0:T(8,128)(2,1)} %copy-done.5), channel_id=1, source_target_pairs={{0,1},{1,0},{2,3},{3,2},{4,5},{5,4},{6,7},{7,6},{8,9},{9,8},{10,11... | collective-permute-start | bytes 2359304 | tf_op jit(solution)/shard_map/ppermute | solution.py:364
  124.3 3.3 %collective-permute-start.8 = (bf16[192,2048]{1,0:T(8,128)(2,1)}, bf16[192,2048]{1,0:T(8,128)(2,1)S(1)}, u32[]{:S(2)}, u32[]{:S(2)}) collective-permute-start(bf16[192,2048]{1,0:T(8,128)(2,1)} %collective-permute-done.1.refs_2_), channel_id=1, source_target_pairs={{0,1},{1,0},{2,3},{3,2},{4,5},{5,4},{6,7},{7,6},{8,9},{9,8},{10,11... | collective-permute-start | bytes 2359304 | tf_op jit(solution)/shard_map/ppermute | solution.py:364
  124.5 3.4 %collective-permute-start.9 = (bf16[192,2048]{1,0:T(8,128)(2,1)}, bf16[192,2048]{1,0:T(8,128)(2,1)S(1)}, u32[]{:S(2)}, u32[]{:S(2)}) collective-permute-start(bf16[192,2048]{1,0:T(8,128)(2,1)} %collective-permute-done.2.refs_3_), channel_id=1, source_target_pairs={{0,1},{1,0},{2,3},{3,2},{4,5},{5,4},{6,7},{7,6},{8,9},{9,8},{10,11... | collective-permute-start | bytes 2359304 | tf_op jit(solution)/shard_map/ppermute | solution.py:364
  124.8 4.2 %collective-permute-start.11 = (bf16[192,2048]{1,0:T(8,128)(2,1)}, bf16[192,2048]{1,0:T(8,128)(2,1)S(1)}, u32[]{:S(2)}, u32[]{:S(2)}) collective-permute-start(bf16[192,2048]{1,0:T(8,128)(2,1)} %collective-permute-done.3.refs_1_), channel_id=1, source_target_pairs={{0,1},{1,0},{2,3},{3,2},{4,5},{5,4},{6,7},{7,6},{8,9},{9,8},{10,11... | collective-permute-start | bytes 2359304 | tf_op jit(solution)/shard_map/ppermute | solution.py:364
  125.0 5.2 %collective-permute-start.12 = (bf16[192,2048]{1,0:T(8,128)(2,1)}, bf16[192,2048]{1,0:T(8,128)(2,1)S(1)}, u32[]{:S(2)}, u32[]{:S(2)}) collective-permute-start(bf16[192,2048]{1,0:T(8,128)(2,1)} %collective-permute-done.4.refs_2_), channel_id=1, source_target_pairs={{0,1},{1,0},{2,3},{3,2},{4,5},{5,4},{6,7},{7,6},{8,9},{9,8},{10,11... | collective-permute-start | bytes 2359304 | tf_op jit(solution)/shard_map/ppermute | solution.py:364
  125.4 6.0 %collective-permute-start.13 = (bf16[192,2048]{1,0:T(8,128)(2,1)}, bf16[192,2048]{1,0:T(8,128)(2,1)S(1)}, u32[]{:S(2)}, u32[]{:S(2)}) collective-permute-start(bf16[192,2048]{1,0:T(8,128)(2,1)} %collective-permute-done.5.refs_3_), channel_id=1, source_target_pairs={{0,1},{1,0},{2,3},{3,2},{4,5},{5,4},{6,7},{7,6},{8,9},{9,8},{10,11... | collective-permute-start | bytes 2359304 | tf_op jit(solution)/shard_map/ppermute | solution.py:364
  129.1 17.2 %copy-start.6 = (bf16[192,2048]{1,0:T(8,128)(2,1)}, bf16[192,2048]{1,0:T(8,128)(2,1)S(1)}, u32[]{:S(2)}) copy-start(bf16[192,2048]{1,0:T(8,128)(2,1)S(1)} %collective-permute-done.11.refs_5_) | copy-start | bytes 2359300
  130.2 16.0 %copy-start.7 = (bf16[192,2048]{1,0:T(8,128)(2,1)}, bf16[192,2048]{1,0:T(8,128)(2,1)S(1)}, u32[]{:S(2)}) copy-start(bf16[192,2048]{1,0:T(8,128)(2,1)S(1)} %collective-permute-done.12.refs_6_) | copy-start | bytes 2359300
  131.3 14.9 %copy-start.8 = (bf16[192,2048]{1,0:T(8,128)(2,1)}, bf16[192,2048]{1,0:T(8,128)(2,1)S(1)}, u32[]{:S(2)}) copy-start(bf16[192,2048]{1,0:T(8,128)(2,1)S(1)} %collective-permute-done.13.refs_7_) | copy-start | bytes 2359300
  147.4 22.7 %collective-permute-start.14 = (bf16[2,48,1024]{2,1,0:T(8,128)(2,1)S(1)}, bf16[2,48,1024]{2,1,0:T(8,128)(2,1)S(1)}, u32[]{:S(2)}, u32[]{:S(2)}) collective-permute-start(bf16[2,48,1024]{2,1,0:T(8,128)(2,1)S(1)} %get-tuple-element.90), channel_id=1, source_target_pairs={{0,8},{8,16},{16,24},{24,0},{1,9},{9,17},{17,25},{25,1},{2,10},{10... | collective-permute-start | bytes 589832 | tf_op jit(solution)/shard_map/ppermute | solution.py:394
  148.2 23.4 %collective-permute-start.16 = (bf16[2,48,1024]{2,1,0:T(8,128)(2,1)S(1)}, bf16[2,48,1024]{2,1,0:T(8,128)(2,1)S(1)}, u32[]{:S(2)}, u32[]{:S(2)}) collective-permute-start(bf16[2,48,1024]{2,1,0:T(8,128)(2,1)S(1)} %get-tuple-element.91), channel_id=1, source_target_pairs={{0,24},{8,0},{16,8},{24,16},{1,25},{9,1},{17,9},{25,17},{2,26},{10... | collective-permute-start | bytes 589832 | tf_op jit(solution)/shard_map/ppermute | solution.py:394
  150.2 21.4 %collective-permute-start.15 = (bf16[2,48,1024]{2,1,0:T(8,128)(2,1)S(1)}, bf16[2,48,1024]{2,1,0:T(8,128)(2,1)S(1)}, u32[]{:S(2)}, u32[]{:S(2)}) collective-permute-start(bf16[2,48,1024]{2,1,0:T(8,128)(2,1)S(1)} %get-tuple-element.92), channel_id=1, source_target_pairs={{0,16},{8,24},{16,0},{24,8},{1,17},{9,25},{17,1},{25,9},{2,18},{10... | collective-permute-start | bytes 589832 | tf_op jit(solution)/shard_map/ppermute | solution.py:394
  166.9 7.4 %collective-permute-start.17 = (bf16[2,48,1024]{2,1,0:T(8,128)(2,1)S(1)}, bf16[2,48,1024]{2,1,0:T(8,128)(2,1)S(1)}, u32[]{:S(2)}, u32[]{:S(2)}) collective-permute-start(bf16[2,48,1024]{2,1,0:T(8,128)(2,1)S(1)} %get-tuple-element.93), channel_id=1, source_target_pairs={{0,32},{32,64},{64,96},{96,0},{1,33},{33,65},{65,97},{97,1},{2,34}... | collective-permute-start | bytes 589832 | tf_op jit(solution)/shard_map/ppermute | solution.py:394
  168.3 6.0 %collective-permute-start.19 = (bf16[2,48,1024]{2,1,0:T(8,128)(2,1)S(1)}, bf16[2,48,1024]{2,1,0:T(8,128)(2,1)S(1)}, u32[]{:S(2)}, u32[]{:S(2)}) collective-permute-start(bf16[2,48,1024]{2,1,0:T(8,128)(2,1)S(1)} %get-tuple-element.94), channel_id=1, source_target_pairs={{0,96},{32,0},{64,32},{96,64},{1,97},{33,1},{65,33},{97,65},{2,98}... | collective-permute-start | bytes 589832 | tf_op jit(solution)/shard_map/ppermute | solution.py:394
  170.1 9.3 %collective-permute-start.18 = (bf16[2,48,1024]{2,1,0:T(8,128)(2,1)S(1)}, bf16[2,48,1024]{2,1,0:T(8,128)(2,1)S(1)}, u32[]{:S(2)}, u32[]{:S(2)}) collective-permute-start(bf16[2,48,1024]{2,1,0:T(8,128)(2,1)S(1)} %get-tuple-element.95), channel_id=1, source_target_pairs={{0,64},{32,96},{64,0},{96,32},{1,65},{33,97},{65,1},{97,33},{2,66}... | collective-permute-start | bytes 589832 | tf_op jit(solution)/shard_map/ppermute | solution.py:394
  171.6 30.2 %copy-start.3 = (f32[2,128]{1,0:T(2,128)S(1)}, f32[2,128]{1,0:T(2,128)}, u32[]{:S(2)}) copy-start(f32[2,128]{1,0:T(2,128)} %find_roots.3) | copy-start | bytes 3076
  171.6 30.2 %copy-start.4 = (f32[1,128]{1,0:T(1,128)S(1)}, f32[1,128]{1,0:T(1,128)}, u32[]{:S(2)}) copy-start(f32[1,128]{1,0:T(1,128)} %find_roots.4) | copy-start | bytes 1540
  181.5 32.1 %collective-permute-start.20 = (f32[2,48,1024]{2,0,1:T(2,128)S(1)}, f32[2,48,1024]{2,0,1:T(2,128)S(1)}, u32[]{:S(2)}, u32[]{:S(2)}) collective-permute-start(f32[2,48,1024]{2,0,1:T(2,128)S(1)} %get-tuple-element.89), channel_id=1, source_target_pairs={{0,1},{1,0},{2,3},{3,2},{4,5},{5,4},{6,7},{7,6},{8,9},{9,8},{10,11... | collective-permute-start | bytes 1179656 | tf_op jit(solution)/shard_map/ppermute | solution.py:398
  203.0 10.6 %all-to-all-start.3 = ((f32[16,4,128]{2,1,0:T(4,128)}), f32[16,4,128]{2,1,0:T(4,128)S(1)}, u32[]{:S(2)}, u32[]{:S(2)}) async-start(f32[16,4,128]{2,1,0:T(4,128)} %broadcast_in_dim.49), calls=%async_computation.3 | async-start | bytes 65536 | tf_op jit(solution)/shard_map/all_to_all | solution.py:282
  (4 other events, 16.3 us)

commit v4 on v3

v4 whole, which is shorter than its diff:
```python
import jax
import jax.numpy as jnp
from jax import lax
from jax.experimental import pallas as pl
from jax.experimental.pallas import tpu as pltpu
from jax.sharding import Mesh
from jax.sharding import PartitionSpec as P

ITERS = 3
ROW = ("z", "x")
COL = ("y", "core")
ALL = ("z", "x", "y", "core")
F32 = jnp.float32
BF16 = jnp.bfloat16
LANES = 128
GROUP = 128
BLOCK = 16
CUT_A = 2
CUT_B = 3


def cost(flops):
    return pl.CostEstimate(flops=int(flops), bytes_accessed=1 << 20, transcendentals=0)


def column(row):
    return jnp.broadcast_to(row, (LANES, LANES)).T


def root_kernel(rank_ref, pw_ref, root_ref, out_ref, w2_ref, ps_ref, c_ref, t_ref, lo_ref, hi_ref):
    w2_ref[...] = pw_ref[1] * pw_ref[1]
    groups = root_ref.shape[1]
    blocks = ps_ref.shape[0] // BLOCK
    for k in range(groups):
        here = pl.ds(k * GROUP, GROUP)
        c_ref[here, :] = column(root_ref[0, k : k + 1, :])
        t_ref[here, :] = column(root_ref[1, k : k + 1, :])
        lo_ref[here, :] = column(root_ref[2, k : k + 1, :])
        hi_ref[here, :] = column(root_ref[3, k : k + 1, :])

    def group_body(g, carry):
        here = pl.ds(g * GROUP, GROUP)
        base = c_ref[pl.ds(g * GROUP + GROUP // 2, 1), :]
        ps_ref[...] = pw_ref[0] - base
        offset = c_ref[here, :] - base
        near_block = jnp.clip((rank_ref[0] // LANES + g - BLOCK // 2) // BLOCK, 0, blocks - 2)

        def step(_, carry):
            t = t_ref[here, :]
            s = offset + t

            def near(r, sums):
                first, second = sums
                for u in range(BLOCK):
                    row = pl.ds((near_block + r) * BLOCK + u, 1)
                    inverse = 1.0 / (ps_ref[row, :] - s)
                    weighted = w2_ref[row, :] * inverse
                    first = first + weighted
                    second = second + weighted * inverse
                return first, second

            def far(i, sums):
                first, second = sums
                for half in range(2):
                    block = 2 * i + half
                    block = jnp.where(block >= near_block, block + 2, block)
                    some = None
                    for u in range(BLOCK):
                        row = pl.ds(block * BLOCK + u, 1)
                        distance = (ps_ref[row, :] - s).astype(BF16)
                        weight = jnp.broadcast_to(w2_ref[row, :], (GROUP, LANES)).astype(BF16)
                        weighted = weight / distance
                        square = weighted / distance
                        some = (weighted, square) if some is None else (some[0] + weighted, some[1] + square)
                    first = first + some[0].astype(F32)
                    second = second + some[1].astype(F32)
                return first, second

            zero = jnp.zeros((GROUP, LANES), F32)
            sums = lax.fori_loop(0, 2, near, (zero, zero))
            first, second = lax.fori_loop(0, (blocks - 2) // 2, far, sums)
            sum_inverse = jnp.sum(first, axis=1, keepdims=True)
            sum_square = jnp.sum(second, axis=1, keepdims=True)
            nearest = jnp.minimum(jnp.abs(lo_ref[here, :] - t), jnp.abs(hi_ref[here, :] - t))
            limit = 0.5 * nearest
            t_ref[here, :] = t - jnp.clip((1.0 + sum_inverse) / sum_square, -limit, limit)
            return carry

        lax.fori_loop(0, ITERS, step, 0)
        return carry

    lax.fori_loop(0, groups, group_body, 0)
    for k in range(groups):
        out_ref[k : k + 1, :] = t_ref[pl.ds(k * GROUP, GROUP), :].T[0:1, :]


def find_roots(rank, pw, root):
    groups = root.shape[1]
    n_pole_rows = pw.shape[1]
    roots = groups * GROUP
    vmem = pl.BlockSpec(memory_space=pltpu.VMEM)
    return pl.pallas_call(
        root_kernel,
        in_specs=[pl.BlockSpec(memory_space=pltpu.SMEM), vmem, vmem],
        out_shape=jax.ShapeDtypeStruct((groups, LANES), F32),
        scratch_shapes=[pltpu.VMEM((n_pole_rows, LANES), F32)] * 2
        + [pltpu.VMEM((roots, LANES), F32)] * 4,
        cost_estimate=cost(ITERS * roots * n_pole_rows * LANES * 10),
        name="find_roots",
    )(rank, pw, root)


def panel_kernel(pw_ref, root_ref, out_ref, w2_ref):
    w2_ref[...] = pw_ref[1] * pw_ref[1]
    count = 16
    c = column(root_ref[0:1, :])[:count]
    t = column(root_ref[1:2, :])[:count]
    unroll = 32
    zero = jnp.zeros((count, LANES), F32)

    def sums_at(t):
        def body(r, sums):
            first, second, nearest = sums
            for u in range(unroll):
                row = pl.ds(r * unroll + u, 1)
                distance = (pw_ref[0, row, :] - c) - t
                inverse = 1.0 / distance
                weighted = w2_ref[row, :] * inverse
                first = first + weighted
                second = second + weighted * inverse
                nearest = jnp.minimum(nearest, jnp.abs(distance))
            return first, second, nearest

        first, second, nearest = lax.fori_loop(
            0, w2_ref.shape[0] // unroll, body, (zero, zero, jnp.full((count, LANES), 3e38, F32))
        )
        return (
            jnp.sum(first, axis=1, keepdims=True),
            jnp.sum(second, axis=1, keepdims=True),
            jnp.min(nearest, axis=1, keepdims=True),
        )

    for _ in range(ITERS):
        sum_inverse, sum_square, nearest = sums_at(t)
        limit = 0.5 * nearest
        t = t - jnp.clip((1.0 + sum_inverse) / sum_square, -limit, limit)
    norm = lax.rsqrt(sums_at(t)[1])
    pad = jnp.zeros((LANES - count, LANES), F32)
    out_ref[0:1, :] = jnp.concatenate([t, pad], axis=0).T[0:1, :]
    out_ref[1:2, :] = jnp.concatenate([jnp.broadcast_to(norm, (count, LANES)), pad], axis=0).T[0:1, :]


def panel_roots(pw, root):
    n_pole_rows = pw.shape[1]
    return pl.pallas_call(
        panel_kernel,
        out_shape=jax.ShapeDtypeStruct((2, LANES), F32),
        scratch_shapes=[pltpu.VMEM((n_pole_rows, LANES), F32)],
        cost_estimate=cost(4 * 20 * n_pole_rows * LANES * 10),
        name="panel_roots",
    )(pw, root)


def pick_kernel(index_ref, pw_ref, out_ref):
    index = jnp.concatenate([index_ref[...], index_ref[...]], axis=0)
    row = index // LANES
    lane = index % LANES
    unroll = 16

    def body(r, carry):
        p, w = carry
        for u in range(unroll):
            at = r * unroll + u
            hit = row == at
            p_row = jnp.broadcast_to(pw_ref[0, pl.ds(at, 1), :], (8, LANES))
            w_row = jnp.broadcast_to(pw_ref[1, pl.ds(at, 1), :], (8, LANES))
            p = jnp.where(hit, jnp.take_along_axis(p_row, lane, axis=1), p)
            w = jnp.where(hit, jnp.take_along_axis(w_row, lane, axis=1), w)
        return p, w

    zero = jnp.zeros((8, LANES), F32)
    p, w = lax.fori_loop(0, pw_ref.shape[1] // unroll, body, (zero, zero))
    out_ref[0] = p[:4]
    out_ref[1] = w[:4]


def pick_columns(index, pw):
    return pl.pallas_call(
        pick_kernel,
        out_shape=jax.ShapeDtypeStruct((2, 4, LANES), F32),
        cost_estimate=cost(5e7),
        name="pick_columns",
    )(index, pw)


def matmul_kernel(place_ref, col_ref, root_ref, *refs):
    blocks = refs[:16]
    outs = refs[16:24]
    p_ref, w_ref, e_ref, acc_ref, sems = refs[24:]
    sources = 4
    halves, _, both, depth = e_ref.shape
    rows = both // 2
    quarter = rows // 4
    n_roots = root_ref.shape[1]
    pieces = depth // LANES

    def moves(half, src):
        return [
            pltpu.make_async_copy(
                blocks[half * 8 + side * 4 + src],
                e_ref.at[half, src, pl.ds(side * rows, rows)],
                sems.at[half, src, side],
            )
            for side in range(2)
        ]

    for half in range(halves):
        for src in range(sources):
            for move in moves(half, src):
                move.start()

    def half_body(half, carry):
        for src in range(sources):
            p = jnp.concatenate([col_ref[half, 0, src]] * (LANES // pieces), axis=0).T
            w = jnp.concatenate([col_ref[half, 1, src]] * (LANES // pieces), axis=0).T
            for piece in range(pieces):
                here = pl.ds(src * depth + piece * LANES, LANES)
                p_ref[here, :] = jnp.broadcast_to(p[:, piece : piece + 1], (LANES, LANES))
                w_ref[here, :] = jnp.broadcast_to(w[:, piece : piece + 1], (LANES, LANES))
        for which in range(halves):

            @pl.when(half == which)
            def _():
                for src in range(sources):
                    for move in moves(which, src):
                        move.wait()

        def cauchy(src):
            down = []
            for piece in range(pieces):
                here = pl.ds(src * depth + piece * LANES, LANES)
                p = p_ref[here, :]
                w = w_ref[here, :]
                across = []
                for part in range(n_roots // LANES):
                    lanes = pl.ds(part * LANES, LANES)
                    distance = (p - root_ref[0:1, lanes]) - root_ref[1:2, lanes]
                    value = w * (1.0 / distance) * root_ref[2:3, lanes]
                    across.append(value.astype(BF16))
                down.append(jnp.concatenate(across, axis=1))
            return jnp.concatenate(down, axis=0)

        acc = None
        for src in range(sources):
            product = jnp.dot(e_ref[half, src], cauchy(src), preferred_element_type=F32)
            acc = product if acc is None else acc + product
        acc_ref[...] = acc
        for which in range(halves):

            @pl.when(half == which)
            def _():
                for shift in range(4):
                    part = (place_ref[which] + shift) % 4
                    for side in range(2):
                        piece = acc_ref[pl.ds(side * rows + part * quarter, quarter), :]
                        out = outs[which * 4 + shift]
                        out[side] = piece.astype(out.dtype)

        return carry

    lax.fori_loop(0, halves, half_body, 0)


def panel_product(places, columns, root, blocks):
    rows, depth = blocks[0].shape
    n_roots = root.shape[1]
    shape = (2, rows // 4, n_roots)
    types = [F32, BF16, BF16, BF16] * 2
    vmem = pl.BlockSpec(memory_space=pltpu.VMEM)
    return pl.pallas_call(
        matmul_kernel,
        in_specs=[pl.BlockSpec(memory_space=pltpu.SMEM), vmem, vmem] + [pl.BlockSpec(memory_space=pl.ANY)] * 16,
        out_shape=[jax.ShapeDtypeStruct(shape, t) for t in types],
        scratch_shapes=[pltpu.VMEM((4 * depth, LANES), F32)] * 2
        + [
            pltpu.VMEM((2, 4, 2 * rows, depth), BF16),
            pltpu.VMEM((2 * rows, n_roots), F32),
            pltpu.SemaphoreType.DMA((2, 4, 2)),
        ],
        cost_estimate=cost(2 * 16 * rows * depth * n_roots),
        compiler_params=pltpu.CompilerParams(vmem_limit_bytes=56 << 20),
        name="panel_product",
    )(places, columns, root, *blocks)


def copies(value, axis):
    size = lax.axis_size(axis)
    return lax.all_to_all(
        jnp.broadcast_to(value[None], (size, *value.shape)), axis, 0, 0, tiled=True
    )


def ring(shift):
    return [(i, (i + shift) % 4) for i in range(4)]


def merge(pole_values, weights, centers, offsets, chosen, column_pole, eigen_blocks):
    z = lax.axis_index("z")
    x = lax.axis_index("x")
    core = lax.axis_index("core")
    row = z * 4 + x
    col = lax.axis_index("y") * 2 + core
    n_col = centers.shape[0]
    n_own = n_col // 16
    swap = [(0, 1), (1, 0)]

    wanted = lax.dynamic_slice_in_dim(chosen, row * LANES, LANES)
    local = wanted - col * n_col
    hit = local[:, None] == lax.broadcasted_iota(jnp.int32, (1, n_col), 1)
    first = jnp.stack(
        [
            jnp.sum(jnp.where(hit, centers[None, :], 0.0), axis=1),
            jnp.sum(jnp.where(hit, offsets[None, :], 0.0), axis=1),
        ]
    )
    spread = jnp.moveaxis(first.reshape(2, 8, 16), 1, 0).reshape(8, 1, 32)
    spread = jnp.tile(jnp.pad(spread, ((0, 0), (0, 0), (0, LANES - 32))), (16, 1, 1))
    part = jnp.concatenate(
        [
            lax.dynamic_slice_in_dim(v.reshape(-1, LANES), col * 4, 4)
            for v in (pole_values, weights)
        ]
    )
    out = jnp.concatenate([jnp.broadcast_to(part[None], (128, 8, LANES)), spread], axis=1)
    arrived = lax.all_to_all(out, ALL, 0, 0, tiled=True)

    axes = ("z", "x")
    places = (z, x)
    wide = eigen_blocks.reshape(4, 4, -1, 2, eigen_blocks.shape[2])
    turned = (
        wide[:, :, :, 0].reshape(4, -1, eigen_blocks.shape[2]),
        jnp.swapaxes(wide[:, :, :, 1], 0, 1).reshape(4, -1, eigen_blocks.shape[2]),
    )
    cut = [
        [
            lax.dynamic_index_in_dim(turned[half], (places[half] + shift) % 4, 0, keepdims=False)
            for shift in range(4)
        ]
        for half in range(2)
    ]

    cut, arrived = lax.optimization_barrier((cut, arrived))
    eigen = [[cut[0][0]], [cut[1][0]]]
    for shift in (1, 2, 3):
        for half in range(2):
            eigen[half].append(lax.ppermute(cut[half][shift], axes[half], ring(shift)))
    peer = [[lax.ppermute(eigen[half][0], "core", swap)] for half in range(2)]

    pw = jnp.moveaxis(arrived[:, :8].reshape(128, 2, 4, LANES), 1, 0).reshape(2, -1, LANES)
    begun = lax.dynamic_slice(arrived, (row * 8, 8, 0), (8, 1, 32))
    panel_start = jnp.pad(
        jnp.sum(begun, axis=(0, 1)).reshape(2, 16),
        ((0, 0), (0, LANES - 16)),
        constant_values=0.25,
    )
    panel_end = panel_roots(pw, panel_start)
    index = lax.dynamic_slice_in_dim(column_pole.reshape(-1, LANES), col * 4, 4)
    picked = pick_columns(index, pw)
    note = jnp.concatenate([picked.reshape(8, LANES), panel_start[:1], panel_end], axis=0)
    notes = copies(note, ALL)

    start = col * n_col + row * n_own
    my_centers = lax.dynamic_slice_in_dim(centers.reshape(-1, LANES), row * 4, 4)
    my_offsets = lax.dynamic_slice_in_dim(offsets.reshape(-1, LANES), row * 4, 4)
    own_poles = lax.dynamic_slice_in_dim(pw[0], start // LANES, 4)
    low = own_poles - my_centers
    ranks = start + jnp.arange(n_own).reshape(-1, LANES)
    high = jnp.where(ranks == pw[0].size - 1, 3e38, -low)
    state = jnp.stack([my_centers, my_offsets, low, high])
    rank = start.reshape(1)
    roots_a = find_roots(rank, pw, state[:, :CUT_A])
    eigen, notes, roots_a = lax.optimization_barrier((eigen, notes, roots_a))

    for half in range(2):
        peer[half] += [lax.ppermute(block, "core", swap) for block in eigen[half][1:]]
    roots_b = find_roots(rank + CUT_A * GROUP, pw, state[:, CUT_A:CUT_B])

    table = notes[:, :8].reshape(4, 4, 2, 4, 2, 4, LANES)
    columns = (
        lax.dynamic_index_in_dim(table[:, :, 0], x, 1, keepdims=False),
        lax.dynamic_index_in_dim(table[:, :, 1], z, 0, keepdims=False),
    )
    columns = [
        jnp.moveaxis(
            jnp.concatenate(
                [lax.dynamic_slice_in_dim(c, (place - s) % 4, 1) for s in range(4)]
            ),
            2,
            0,
        ).reshape(2, 4, -1, LANES)
        for c, place in zip(columns, places)
    ]
    panel_root = jnp.moveaxis(notes[:, 8:, :16], 1, 0).reshape(3, 2, -1)
    panel_root = lax.dynamic_index_in_dim(panel_root, core, 1, keepdims=False)
    panel_root, columns, peer, roots_b = lax.optimization_barrier(
        (panel_root, columns, peer, roots_b)
    )
    sums = panel_product(
        jnp.stack([x, z]).astype(jnp.int32),
        jnp.stack(columns),
        panel_root,
        eigen[0] + peer[0] + eigen[1] + peer[1],
    )
    pieces = []
    for half in range(2):
        mine = sums[4 * half : 4 * half + 4]
        pieces.append(
            [mine[0]]
            + [lax.ppermute(mine[s], axes[1 - half], ring(s)) for s in (1, 2, 3)]
        )
    roots_c = find_roots(rank + CUT_B * GROUP, pw, state[:, CUT_B:])

    def added(side):
        return jnp.stack([p[0][side] + p[1][side] + p[2][side] + p[3][side] for p in pieces])

    roots = copies(jnp.concatenate([roots_a, roots_b, roots_c]), ROW)
    got = lax.ppermute(added(1), "core", swap)
    keep = added(0)
    panel = jnp.where(
        core == 0, jnp.concatenate([keep, got], axis=2), jnp.concatenate([got, keep], axis=2)
    )
    return roots.reshape(-1), jnp.moveaxis(panel, 0, 1)


def solution(mesh):
    torus = Mesh(mesh.devices.reshape(4, 4, 4, 2), ALL)
    placed = (P(ROW), P(ROW), P(COL), P(COL), P(), P(None, ROW), P(COL, None, ROW))
    return jax.shard_map(
        merge,
        mesh=torus,
        in_specs=placed,
        out_specs=(P(COL), P(COL + ROW, None, None)),
        check_vma=False,
    )
```

time: 217 us -> 223 us (1.028)
  starting transfers between devices: 47.5 us -> 58.3 us
  Pallas kernels: 115 us -> 105 us
  waiting for transfers between devices: 16.7 us -> 20.4 us
    pallas_call x2 -> x1, Pallas kernels: 29.5 us -> 21.6 us  [panel_product(): pl.pallas_call(matmul_kernel, in_specs=[pl.BlockSpec(memory_space=pltpu.S...]
    all_to_all x1, starting transfers between devices: 5.43 us -> 11.9 us  [merge(): arrived = lax.all_to_all(out, ALL, 0, 0, tiled=True)]
    all_to_all x3 -> x2, starting transfers between devices: 18.8 us -> 24.2 us  [copies(): lax.all_to_all(jnp.broadcast_to(value[None], (size, *value.shape)), axis,...]
    all_to_all x1, waiting for transfers between devices: 0.01 us -> 3.38 us  [merge(): arrived = lax.all_to_all(out, ALL, 0, 0, tiled=True)]
    ppermute x6, starting transfers between devices: 9.87 us -> 6.88 us  [merge(): eigen[half].append(lax.ppermute(cut[half][shift], axes[half], ring(shift)))]
    squeeze x2 -> x0, local copies, waits for them, and re-layouts: 2.34 us -> none  [merge(): lax.dynamic_index_in_dim(send, (other + shift) % 4, 0, keepdims=False)]
    unnamed x25 -> x24, local copies, waits for them, and re-layouts: 6.96 us -> 8.61 us
    all_to_all x3 -> x2, waiting for transfers between devices: 6.45 us -> 6.45 us  [copies(): lax.all_to_all(jnp.broadcast_to(value[None], (size, *value.shape)), axis,...]
  transfers between devices with their start and end apart: 25 -> 24, of which waited for: 7 -> 10; matrix products, arithmetic and copies ran while one was open for 13% -> 13% of each run, Pallas kernels for 46% -> 38%
where the time goes in v4:
time: 223 us; the launch traced here: 222 us
  Pallas kernels  105 us (47%)
  starting transfers between devices  58.3 us (26%)
  local copies, waits for them, and re-layouts  26.3 us (12%)
  waiting for transfers between devices  20.4 us (9%)
  other arithmetic  11.3 us (5%)
    pallas_call x3, Pallas kernels, find_roots(): pl.pallas_call(root_kernel, in_specs=[pl.BlockSpec(memory_space=pltpu.SME...  71.6 us
    all_to_all x2, starting transfers between devices, copies(): lax.all_to_all(jnp.broadcast_to(value[None], (size, *value.shape)), axis,...  24.2 us
    pallas_call x1, Pallas kernels, panel_product(): pl.pallas_call(matmul_kernel, in_specs=[pl.BlockSpec(memory_space=pltpu.S...  21.6 us
    all_to_all x1, starting transfers between devices, merge(): arrived = lax.all_to_all(out, ALL, 0, 0, tiled=True)  11.9 us
    ppermute x6, starting transfers between devices, merge(): lax.ppermute(mine[s], axes[1 - half], ring(s))  10.1 us
    unnamed x24, local copies, waits for them, and re-layouts  8.61 us
    pallas_call x1, Pallas kernels, panel_roots(): pl.pallas_call(panel_kernel, out_shape=jax.ShapeDtypeStruct((2, LANES), F...  7.05 us
    ppermute x6, starting transfers between devices, merge(): eigen[half].append(lax.ppermute(cut[half][shift], axes[half], ring(shift)))  6.88 us
  transfers between devices with their start and end apart: 24, of which 10 were waited for; matrix products, arithmetic and copies ran while one was open for 13% of the time, Pallas kernels for 38%

profile of v4, /device:TPU:1, one launch (start us, length us, event | category | flops | bytes accessed | tf_op | source)
XLA Modules:
  0.0 222.3 jit_solution(5887301386309791236)
XLA Ops:
  1.4 2.1 select_reduce_fusion.1
  4.6 1.1 pad_maximum_fusion
  5.8 11.9 %all-to-all-start = ((f32[128,9,128]{2,1,0:T(8,128)}), f32[128,9,128]{2,1,0:T(8,128)}, u32[]{:S(2)}, u32[]{:S(2)}) async-start(f32[128,9,128]{2,1,0:T(8,128)} %pad_maximum_fusion), calls=%async_computation | async-start | bytes 2097152 | tf_op jit(solution)/shard_map/all_to_all | solution.py:335
  17.7 5.7 %copy.36 = bf16[768,2,2048]{2,0,1:T(8,128)(2,1)S(1)} copy(bf16[768,2,2048]{2,1,0:T(2,128)(2,1)} %param.13) | data formatting | bytes 12582912 | tf_op args[6]
  23.4 2.2 slice_bitcast_fusion
  25.6 1.9 copy.37
  27.5 5.2 %dynamic-slice_bitcast_fusion = (bf16[192,2048]{1,0:T(8,128)(2,1)}, bf16[192,2048]{1,0:T(8,128)(2,1)}, bf16[192,2048]{1,0:T(8,128)(2,1)}, bf16[192,2048]{1,0:T(8...) fusion(bf16[4,192,2048]{2,1,0:T(8,128)(2,1)} %bitcast.83, ...), kind=kLoop, calls=%fused_computation.7 | loop fusion | bytes 12582944 | tf_op jit(solution)/shard_map/jit(dynamic_index_in_dim)/squeeze | solution.py:346
  32.8 3.4 %all-to-all-done = f32[128,9,128]{2,1,0:T(8,128)} async-done(((f32[128,9,128]{2,1,0:T(8,128)}), f32[128,9,128]{2,1,0:T(8,128)}, u32[]{:S(2)}, u32[]{:S(2)}) %all-to-all-start) | async-done | bytes 589856 | tf_op jit(solution)/shard_map/all_to_all | solution.py:335
  37.3 1.4 copy.39
  40.8 1.2 collective-permute-start.1
  42.0 1.5 collective-permute-start.2
  43.6 2.2 %collective-permute-start.4 = (bf16[192,2048]{1,0:T(8,128)(2,1)}, bf16[192,2048]{1,0:T(8,128)(2,1)}, u32[]{:S(2)}, u32[]{:S(2)}) collective-permute-start(bf16[192,2048]{1,0:T(8,128)(2,1)} %get-tuple-element.47), channel_id=1, source_target_pairs={{0,16},{8,24},{16,0},{24,8},{1,17},{9,25},{17,1},{25,9},{2,18},{10... | collective-permute-start | bytes 2359304 | tf_op jit(solution)/shard_map/ppermute | solution.py:356
  46.4 5.0 %pick_columns.1 = f32[2,4,128]{2,1,0:T(4,128)} custom-call(s32[4,128]{1,0:T(4,128)} %constant_dynamic-slice_fusion.5.index_ref, f32[2,512,128]{2,1,0:T(8,128)} %bitcast.85), custom_call_target="tpu_custom_call" | custom-call | flops 50000000 | bytes 1048576 | tf_op jit(solution)/shard_map/pick_columns/pallas_call | solution.py:188
  51.4 7.0 %panel_roots.1 = f32[2,128]{1,0:T(2,128)} custom-call(f32[2,512,128]{2,1,0:T(8,128)} %bitcast.86, f32[2,128]{1,0:T(2,128)} %pad.9.root_ref), custom_call_target="tpu_custom_call" | custom-call | flops 52428800 | bytes 1048576 | tf_op jit(solution)/shard_map/panel_roots/pallas_call | solution.py:155
  58.4 1.2 collective-permute-start.5
  61.4 20.2 %all-to-all-start.1 = ((f32[128,11,128]{2,1,0:T(8,128)}), f32[128,11,128]{2,1,0:T(8,128)S(1)}, u32[]{:S(2)}, u32[]{:S(2)}) async-start(f32[128,11,128]{2,1,0:T(8,128)} %broadcast_in_dim.47), calls=%async_computation.1 | async-start | bytes 2097152 | tf_op jit(solution)/shard_map/all_to_all | solution.py:298
  83.9 35.0 %find_roots.3 = f32[2,128]{1,0:T(2,128)} custom-call(s32[1]{0:T(128)} %bitcast.22.rank_ref, f32[2,512,128]{2,1,0:T(8,128)} %bitcast.87, f32[4,2,128]{2,1,0:T(2,128)} %slice.117.root_ref), custom_call_target="tpu_custom_call" | custom-call | flops 503316480 | bytes 1048576 | tf_op jit(solution)/shard_map/find_roots/pallas_call | solution.py:102
  118.9 1.2 collective-permute-start.6
  122.0 18.3 %find_roots.4 = f32[1,128]{1,0:T(1,128)} custom-call(s32[1]{0:T(128)S(6)} %add.322.rank_ref, f32[2,512,128]{2,1,0:T(8,128)} %bitcast.88, f32[4,1,128]{2,1,0:T(1,128)} %get-tuple-element.119.root_ref), custom_call_target="tpu_custom_call" | custom-call | flops 251658240 | bytes 1048576 | tf_op jit(solution)/shard_map/find_roots/pallas_call | solution.py:102
  148.5 21.6 %panel_product.1 = (f32[2,48,1024]{2,1,0:T(8,128)}, bf16[2,48,1024]{2,1,0:T(8,128)(2,1)}, bf16[2,48,1024]{2,1,0:T(8,128)(2,1)}, bf16[2,48,1024]{2,1,0:T(8,128)(2...) custom-call(s32[2]{0:T(128)} %pad_add_fusion.place_ref, ...), custom_call_target="tpu_custom_call" | custom-call | flops 12884901888 | bytes 1048576 | tf_op jit(solution)/shard_map/panel_product/pallas_call | solution.py:280
  170.7 2.4 %collective-permute-start.15 = (bf16[2,48,1024]{2,1,0:T(8,128)(2,1)}, bf16[2,48,1024]{2,1,0:T(8,128)(2,1)S(1)}, u32[]{:S(2)}, u32[]{:S(2)}) collective-permute-start(bf16[2,48,1024]{2,1,0:T(8,128)(2,1)} %get-tuple-element.74), channel_id=1, source_target_pairs={{0,16},{8,24},{16,0},{24,8},{1,17},{9,25},{17,1},{25,9},{2,18},{10... | collective-permute-start | bytes 589832 | tf_op jit(solution)/shard_map/ppermute | solution.py:419
  173.1 1.2 collective-permute-start.16
  174.3 1.3 collective-permute-start.17
  175.6 2.9 %collective-permute-start.18 = (bf16[2,48,1024]{2,1,0:T(8,128)(2,1)}, bf16[2,48,1024]{2,1,0:T(8,128)(2,1)S(1)}, u32[]{:S(2)}, u32[]{:S(2)}) collective-permute-start(bf16[2,48,1024]{2,1,0:T(8,128)(2,1)} %get-tuple-element.78), channel_id=1, source_target_pairs={{0,64},{32,96},{64,0},{96,32},{1,65},{33,97},{65,1},{97,33},{2,66}... | collective-permute-start | bytes 589832 | tf_op jit(solution)/shard_map/ppermute | solution.py:419
  178.6 1.7 collective-permute-start.19
  180.3 2.1 collective-permute-done.15
  183.6 3.4 %collective-permute-done.18 = bf16[2,48,1024]{2,1,0:T(8,128)(2,1)S(1)} collective-permute-done((bf16[2,48,1024]{2,1,0:T(8,128)(2,1)}, bf16[2,48,1024]{2,1,0:T(8,128)(2,1)S(1)}, u32[]{:S(2)}, u32[]{:S(2)}) %collective-permute-start.18) | collective-permute-done | bytes 196640 | tf_op jit(solution)/shard_map/ppermute | solution.py:419
  188.1 1.9 collective-permute-start.20
  190.1 18.3 %find_roots.5 = f32[1,128]{1,0:T(1,128)} custom-call(s32[1]{0:T(128)S(6)} %add.323.rank_ref, f32[2,512,128]{2,1,0:T(8,128)} %bitcast.89, f32[4,1,128]{2,1,0:T(1,128)} %get-tuple-element.120.root_ref), custom_call_target="tpu_custom_call" | custom-call | flops 251658240 | bytes 1048576 | tf_op jit(solution)/shard_map/find_roots/pallas_call | solution.py:102
  209.7 4.0 %all-to-all-start.2 = ((f32[16,4,128]{2,1,0:T(4,128)}), f32[16,4,128]{2,1,0:T(4,128)S(1)}, u32[]{:S(2)}, u32[]{:S(2)}) async-start(f32[16,4,128]{2,1,0:T(4,128)} %broadcast_in_dim.49), calls=%async_computation.2 | async-start | bytes 65536 | tf_op jit(solution)/shard_map/all_to_all | solution.py:298
  213.7 6.4 %all-to-all-done.2 = f32[16,4,128]{2,1,0:T(4,128)S(1)} async-done(((f32[16,4,128]{2,1,0:T(4,128)}), f32[16,4,128]{2,1,0:T(4,128)S(1)}, u32[]{:S(2)}, u32[]{:S(2)}) %all-to-all-start.2) | async-done | bytes 32800 | tf_op jit(solution)/shard_map/all_to_all | solution.py:298
  220.2 1.5 copy.45
  (100 shorter events, 24.5 us)
Async XLA Ops:
  5.8 30.4 %all-to-all-start = ((f32[128,9,128]{2,1,0:T(8,128)}), f32[128,9,128]{2,1,0:T(8,128)}, u32[]{:S(2)}, u32[]{:S(2)}) async-start(f32[128,9,128]{2,1,0:T(8,128)} %pad_maximum_fusion), calls=%async_computation | async-start | bytes 2097152 | tf_op jit(solution)/shard_map/all_to_all | solution.py:335
  27.5 9.2 %copy-start.2 = (s32[2,2048]{1,0:T(2,128)S(1)}, s32[2,2048]{1,0:T(2,128)}, u32[]{:S(2)}) copy-start(s32[2,2048]{1,0:T(2,128)} %param.12) | copy-start | bytes 49156
  32.7 86.1 %copy-start.1 = (bf16[192,2048]{1,0:T(8,128)(2,1)}, bf16[192,2048]{1,0:T(8,128)(2,1)S(1)}, u32[]{:S(2)}) copy-start(bf16[192,2048]{1,0:T(8,128)(2,1)S(1)} %get-tuple-element.62.refs_0_) | copy-start | bytes 2359300
  32.8 87.4 %copy-start = (bf16[192,2048]{1,0:T(8,128)(2,1)}, bf16[192,2048]{1,0:T(8,128)(2,1)S(1)}, u32[]{:S(2)}) copy-start(bf16[192,2048]{1,0:T(8,128)(2,1)S(1)} %get-tuple-element.67.refs_8_) | copy-start | bytes 2359300
  36.1 22.3 %collective-permute-start = (bf16[192,2048]{1,0:T(8,128)(2,1)}, bf16[192,2048]{1,0:T(8,128)(2,1)}, u32[]{:S(2)}, u32[]{:S(2)}) collective-permute-start(bf16[192,2048]{1,0:T(8,128)(2,1)} %get-tuple-element.42), channel_id=1, source_target_pairs={{0,32},{32,64},{64,96},{96,0},{1,33},{33,65},{65,97},{97,1},{2,34}... | collective-permute-start | bytes 2359304 | tf_op jit(solution)/shard_map/ppermute | solution.py:356
  40.8 78.1 %collective-permute-start.1 = (bf16[192,2048]{1,0:T(8,128)(2,1)}, bf16[192,2048]{1,0:T(8,128)(2,1)}, u32[]{:S(2)}, u32[]{:S(2)}) collective-permute-start(bf16[192,2048]{1,0:T(8,128)(2,1)} %get-tuple-element.43), channel_id=1, source_target_pairs={{0,64},{32,96},{64,0},{96,32},{1,65},{33,97},{65,1},{97,33},{2,66}... | collective-permute-start | bytes 2359304 | tf_op jit(solution)/shard_map/ppermute | solution.py:356
  42.0 78.1 %collective-permute-start.2 = (bf16[192,2048]{1,0:T(8,128)(2,1)}, bf16[192,2048]{1,0:T(8,128)(2,1)}, u32[]{:S(2)}, u32[]{:S(2)}) collective-permute-start(bf16[192,2048]{1,0:T(8,128)(2,1)} %get-tuple-element.44), channel_id=1, source_target_pairs={{0,96},{32,0},{64,32},{96,64},{1,97},{33,1},{65,33},{97,65},{2,98}... | collective-permute-start | bytes 2359304 | tf_op jit(solution)/shard_map/ppermute | solution.py:356
  43.6 76.7 %collective-permute-start.3 = (bf16[192,2048]{1,0:T(8,128)(2,1)}, bf16[192,2048]{1,0:T(8,128)(2,1)}, u32[]{:S(2)}, u32[]{:S(2)}) collective-permute-start(bf16[192,2048]{1,0:T(8,128)(2,1)} %get-tuple-element.46), channel_id=1, source_target_pairs={{0,8},{8,16},{16,24},{24,0},{1,9},{9,17},{17,25},{25,1},{2,10},{10... | collective-permute-start | bytes 2359304 | tf_op jit(solution)/shard_map/ppermute | solution.py:356
  43.6 76.6 %collective-permute-start.4 = (bf16[192,2048]{1,0:T(8,128)(2,1)}, bf16[192,2048]{1,0:T(8,128)(2,1)}, u32[]{:S(2)}, u32[]{:S(2)}) collective-permute-start(bf16[192,2048]{1,0:T(8,128)(2,1)} %get-tuple-element.47), channel_id=1, source_target_pairs={{0,16},{8,24},{16,0},{24,8},{1,17},{9,25},{17,1},{25,9},{2,18},{10... | collective-permute-start | bytes 2359304 | tf_op jit(solution)/shard_map/ppermute | solution.py:356
  58.4 61.8 %collective-permute-start.5 = (bf16[192,2048]{1,0:T(8,128)(2,1)}, bf16[192,2048]{1,0:T(8,128)(2,1)}, u32[]{:S(2)}, u32[]{:S(2)}) collective-permute-start(bf16[192,2048]{1,0:T(8,128)(2,1)} %get-tuple-element.48), channel_id=1, source_target_pairs={{0,24},{8,0},{16,8},{24,16},{1,25},{9,1},{17,9},{25,17},{2,26},{10... | collective-permute-start | bytes 2359304 | tf_op jit(solution)/shard_map/ppermute | solution.py:356
  61.4 58.8 %all-to-all-start.1 = ((f32[128,11,128]{2,1,0:T(8,128)}), f32[128,11,128]{2,1,0:T(8,128)S(1)}, u32[]{:S(2)}, u32[]{:S(2)}) async-start(f32[128,11,128]{2,1,0:T(8,128)} %broadcast_in_dim.47), calls=%async_computation.1 | async-start | bytes 2097152 | tf_op jit(solution)/shard_map/all_to_all | solution.py:298
  118.9 22.2 %collective-permute-start.6 = (bf16[192,2048]{1,0:T(8,128)(2,1)S(1)}, bf16[192,2048]{1,0:T(8,128)(2,1)}, u32[]{:S(2)}, u32[]{:S(2)}) collective-permute-start(bf16[192,2048]{1,0:T(8,128)(2,1)S(1)} %get-tuple-element.62.refs_0_), channel_id=1, source_target_pairs={{0,1},{1,0},{2,3},{3,2},{4,5},{5,4},{6,7},{7,6},{8,9},{9,8},{10,11... | collective-permute-start | bytes 2359304 | tf_op jit(solution)/shard_map/ppermute | solution.py:357
  120.1 21.2 %collective-permute-start.10 = (bf16[192,2048]{1,0:T(8,128)(2,1)S(1)}, bf16[192,2048]{1,0:T(8,128)(2,1)}, u32[]{:S(2)}, u32[]{:S(2)}) collective-permute-start(bf16[192,2048]{1,0:T(8,128)(2,1)S(1)} %get-tuple-element.67.refs_8_), channel_id=1, source_target_pairs={{0,1},{1,0},{2,3},{3,2},{4,5},{5,4},{6,7},{7,6},{8,9},{9,8},{10,11... | collective-permute-start | bytes 2359304 | tf_op jit(solution)/shard_map/ppermute | solution.py:357
  120.3 21.4 %collective-permute-start.7 = (bf16[192,2048]{1,0:T(8,128)(2,1)}, bf16[192,2048]{1,0:T(8,128)(2,1)}, u32[]{:S(2)}, u32[]{:S(2)}) collective-permute-start(bf16[192,2048]{1,0:T(8,128)(2,1)} %collective-permute-done.refs_1_), channel_id=1, source_target_pairs={{0,1},{1,0},{2,3},{3,2},{4,5},{5,4},{6,7},{7,6},{8,9},{9,8},{10,11... | collective-permute-start | bytes 2359304 | tf_op jit(solution)/shard_map/ppermute | solution.py:385
  140.5 2.6 %collective-permute-start.8 = (bf16[192,2048]{1,0:T(8,128)(2,1)}, bf16[192,2048]{1,0:T(8,128)(2,1)S(1)}, u32[]{:S(2)}, u32[]{:S(2)}) collective-permute-start(bf16[192,2048]{1,0:T(8,128)(2,1)} %collective-permute-done.1.refs_2_), channel_id=1, source_target_pairs={{0,1},{1,0},{2,3},{3,2},{4,5},{5,4},{6,7},{7,6},{8,9},{9,8},{10,11... | collective-permute-start | bytes 2359304 | tf_op jit(solution)/shard_map/ppermute | solution.py:385
  140.8 3.4 %collective-permute-start.9 = (bf16[192,2048]{1,0:T(8,128)(2,1)}, bf16[192,2048]{1,0:T(8,128)(2,1)S(1)}, u32[]{:S(2)}, u32[]{:S(2)}) collective-permute-start(bf16[192,2048]{1,0:T(8,128)(2,1)} %collective-permute-done.2.refs_3_), channel_id=1, source_target_pairs={{0,1},{1,0},{2,3},{3,2},{4,5},{5,4},{6,7},{7,6},{8,9},{9,8},{10,11... | collective-permute-start | bytes 2359304 | tf_op jit(solution)/shard_map/ppermute | solution.py:385
  141.1 4.2 %collective-permute-start.11 = (bf16[192,2048]{1,0:T(8,128)(2,1)}, bf16[192,2048]{1,0:T(8,128)(2,1)S(1)}, u32[]{:S(2)}, u32[]{:S(2)}) collective-permute-start(bf16[192,2048]{1,0:T(8,128)(2,1)} %collective-permute-done.3.refs_9_), channel_id=1, source_target_pairs={{0,1},{1,0},{2,3},{3,2},{4,5},{5,4},{6,7},{7,6},{8,9},{9,8},{10,11... | collective-permute-start | bytes 2359304 | tf_op jit(solution)/shard_map/ppermute | solution.py:385
  141.3 5.2 %collective-permute-start.12 = (bf16[192,2048]{1,0:T(8,128)(2,1)}, bf16[192,2048]{1,0:T(8,128)(2,1)S(1)}, u32[]{:S(2)}, u32[]{:S(2)}) collective-permute-start(bf16[192,2048]{1,0:T(8,128)(2,1)} %collective-permute-done.4.refs_10_), channel_id=1, source_target_pairs={{0,1},{1,0},{2,3},{3,2},{4,5},{5,4},{6,7},{7,6},{8,9},{9,8},{10,11... | collective-permute-start | bytes 2359304 | tf_op jit(solution)/shard_map/ppermute | solution.py:385
  141.7 6.0 %collective-permute-start.13 = (bf16[192,2048]{1,0:T(8,128)(2,1)}, bf16[192,2048]{1,0:T(8,128)(2,1)S(1)}, u32[]{:S(2)}, u32[]{:S(2)}) collective-permute-start(bf16[192,2048]{1,0:T(8,128)(2,1)} %collective-permute-done.5.refs_11_), channel_id=1, source_target_pairs={{0,1},{1,0},{2,3},{3,2},{4,5},{5,4},{6,7},{7,6},{8,9},{9,8},{10,11... | collective-permute-start | bytes 2359304 | tf_op jit(solution)/shard_map/ppermute | solution.py:385
  143.1 5.2 %copy-start.5 = (bf16[192,2048]{1,0:T(8,128)(2,1)}, bf16[192,2048]{1,0:T(8,128)(2,1)S(1)}, u32[]{:S(2)}) copy-start(bf16[192,2048]{1,0:T(8,128)(2,1)S(1)} %collective-permute-done.8.refs_6_) | copy-start | bytes 2359300
  144.2 4.1 %copy-start.6 = (bf16[192,2048]{1,0:T(8,128)(2,1)}, bf16[192,2048]{1,0:T(8,128)(2,1)S(1)}, u32[]{:S(2)}) copy-start(bf16[192,2048]{1,0:T(8,128)(2,1)S(1)} %collective-permute-done.9.refs_7_) | copy-start | bytes 2359300
  145.4 3.0 %copy-start.7 = (bf16[192,2048]{1,0:T(8,128)(2,1)}, bf16[192,2048]{1,0:T(8,128)(2,1)S(1)}, u32[]{:S(2)}) copy-start(bf16[192,2048]{1,0:T(8,128)(2,1)S(1)} %collective-permute-done.11.refs_13_) | copy-start | bytes 2359300
  170.1 38.2 %copy-start.3 = (f32[2,128]{1,0:T(2,128)S(1)}, f32[2,128]{1,0:T(2,128)}, u32[]{:S(2)}) copy-start(f32[2,128]{1,0:T(2,128)} %find_roots.3) | copy-start | bytes 3076
  170.1 38.2 %copy-start.4 = (f32[1,128]{1,0:T(1,128)S(1)}, f32[1,128]{1,0:T(1,128)}, u32[]{:S(2)}) copy-start(f32[1,128]{1,0:T(1,128)} %find_roots.4) | copy-start | bytes 1540
  170.1 8.4 %collective-permute-start.14 = (bf16[2,48,1024]{2,1,0:T(8,128)(2,1)}, bf16[2,48,1024]{2,1,0:T(8,128)(2,1)S(1)}, u32[]{:S(2)}, u32[]{:S(2)}) collective-permute-start(bf16[2,48,1024]{2,1,0:T(8,128)(2,1)} %get-tuple-element.73), channel_id=1, source_target_pairs={{0,8},{8,16},{16,24},{24,0},{1,9},{9,17},{17,25},{25,1},{2,10},{10... | collective-permute-start | bytes 589832 | tf_op jit(solution)/shard_map/ppermute | solution.py:419
  170.7 11.6 %collective-permute-start.15 = (bf16[2,48,1024]{2,1,0:T(8,128)(2,1)}, bf16[2,48,1024]{2,1,0:T(8,128)(2,1)S(1)}, u32[]{:S(2)}, u32[]{:S(2)}) collective-permute-start(bf16[2,48,1024]{2,1,0:T(8,128)(2,1)} %get-tuple-element.74), channel_id=1, source_target_pairs={{0,16},{8,24},{16,0},{24,8},{1,17},{9,25},{17,1},{25,9},{2,18},{10... | collective-permute-start | bytes 589832 | tf_op jit(solution)/shard_map/ppermute | solution.py:419
  173.1 9.4 %collective-permute-start.16 = (bf16[2,48,1024]{2,1,0:T(8,128)(2,1)}, bf16[2,48,1024]{2,1,0:T(8,128)(2,1)S(1)}, u32[]{:S(2)}, u32[]{:S(2)}) collective-permute-start(bf16[2,48,1024]{2,1,0:T(8,128)(2,1)} %get-tuple-element.75), channel_id=1, source_target_pairs={{0,24},{8,0},{16,8},{24,16},{1,25},{9,1},{17,9},{25,17},{2,26},{10... | collective-permute-start | bytes 589832 | tf_op jit(solution)/shard_map/ppermute | solution.py:419
  174.3 9.3 %collective-permute-start.17 = (bf16[2,48,1024]{2,1,0:T(8,128)(2,1)}, bf16[2,48,1024]{2,1,0:T(8,128)(2,1)S(1)}, u32[]{:S(2)}, u32[]{:S(2)}) collective-permute-start(bf16[2,48,1024]{2,1,0:T(8,128)(2,1)} %get-tuple-element.77), channel_id=1, source_target_pairs={{0,32},{32,64},{64,96},{96,0},{1,33},{33,65},{65,97},{97,1},{2,34}... | collective-permute-start | bytes 589832 | tf_op jit(solution)/shard_map/ppermute | solution.py:419
  175.6 11.3 %collective-permute-start.18 = (bf16[2,48,1024]{2,1,0:T(8,128)(2,1)}, bf16[2,48,1024]{2,1,0:T(8,128)(2,1)S(1)}, u32[]{:S(2)}, u32[]{:S(2)}) collective-permute-start(bf16[2,48,1024]{2,1,0:T(8,128)(2,1)} %get-tuple-element.78), channel_id=1, source_target_pairs={{0,64},{32,96},{64,0},{96,32},{1,65},{33,97},{65,1},{97,33},{2,66}... | collective-permute-start | bytes 589832 | tf_op jit(solution)/shard_map/ppermute | solution.py:419
  178.6 8.4 %collective-permute-start.19 = (bf16[2,48,1024]{2,1,0:T(8,128)(2,1)}, bf16[2,48,1024]{2,1,0:T(8,128)(2,1)S(1)}, u32[]{:S(2)}, u32[]{:S(2)}) collective-permute-start(bf16[2,48,1024]{2,1,0:T(8,128)(2,1)} %get-tuple-element.79), channel_id=1, source_target_pairs={{0,96},{32,0},{64,32},{96,64},{1,97},{33,1},{65,33},{97,65},{2,98}... | collective-permute-start | bytes 589832 | tf_op jit(solution)/shard_map/ppermute | solution.py:419
  188.1 32.0 %collective-permute-start.20 = (f32[2,48,1024]{2,1,0:T(8,128)S(1)}, f32[2,48,1024]{2,1,0:T(8,128)S(1)}, u32[]{:S(2)}, u32[]{:S(2)}) collective-permute-start(f32[2,48,1024]{2,1,0:T(8,128)S(1)} %pad_maximum_fusion.1), channel_id=1, source_target_pairs={{0,1},{1,0},{2,3},{3,2},{4,5},{5,4},{6,7},{7,6},{8,9},{9,8},{10,11... | collective-permute-start | bytes 1179656 | tf_op jit(solution)/shard_map/ppermute | solution.py:427
  209.7 10.5 %all-to-all-start.2 = ((f32[16,4,128]{2,1,0:T(4,128)}), f32[16,4,128]{2,1,0:T(4,128)S(1)}, u32[]{:S(2)}, u32[]{:S(2)}) async-start(f32[16,4,128]{2,1,0:T(4,128)} %broadcast_in_dim.49), calls=%async_computation.2 | async-start | bytes 65536 | tf_op jit(solution)/shard_map/all_to_all | solution.py:298
  (2 other events, 2.8 us)

commit v5 on v4

--- a/solution.py
+++ b/solution.py
@@ -191,6 +191,67 @@
         cost_estimate=cost(5e7),
         name="pick_columns",
     )(index, pw)
+
+
+def turn_kernel(place_ref, in_ref, *refs):
+    outs = refs[:8]
+    wide_ref, half_ref, in_sems, out_sems = refs[8:]
+    blocks, rows = wide_ref.shape[:2]
+
+    def fetch(i):
+        return pltpu.make_async_copy(in_ref.at[pl.ds(i * rows, rows)], wide_ref.at[i], in_sems.at[i])
+
+    def leave(i, half, shift):
+        first = (i % 4 if half == 0 else i // 4) * rows
+        return pltpu.make_async_copy(
+            half_ref.at[half, i], outs[half * 4 + shift].at[pl.ds(first, rows)], out_sems.at[half, i]
+        )
+
+    for i in range(blocks):
+        fetch(i).start()
+
+    def body(i, carry):
+        fetch(i).wait()
+        both = jnp.swapaxes(wide_ref[i], 0, 1)
+        for half in range(2):
+            half_ref[half, i] = both[half]
+            to = ((i // 4 if half == 0 else i % 4) - place_ref[half] + 4) % 4
+            for shift in range(4):
+
+                @pl.when(to == shift)
+                def _():
+                    leave(i, half, shift).start()
+
+        return carry
+
+    lax.fori_loop(0, blocks, body, 0)
+
+    def finish(i, carry):
+        for half in range(2):
+            leave(i, half, 0).wait()
+        return carry
+
+    lax.fori_loop(0, blocks, finish, 0)
+
+
+def turn_blocks(places, wide):
+    n, halves, depth = wide.shape
+    rows = n // 16
+    hbm = pl.BlockSpec(memory_space=pl.ANY)
+    return pl.pallas_call(
+        turn_kernel,
+        in_specs=[pl.BlockSpec(memory_space=pltpu.SMEM), hbm],
+        out_specs=[hbm] * 8,
+        out_shape=[jax.ShapeDtypeStruct((n // 4, depth), BF16)] * 8,
+        scratch_shapes=[
+            pltpu.VMEM((16, rows, halves, depth), BF16),
+            pltpu.VMEM((halves, 16, rows, depth), BF16),
+            pltpu.SemaphoreType.DMA((16,)),
+            pltpu.SemaphoreType.DMA((halves, 16)),
+        ],
+        cost_estimate=cost(5e7),
+        name="turn_blocks",
+    )(places, wide)
 
 
 def matmul_kernel(place_ref, col_ref, root_ref, *refs):
@@ -314,6 +375,13 @@
     n_own = n_col // 16
     swap = [(0, 1), (1, 0)]
 
+    parted = jnp.stack([pole_values.reshape(-1, LANES), weights.reshape(-1, LANES)])
+    arrived = copies(parted, ROW)
+
+    axes = ("z", "x")
+    places = (z, x)
+    cut = turn_blocks(jnp.stack(places).astype(jnp.int32), eigen_blocks)
+
     wanted = lax.dynamic_slice_in_dim(chosen, row * LANES, LANES)
     local = wanted - col * n_col
     hit = local[:, None] == lax.broadcasted_iota(jnp.int32, (1, n_col), 1)
@@ -323,45 +391,19 @@
             jnp.sum(jnp.where(hit, offsets[None, :], 0.0), axis=1),
         ]
     )
-    spread = jnp.moveaxis(first.reshape(2, 8, 16), 1, 0).reshape(8, 1, 32)
-    spread = jnp.tile(jnp.pad(spread, ((0, 0), (0, 0), (0, LANES - 32))), (16, 1, 1))
-    part = jnp.concatenate(
-        [
-            lax.dynamic_slice_in_dim(v.reshape(-1, LANES), col * 4, 4)
-            for v in (pole_values, weights)
-        ]
-    )
-    out = jnp.concatenate([jnp.broadcast_to(part[None], (128, 8, LANES)), spread], axis=1)
-    arrived = lax.all_to_all(out, ALL, 0, 0, tiled=True)
-
-    axes = ("z", "x")
-    places = (z, x)
-    wide = eigen_blocks.reshape(4, 4, -1, 2, eigen_blocks.shape[2])
-    turned = (
-        wide[:, :, :, 0].reshape(4, -1, eigen_blocks.shape[2]),
-        jnp.swapaxes(wide[:, :, :, 1], 0, 1).reshape(4, -1, eigen_blocks.shape[2]),
-    )
-    cut = [
-        [
-            lax.dynamic_index_in_dim(turned[half], (places[half] + shift) % 4, 0, keepdims=False)
-            for shift in range(4)
-        ]
-        for half in range(2)
-    ]
-
-    cut, arrived = lax.optimization_barrier((cut, arrived))
+    spread = jnp.moveaxis(first.reshape(2, 8, 16), 1, 0)
+    arrived, cut, spread = lax.optimization_barrier((arrived, cut, spread))
+    cut = (cut[:4], cut[4:])
+    pw = jnp.moveaxis(arrived, 1, 0).reshape(2, -1, LANES)
+    begun = lax.all_to_all(spread, COL, 0, 0, tiled=True)
     eigen = [[cut[0][0]], [cut[1][0]]]
     for shift in (1, 2, 3):
         for half in range(2):
             eigen[half].append(lax.ppermute(cut[half][shift], axes[half], ring(shift)))
     peer = [[lax.ppermute(eigen[half][0], "core", swap)] for half in range(2)]
 
-    pw = jnp.moveaxis(arrived[:, :8].reshape(128, 2, 4, LANES), 1, 0).reshape(2, -1, LANES)
-    begun = lax.dynamic_slice(arrived, (row * 8, 8, 0), (8, 1, 32))
     panel_start = jnp.pad(
-        jnp.sum(begun, axis=(0, 1)).reshape(2, 16),
-        ((0, 0), (0, LANES - 16)),
-        constant_values=0.25,
+        jnp.sum(begun, axis=0), ((0, 0), (0, LANES - 16)), constant_values=0.25
     )
     panel_end = panel_roots(pw, panel_start)
     index = lax.dynamic_slice_in_dim(column_pole.reshape(-1, LANES), col * 4, 4)

time: 223 us -> 200 us (0.90)
  local copies, waits for them, and re-layouts: 26.3 us -> 9.9 us
  starting transfers between devices: 58.3 us -> 49.8 us
  Pallas kernels: 105 us -> 112 us
  waiting for transfers between devices: 20.4 us -> 17.2 us
    pallas_call x0 -> x1, Pallas kernels: none -> 6.35 us  [turn_blocks(): pl.pallas_call(turn_kernel, in_specs=[pl.BlockSpec(memory_space=pltpu.SME...]
    all_to_all x1, starting transfers between devices: 11.9 us -> 5.98 us  [merge(): begun = lax.all_to_all(spread, COL, 0, 0, tiled=True)]
    unnamed x24 -> x25, local copies, waits for them, and re-layouts: 8.61 us -> 2.98 us
    all_to_all x2 -> x3, starting transfers between devices: 24.2 us -> 19 us  [copies(): lax.all_to_all(jnp.broadcast_to(value[None], (size, *value.shape)), axis,...]
    squeeze x1 -> x0, local copies, waits for them, and re-layouts: 5.22 us -> none  [merge(): lax.dynamic_index_in_dim(turned[half], (places[half] + shift) % 4, 0, kee...]
    transpose x4 -> x1, local copies, waits for them, and re-layouts: 5.26 us -> 0.82 us  [merge(): pw = jnp.moveaxis(arrived, 1, 0).reshape(2, -1, LANES)]
    all_to_all x1, waiting for transfers between devices: 3.38 us -> 0.01 us  [merge(): begun = lax.all_to_all(spread, COL, 0, 0, tiled=True)]
    ppermute x6, starting transfers between devices: 6.88 us -> 9.55 us  [merge(): eigen[half].append(lax.ppermute(cut[half][shift], axes[half], ring(shift)))]
  transfers between devices with their start and end apart: 24 -> 25, of which waited for: 10 -> 9; matrix products, arithmetic and copies ran while one was open for 13% -> 7% of each run, Pallas kernels for 38% -> 45%
where the time goes in v5:
time: 200 us; the launch traced here: 199 us
  Pallas kernels  112 us (56%)
  starting transfers between devices  49.8 us (25%)
  waiting for transfers between devices  17.2 us (9%)
  other arithmetic  10.1 us (5%)
  local copies, waits for them, and re-layouts  9.9 us (5%)
    pallas_call x3, Pallas kernels, find_roots(): pl.pallas_call(root_kernel, in_specs=[pl.BlockSpec(memory_space=pltpu.SME...  71.6 us
    pallas_call x1, Pallas kernels, panel_product(): pl.pallas_call(matmul_kernel, in_specs=[pl.BlockSpec(memory_space=pltpu.S...  21.6 us
    all_to_all x3, starting transfers between devices, copies(): lax.all_to_all(jnp.broadcast_to(value[None], (size, *value.shape)), axis,...  19 us
    ppermute x6, starting transfers between devices, merge(): lax.ppermute(mine[s], axes[1 - half], ring(s))  10.3 us
    ppermute x6, starting transfers between devices, merge(): eigen[half].append(lax.ppermute(cut[half][shift], axes[half], ring(shift)))  9.55 us
    pallas_call x1, Pallas kernels, panel_roots(): pl.pallas_call(panel_kernel, out_shape=jax.ShapeDtypeStruct((2, LANES), F...  7.06 us
    all_to_all x3, waiting for transfers between devices, copies(): lax.all_to_all(jnp.broadcast_to(value[None], (size, *value.shape)), axis,...  6.72 us
    pallas_call x1, Pallas kernels, turn_blocks(): pl.pallas_call(turn_kernel, in_specs=[pl.BlockSpec(memory_space=pltpu.SME...  6.35 us
  transfers between devices with their start and end apart: 25, of which 9 were waited for; matrix products, arithmetic and copies ran while one was open for 7% of the time, Pallas kernels for 45%

profile of v5, /device:TPU:1, one launch (start us, length us, event | category | flops | bytes accessed | tf_op | source)
XLA Modules:
  0.0 199.5 jit_solution(2069334330842116193)
XLA Ops:
  2.2 8.4 %all-to-all-start = ((f32[16,2,32,128]{3,2,1,0:T(8,128)}), f32[16,2,32,128]{3,2,1,0:T(8,128)S(1)}, u32[]{:S(2)}, u32[]{:S(2)}) async-start(f32[16,2,32,128]{3,2,1,0:T(8,128)} %broadcast_in_dim.43), calls=%async_computation | async-start | bytes 1048576 | tf_op jit(solution)/shard_map/all_to_all | solution.py:359
  11.4 2.1 %select_reduce_fusion.1 = (f32[128]{0:T(128)S(1)}, f32[128]{0:T(128)S(1)}) fusion(f32[8192]{0:T(1024)} %param.9, s32[128]{0:T(128)S(1)} %dynamic-slice_subtract_fusion, f32[8192]{0:T(1024)} %param.10), kind=kLoop, calls=%fused_computation.1 | loop fusion | flops 5242624 | bytes 67072 | tf_op jit(solution)/shard_map/reduce_sum | solution.py:390
  14.4 6.3 %turn_blocks.1 = (bf16[192,2048]{1,0:T(8,128)(2,1)}, bf16[192,2048]{1,0:T(8,128)(2,1)}, bf16[192,2048]{1,0:T(8,128)(2,1)}, bf16[192,2048]{1,0:T(8,128)(2,1)}, bf...) custom-call(s32[2]{0:T(128)} %get-tuple-element.129.place_ref, ...), custom_call_target="tpu_custom_call" | custom-call | flops 50000000 | bytes 1048576 | tf_op jit(solution)/shard_map/turn_blocks/pallas_call | solution.py:241
  21.1 1.2 collective-permute-start
  23.4 6.0 %all-to-all-start.1 = ((f32[8,2,16]{2,1,0:T(2,128)}), f32[8,2,16]{2,1,0:T(2,128)S(1)}, u32[]{:S(2)}, u32[]{:S(2)}) async-start(f32[8,2,16]{2,1,0:T(2,128)} %copy.23), calls=%async_computation.1 | async-start | bytes 16384 | tf_op jit(solution)/shard_map/all_to_all | solution.py:398
  30.2 2.4 %collective-permute-start.1 = (bf16[192,2048]{1,0:T(8,128)(2,1)}, bf16[192,2048]{1,0:T(8,128)(2,1)}, u32[]{:S(2)}, u32[]{:S(2)}) collective-permute-start(bf16[192,2048]{1,0:T(8,128)(2,1)} %get-tuple-element.60), channel_id=1, source_target_pairs={{0,64},{32,96},{64,0},{96,32},{1,65},{33,97},{65,1},{97,33},{2,66}... | collective-permute-start | bytes 2359304 | tf_op jit(solution)/shard_map/ppermute | solution.py:402
  32.6 1.2 collective-permute-start.2
  33.8 1.2 collective-permute-start.3
  35.0 2.4 %collective-permute-start.4 = (bf16[192,2048]{1,0:T(8,128)(2,1)}, bf16[192,2048]{1,0:T(8,128)(2,1)}, u32[]{:S(2)}, u32[]{:S(2)}) collective-permute-start(bf16[192,2048]{1,0:T(8,128)(2,1)} %get-tuple-element.64), channel_id=1, source_target_pairs={{0,16},{8,24},{16,0},{24,8},{1,17},{9,25},{17,1},{25,9},{2,18},{10... | collective-permute-start | bytes 2359304 | tf_op jit(solution)/shard_map/ppermute | solution.py:402
  37.4 5.0 %pick_columns.1 = f32[2,4,128]{2,1,0:T(4,128)} custom-call(s32[4,128]{1,0:T(4,128)} %constant_dynamic-slice_fusion.4.index_ref, f32[2,512,128]{2,1,0:T(8,128)} %bitcast.54), custom_call_target="tpu_custom_call" | custom-call | flops 50000000 | bytes 1048576 | tf_op jit(solution)/shard_map/pick_columns/pallas_call | solution.py:188
  43.0 7.1 %panel_roots.1 = f32[2,128]{1,0:T(2,128)} custom-call(f32[2,512,128]{2,1,0:T(8,128)} %bitcast.55, f32[2,128]{1,0:T(2,128)} %pad.4.root_ref), custom_call_target="tpu_custom_call" | custom-call | flops 52428800 | bytes 1048576 | tf_op jit(solution)/shard_map/panel_roots/pallas_call | solution.py:155
  50.0 1.2 collective-permute-start.5
  53.0 6.7 %all-to-all-start.2 = ((f32[128,11,128]{2,1,0:T(8,128)}), f32[128,11,128]{2,1,0:T(8,128)S(1)}, u32[]{:S(2)}, u32[]{:S(2)}) async-start(f32[128,11,128]{2,1,0:T(8,128)} %broadcast_in_dim.47), calls=%async_computation.2 | async-start | bytes 2097152 | tf_op jit(solution)/shard_map/all_to_all | solution.py:359
  61.8 35.0 %find_roots.3 = f32[2,128]{1,0:T(2,128)} custom-call(s32[1]{0:T(128)} %bitcast.8.rank_ref, f32[2,512,128]{2,1,0:T(8,128)} %bitcast.56, f32[4,2,128]{2,1,0:T(2,128)} %slice.102.root_ref), custom_call_target="tpu_custom_call" | custom-call | flops 503316480 | bytes 1048576 | tf_op jit(solution)/shard_map/find_roots/pallas_call | solution.py:102
  99.0 18.3 %find_roots.4 = f32[1,128]{1,0:T(1,128)} custom-call(s32[1]{0:T(128)S(6)} %add.237.rank_ref, f32[2,512,128]{2,1,0:T(8,128)} %bitcast.57, f32[4,1,128]{2,1,0:T(1,128)} %get-tuple-element.127.root_ref), custom_call_target="tpu_custom_call" | custom-call | flops 251658240 | bytes 1048576 | tf_op jit(solution)/shard_map/find_roots/pallas_call | solution.py:102
  120.2 1.1 collective-permute-done.9.refs_7_
  121.3 1.1 collective-permute-done.11.refs_13_
  125.6 21.6 %panel_product.1 = (f32[2,48,1024]{2,1,0:T(8,128)}, bf16[2,48,1024]{2,1,0:T(8,128)(2,1)}, bf16[2,48,1024]{2,1,0:T(8,128)(2,1)}, bf16[2,48,1024]{2,1,0:T(8,128)(2...) custom-call(s32[2]{0:T(128)} %get-tuple-element.130.place_ref, ...), custom_call_target="tpu_custom_call" | custom-call | flops 12884901888 | bytes 1048576 | tf_op jit(solution)/shard_map/panel_product/pallas_call | solution.py:341
  148.0 2.4 %collective-permute-start.15 = (bf16[2,48,1024]{2,1,0:T(8,128)(2,1)}, bf16[2,48,1024]{2,1,0:T(8,128)(2,1)S(1)}, u32[]{:S(2)}, u32[]{:S(2)}) collective-permute-start(bf16[2,48,1024]{2,1,0:T(8,128)(2,1)} %get-tuple-element.92), channel_id=1, source_target_pairs={{0,16},{8,24},{16,0},{24,8},{1,17},{9,25},{17,1},{25,9},{2,18},{10... | collective-permute-start | bytes 589832 | tf_op jit(solution)/shard_map/ppermute | solution.py:461
  150.4 1.2 collective-permute-start.16
  151.6 1.3 collective-permute-start.17
  152.9 2.9 %collective-permute-start.18 = (bf16[2,48,1024]{2,1,0:T(8,128)(2,1)}, bf16[2,48,1024]{2,1,0:T(8,128)(2,1)S(1)}, u32[]{:S(2)}, u32[]{:S(2)}) collective-permute-start(bf16[2,48,1024]{2,1,0:T(8,128)(2,1)} %get-tuple-element.96), channel_id=1, source_target_pairs={{0,64},{32,96},{64,0},{96,32},{1,65},{33,97},{65,1},{97,33},{2,66}... | collective-permute-start | bytes 589832 | tf_op jit(solution)/shard_map/ppermute | solution.py:461
  155.8 1.7 collective-permute-start.19
  157.5 2.1 %collective-permute-done.15 = bf16[2,48,1024]{2,1,0:T(8,128)(2,1)S(1)} collective-permute-done((bf16[2,48,1024]{2,1,0:T(8,128)(2,1)}, bf16[2,48,1024]{2,1,0:T(8,128)(2,1)S(1)}, u32[]{:S(2)}, u32[]{:S(2)}) %collective-permute-start.15) | collective-permute-done | bytes 196640 | tf_op jit(solution)/shard_map/ppermute | solution.py:461
  159.6 1.1 convert_add_fusion.3
  160.7 3.5 %collective-permute-done.18 = bf16[2,48,1024]{2,1,0:T(8,128)(2,1)S(1)} collective-permute-done((bf16[2,48,1024]{2,1,0:T(8,128)(2,1)}, bf16[2,48,1024]{2,1,0:T(8,128)(2,1)S(1)}, u32[]{:S(2)}, u32[]{:S(2)}) %collective-permute-start.18) | collective-permute-done | bytes 196640 | tf_op jit(solution)/shard_map/ppermute | solution.py:461
  164.2 1.1 convert_add_fusion.2
  165.4 2.0 collective-permute-start.20
  167.4 18.3 %find_roots.5 = f32[1,128]{1,0:T(1,128)} custom-call(s32[1]{0:T(128)S(6)} %add.238.rank_ref, f32[2,512,128]{2,1,0:T(8,128)} %bitcast.58, f32[4,1,128]{2,1,0:T(1,128)} %get-tuple-element.128.root_ref), custom_call_target="tpu_custom_call" | custom-call | flops 251658240 | bytes 1048576 | tf_op jit(solution)/shard_map/find_roots/pallas_call | solution.py:102
  186.9 3.9 %all-to-all-start.3 = ((f32[16,4,128]{2,1,0:T(4,128)}), f32[16,4,128]{2,1,0:T(4,128)S(1)}, u32[]{:S(2)}, u32[]{:S(2)}) async-start(f32[16,4,128]{2,1,0:T(4,128)} %broadcast_in_dim.49), calls=%async_computation.3 | async-start | bytes 65536 | tf_op jit(solution)/shard_map/all_to_all | solution.py:359
  190.8 6.4 %all-to-all-done.3 = f32[16,4,128]{2,1,0:T(4,128)S(1)} async-done(((f32[16,4,128]{2,1,0:T(4,128)}), f32[16,4,128]{2,1,0:T(4,128)S(1)}, u32[]{:S(2)}, u32[]{:S(2)}) %all-to-all-start.3) | async-done | bytes 32800 | tf_op jit(solution)/shard_map/all_to_all | solution.py:359
  197.4 1.5 copy.27
  (92 shorter events, 20.9 us)
Async XLA Ops:
  0.6 21.6 %copy-start = (s32[2,2048]{1,0:T(2,128)S(1)}, s32[2,2048]{1,0:T(2,128)}, u32[]{:S(2)}) copy-start(s32[2,2048]{1,0:T(2,128)} %param.12) | copy-start | bytes 49156
  2.2 18.8 %all-to-all-start = ((f32[16,2,32,128]{3,2,1,0:T(8,128)}), f32[16,2,32,128]{3,2,1,0:T(8,128)S(1)}, u32[]{:S(2)}, u32[]{:S(2)}) async-start(f32[16,2,32,128]{3,2,1,0:T(8,128)} %broadcast_in_dim.43), calls=%async_computation | async-start | bytes 1048576 | tf_op jit(solution)/shard_map/all_to_all | solution.py:359
  20.8 76.0 %copy-start.3 = (bf16[192,2048]{1,0:T(8,128)(2,1)S(1)}, bf16[192,2048]{1,0:T(8,128)(2,1)}, u32[]{:S(2)}) copy-start(bf16[192,2048]{1,0:T(8,128)(2,1)} %get-tuple-element.80.refs_0_) | copy-start | bytes 2359300
  20.8 77.1 %copy-start.4 = (bf16[192,2048]{1,0:T(8,128)(2,1)S(1)}, bf16[192,2048]{1,0:T(8,128)(2,1)}, u32[]{:S(2)}) copy-start(bf16[192,2048]{1,0:T(8,128)(2,1)} %get-tuple-element.85.refs_8_) | copy-start | bytes 2359300
  21.1 29.0 %collective-permute-start = (bf16[192,2048]{1,0:T(8,128)(2,1)}, bf16[192,2048]{1,0:T(8,128)(2,1)S(1)}, u32[]{:S(2)}, u32[]{:S(2)}) collective-permute-start(bf16[192,2048]{1,0:T(8,128)(2,1)} %get-tuple-element.59), channel_id=1, source_target_pairs={{0,32},{32,64},{64,96},{96,0},{1,33},{33,65},{65,97},{97,1},{2,34}... | collective-permute-start | bytes 2359304 | tf_op jit(solution)/shard_map/ppermute | solution.py:402
  23.4 18.9 %all-to-all-start.1 = ((f32[8,2,16]{2,1,0:T(2,128)}), f32[8,2,16]{2,1,0:T(2,128)S(1)}, u32[]{:S(2)}, u32[]{:S(2)}) async-start(f32[8,2,16]{2,1,0:T(2,128)} %copy.23), calls=%async_computation.1 | async-start | bytes 16384 | tf_op jit(solution)/shard_map/all_to_all | solution.py:398
  30.2 66.5 %collective-permute-start.1 = (bf16[192,2048]{1,0:T(8,128)(2,1)}, bf16[192,2048]{1,0:T(8,128)(2,1)}, u32[]{:S(2)}, u32[]{:S(2)}) collective-permute-start(bf16[192,2048]{1,0:T(8,128)(2,1)} %get-tuple-element.60), channel_id=1, source_target_pairs={{0,64},{32,96},{64,0},{96,32},{1,65},{33,97},{65,1},{97,33},{2,66}... | collective-permute-start | bytes 2359304 | tf_op jit(solution)/shard_map/ppermute | solution.py:402
  32.6 65.2 %collective-permute-start.2 = (bf16[192,2048]{1,0:T(8,128)(2,1)}, bf16[192,2048]{1,0:T(8,128)(2,1)}, u32[]{:S(2)}, u32[]{:S(2)}) collective-permute-start(bf16[192,2048]{1,0:T(8,128)(2,1)} %get-tuple-element.61), channel_id=1, source_target_pairs={{0,96},{32,0},{64,32},{96,64},{1,97},{33,1},{65,33},{97,65},{2,98}... | collective-permute-start | bytes 2359304 | tf_op jit(solution)/shard_map/ppermute | solution.py:402
  33.8 64.1 %collective-permute-start.3 = (bf16[192,2048]{1,0:T(8,128)(2,1)}, bf16[192,2048]{1,0:T(8,128)(2,1)}, u32[]{:S(2)}, u32[]{:S(2)}) collective-permute-start(bf16[192,2048]{1,0:T(8,128)(2,1)} %get-tuple-element.63), channel_id=1, source_target_pairs={{0,8},{8,16},{16,24},{24,0},{1,9},{9,17},{17,25},{25,1},{2,10},{10... | collective-permute-start | bytes 2359304 | tf_op jit(solution)/shard_map/ppermute | solution.py:402
  35.0 62.9 %collective-permute-start.4 = (bf16[192,2048]{1,0:T(8,128)(2,1)}, bf16[192,2048]{1,0:T(8,128)(2,1)}, u32[]{:S(2)}, u32[]{:S(2)}) collective-permute-start(bf16[192,2048]{1,0:T(8,128)(2,1)} %get-tuple-element.64), channel_id=1, source_target_pairs={{0,16},{8,24},{16,0},{24,8},{1,17},{9,25},{17,1},{25,9},{2,18},{10... | collective-permute-start | bytes 2359304 | tf_op jit(solution)/shard_map/ppermute | solution.py:402
  50.0 47.9 %collective-permute-start.5 = (bf16[192,2048]{1,0:T(8,128)(2,1)}, bf16[192,2048]{1,0:T(8,128)(2,1)}, u32[]{:S(2)}, u32[]{:S(2)}) collective-permute-start(bf16[192,2048]{1,0:T(8,128)(2,1)} %get-tuple-element.65), channel_id=1, source_target_pairs={{0,24},{8,0},{16,8},{24,16},{1,25},{9,1},{17,9},{25,17},{2,26},{10... | collective-permute-start | bytes 2359304 | tf_op jit(solution)/shard_map/ppermute | solution.py:402
  53.0 44.9 %all-to-all-start.2 = ((f32[128,11,128]{2,1,0:T(8,128)}), f32[128,11,128]{2,1,0:T(8,128)S(1)}, u32[]{:S(2)}, u32[]{:S(2)}) async-start(f32[128,11,128]{2,1,0:T(8,128)} %broadcast_in_dim.47), calls=%async_computation.2 | async-start | bytes 2097152 | tf_op jit(solution)/shard_map/all_to_all | solution.py:359
  96.8 21.4 %collective-permute-start.6 = (bf16[192,2048]{1,0:T(8,128)(2,1)S(1)}, bf16[192,2048]{1,0:T(8,128)(2,1)}, u32[]{:S(2)}, u32[]{:S(2)}) collective-permute-start(bf16[192,2048]{1,0:T(8,128)(2,1)S(1)} %copy-done.3), channel_id=1, source_target_pairs={{0,1},{1,0},{2,3},{3,2},{4,5},{5,4},{6,7},{7,6},{8,9},{9,8},{10,11... | collective-permute-start | bytes 2359304 | tf_op jit(solution)/shard_map/ppermute | solution.py:403
  97.8 20.6 %collective-permute-start.10 = (bf16[192,2048]{1,0:T(8,128)(2,1)S(1)}, bf16[192,2048]{1,0:T(8,128)(2,1)}, u32[]{:S(2)}, u32[]{:S(2)}) collective-permute-start(bf16[192,2048]{1,0:T(8,128)(2,1)S(1)} %copy-done.4), channel_id=1, source_target_pairs={{0,1},{1,0},{2,3},{3,2},{4,5},{5,4},{6,7},{7,6},{8,9},{9,8},{10,11... | collective-permute-start | bytes 2359304 | tf_op jit(solution)/shard_map/ppermute | solution.py:403
  98.0 20.8 %collective-permute-start.7 = (bf16[192,2048]{1,0:T(8,128)(2,1)}, bf16[192,2048]{1,0:T(8,128)(2,1)}, u32[]{:S(2)}, u32[]{:S(2)}) collective-permute-start(bf16[192,2048]{1,0:T(8,128)(2,1)} %copy-done.5), channel_id=1, source_target_pairs={{0,1},{1,0},{2,3},{3,2},{4,5},{5,4},{6,7},{7,6},{8,9},{9,8},{10,11... | collective-permute-start | bytes 2359304 | tf_op jit(solution)/shard_map/ppermute | solution.py:427
  117.6 2.6 %collective-permute-start.8 = (bf16[192,2048]{1,0:T(8,128)(2,1)}, bf16[192,2048]{1,0:T(8,128)(2,1)S(1)}, u32[]{:S(2)}, u32[]{:S(2)}) collective-permute-start(bf16[192,2048]{1,0:T(8,128)(2,1)} %collective-permute-done.1.refs_2_), channel_id=1, source_target_pairs={{0,1},{1,0},{2,3},{3,2},{4,5},{5,4},{6,7},{7,6},{8,9},{9,8},{10,11... | collective-permute-start | bytes 2359304 | tf_op jit(solution)/shard_map/ppermute | solution.py:427
  117.9 3.4 %collective-permute-start.9 = (bf16[192,2048]{1,0:T(8,128)(2,1)}, bf16[192,2048]{1,0:T(8,128)(2,1)S(1)}, u32[]{:S(2)}, u32[]{:S(2)}) collective-permute-start(bf16[192,2048]{1,0:T(8,128)(2,1)} %collective-permute-done.2.refs_3_), channel_id=1, source_target_pairs={{0,1},{1,0},{2,3},{3,2},{4,5},{5,4},{6,7},{7,6},{8,9},{9,8},{10,11... | collective-permute-start | bytes 2359304 | tf_op jit(solution)/shard_map/ppermute | solution.py:427
  118.2 4.2 %collective-permute-start.11 = (bf16[192,2048]{1,0:T(8,128)(2,1)}, bf16[192,2048]{1,0:T(8,128)(2,1)S(1)}, u32[]{:S(2)}, u32[]{:S(2)}) collective-permute-start(bf16[192,2048]{1,0:T(8,128)(2,1)} %collective-permute-done.3.refs_9_), channel_id=1, source_target_pairs={{0,1},{1,0},{2,3},{3,2},{4,5},{5,4},{6,7},{7,6},{8,9},{9,8},{10,11... | collective-permute-start | bytes 2359304 | tf_op jit(solution)/shard_map/ppermute | solution.py:427
  118.4 5.2 %collective-permute-start.12 = (bf16[192,2048]{1,0:T(8,128)(2,1)}, bf16[192,2048]{1,0:T(8,128)(2,1)S(1)}, u32[]{:S(2)}, u32[]{:S(2)}) collective-permute-start(bf16[192,2048]{1,0:T(8,128)(2,1)} %collective-permute-done.4.refs_10_), channel_id=1, source_target_pairs={{0,1},{1,0},{2,3},{3,2},{4,5},{5,4},{6,7},{7,6},{8,9},{9,8},{10,11... | collective-permute-start | bytes 2359304 | tf_op jit(solution)/shard_map/ppermute | solution.py:427
  118.7 6.0 %collective-permute-start.13 = (bf16[192,2048]{1,0:T(8,128)(2,1)}, bf16[192,2048]{1,0:T(8,128)(2,1)S(1)}, u32[]{:S(2)}, u32[]{:S(2)}) collective-permute-start(bf16[192,2048]{1,0:T(8,128)(2,1)} %collective-permute-done.5.refs_11_), channel_id=1, source_target_pairs={{0,1},{1,0},{2,3},{3,2},{4,5},{5,4},{6,7},{7,6},{8,9},{9,8},{10,11... | collective-permute-start | bytes 2359304 | tf_op jit(solution)/shard_map/ppermute | solution.py:427
  120.2 5.2 %copy-start.6 = (bf16[192,2048]{1,0:T(8,128)(2,1)}, bf16[192,2048]{1,0:T(8,128)(2,1)S(1)}, u32[]{:S(2)}) copy-start(bf16[192,2048]{1,0:T(8,128)(2,1)S(1)} %collective-permute-done.8.refs_6_) | copy-start | bytes 2359300
  121.3 4.1 %copy-start.7 = (bf16[192,2048]{1,0:T(8,128)(2,1)}, bf16[192,2048]{1,0:T(8,128)(2,1)S(1)}, u32[]{:S(2)}) copy-start(bf16[192,2048]{1,0:T(8,128)(2,1)S(1)} %collective-permute-done.9.refs_7_) | copy-start | bytes 2359300
  147.2 38.4 %copy-start.1 = (f32[2,128]{1,0:T(2,128)S(1)}, f32[2,128]{1,0:T(2,128)}, u32[]{:S(2)}) copy-start(f32[2,128]{1,0:T(2,128)} %find_roots.3) | copy-start | bytes 3076
  147.2 38.4 %copy-start.2 = (f32[1,128]{1,0:T(1,128)S(1)}, f32[1,128]{1,0:T(1,128)}, u32[]{:S(2)}) copy-start(f32[1,128]{1,0:T(1,128)} %find_roots.4) | copy-start | bytes 1540
  147.2 8.6 %collective-permute-start.14 = (bf16[2,48,1024]{2,1,0:T(8,128)(2,1)}, bf16[2,48,1024]{2,1,0:T(8,128)(2,1)S(1)}, u32[]{:S(2)}, u32[]{:S(2)}) collective-permute-start(bf16[2,48,1024]{2,1,0:T(8,128)(2,1)} %get-tuple-element.91), channel_id=1, source_target_pairs={{0,8},{8,16},{16,24},{24,0},{1,9},{9,17},{17,25},{25,1},{2,10},{10... | collective-permute-start | bytes 589832 | tf_op jit(solution)/shard_map/ppermute | solution.py:461
  148.0 11.6 %collective-permute-start.15 = (bf16[2,48,1024]{2,1,0:T(8,128)(2,1)}, bf16[2,48,1024]{2,1,0:T(8,128)(2,1)S(1)}, u32[]{:S(2)}, u32[]{:S(2)}) collective-permute-start(bf16[2,48,1024]{2,1,0:T(8,128)(2,1)} %get-tuple-element.92), channel_id=1, source_target_pairs={{0,16},{8,24},{16,0},{24,8},{1,17},{9,25},{17,1},{25,9},{2,18},{10... | collective-permute-start | bytes 589832 | tf_op jit(solution)/shard_map/ppermute | solution.py:461
  150.4 9.2 %collective-permute-start.16 = (bf16[2,48,1024]{2,1,0:T(8,128)(2,1)}, bf16[2,48,1024]{2,1,0:T(8,128)(2,1)S(1)}, u32[]{:S(2)}, u32[]{:S(2)}) collective-permute-start(bf16[2,48,1024]{2,1,0:T(8,128)(2,1)} %get-tuple-element.93), channel_id=1, source_target_pairs={{0,24},{8,0},{16,8},{24,16},{1,25},{9,1},{17,9},{25,17},{2,26},{10... | collective-permute-start | bytes 589832 | tf_op jit(solution)/shard_map/ppermute | solution.py:461
  151.6 9.2 %collective-permute-start.17 = (bf16[2,48,1024]{2,1,0:T(8,128)(2,1)}, bf16[2,48,1024]{2,1,0:T(8,128)(2,1)S(1)}, u32[]{:S(2)}, u32[]{:S(2)}) collective-permute-start(bf16[2,48,1024]{2,1,0:T(8,128)(2,1)} %get-tuple-element.95), channel_id=1, source_target_pairs={{0,32},{32,64},{64,96},{96,0},{1,33},{33,65},{65,97},{97,1},{2,34}... | collective-permute-start | bytes 589832 | tf_op jit(solution)/shard_map/ppermute | solution.py:461
  152.9 11.3 %collective-permute-start.18 = (bf16[2,48,1024]{2,1,0:T(8,128)(2,1)}, bf16[2,48,1024]{2,1,0:T(8,128)(2,1)S(1)}, u32[]{:S(2)}, u32[]{:S(2)}) collective-permute-start(bf16[2,48,1024]{2,1,0:T(8,128)(2,1)} %get-tuple-element.96), channel_id=1, source_target_pairs={{0,64},{32,96},{64,0},{96,32},{1,65},{33,97},{65,1},{97,33},{2,66}... | collective-permute-start | bytes 589832 | tf_op jit(solution)/shard_map/ppermute | solution.py:461
  155.8 8.4 %collective-permute-start.19 = (bf16[2,48,1024]{2,1,0:T(8,128)(2,1)}, bf16[2,48,1024]{2,1,0:T(8,128)(2,1)S(1)}, u32[]{:S(2)}, u32[]{:S(2)}) collective-permute-start(bf16[2,48,1024]{2,1,0:T(8,128)(2,1)} %get-tuple-element.97), channel_id=1, source_target_pairs={{0,96},{32,0},{64,32},{96,64},{1,97},{33,1},{65,33},{97,65},{2,98}... | collective-permute-start | bytes 589832 | tf_op jit(solution)/shard_map/ppermute | solution.py:461
  165.4 31.9 %collective-permute-start.20 = (f32[2,48,1024]{2,1,0:T(8,128)S(1)}, f32[2,48,1024]{2,1,0:T(8,128)S(1)}, u32[]{:S(2)}, u32[]{:S(2)}) collective-permute-start(f32[2,48,1024]{2,1,0:T(8,128)S(1)} %pad_maximum_fusion), channel_id=1, source_target_pairs={{0,1},{1,0},{2,3},{3,2},{4,5},{5,4},{6,7},{7,6},{8,9},{9,8},{10,11... | collective-permute-start | bytes 1179656 | tf_op jit(solution)/shard_map/ppermute | solution.py:469
  186.9 10.4 %all-to-all-start.3 = ((f32[16,4,128]{2,1,0:T(4,128)}), f32[16,4,128]{2,1,0:T(4,128)S(1)}, u32[]{:S(2)}, u32[]{:S(2)}) async-start(f32[16,4,128]{2,1,0:T(4,128)} %broadcast_in_dim.49), calls=%async_computation.3 | async-start | bytes 65536 | tf_op jit(solution)/shard_map/all_to_all | solution.py:359
  (4 other events, 8.8 us)

commit v6 on v5

--- a/solution.py
+++ b/solution.py
@@ -16,7 +16,6 @@
 GROUP = 128
 BLOCK = 16
 CUT_A = 2
-CUT_B = 3
 
 
 def cost(flops):
@@ -165,29 +164,25 @@
     index = jnp.concatenate([index_ref[...], index_ref[...]], axis=0)
     row = index // LANES
     lane = index % LANES
-    unroll = 16
-
-    def body(r, carry):
-        p, w = carry
+    upper = lax.broadcasted_iota(jnp.int32, (8, LANES), 0) < 4
+    unroll = 32
+
+    def body(r, found):
         for u in range(unroll):
             at = r * unroll + u
-            hit = row == at
-            p_row = jnp.broadcast_to(pw_ref[0, pl.ds(at, 1), :], (8, LANES))
-            w_row = jnp.broadcast_to(pw_ref[1, pl.ds(at, 1), :], (8, LANES))
-            p = jnp.where(hit, jnp.take_along_axis(p_row, lane, axis=1), p)
-            w = jnp.where(hit, jnp.take_along_axis(w_row, lane, axis=1), w)
-        return p, w
-
-    zero = jnp.zeros((8, LANES), F32)
-    p, w = lax.fori_loop(0, pw_ref.shape[1] // unroll, body, (zero, zero))
-    out_ref[0] = p[:4]
-    out_ref[1] = w[:4]
+            values = jnp.where(upper, pw_ref[0, pl.ds(at, 1), :], pw_ref[1, pl.ds(at, 1), :])
+            found = jnp.where(row == at, jnp.take_along_axis(values, lane, axis=1), found)
+        return found
+
+    out_ref[...] = lax.fori_loop(
+        0, pw_ref.shape[1] // unroll, body, jnp.zeros((8, LANES), F32)
+    )
 
 
 def pick_columns(index, pw):
     return pl.pallas_call(
         pick_kernel,
-        out_shape=jax.ShapeDtypeStruct((2, 4, LANES), F32),
+        out_shape=jax.ShapeDtypeStruct((8, LANES), F32),
         cost_estimate=cost(5e7),
         name="pick_columns",
     )(index, pw)
@@ -408,7 +403,7 @@
     panel_end = panel_roots(pw, panel_start)
     index = lax.dynamic_slice_in_dim(column_pole.reshape(-1, LANES), col * 4, 4)
     picked = pick_columns(index, pw)
-    note = jnp.concatenate([picked.reshape(8, LANES), panel_start[:1], panel_end], axis=0)
+    note = jnp.concatenate([picked, panel_start[:1], panel_end], axis=0)
     notes = copies(note, ALL)
 
     start = col * n_col + row * n_own
@@ -425,7 +420,7 @@
 
     for half in range(2):
         peer[half] += [lax.ppermute(block, "core", swap) for block in eigen[half][1:]]
-    roots_b = find_roots(rank + CUT_A * GROUP, pw, state[:, CUT_A:CUT_B])
+    roots_b = find_roots(rank + CUT_A * GROUP, pw, state[:, CUT_A:])
 
     table = notes[:, :8].reshape(4, 4, 2, 4, 2, 4, LANES)
     columns = (
@@ -447,6 +442,7 @@
     panel_root, columns, peer, roots_b = lax.optimization_barrier(
         (panel_root, columns, peer, roots_b)
     )
+    roots = copies(jnp.concatenate([roots_a, roots_b]), ROW)
     sums = panel_product(
         jnp.stack([x, z]).astype(jnp.int32),
         jnp.stack(columns),
@@ -460,12 +456,10 @@
             [mine[0]]
             + [lax.ppermute(mine[s], axes[1 - half], ring(s)) for s in (1, 2, 3)]
         )
-    roots_c = find_roots(rank + CUT_B * GROUP, pw, state[:, CUT_B:])
 
     def added(side):
         return jnp.stack([p[0][side] + p[1][side] + p[2][side] + p[3][side] for p in pieces])
 
-    roots = copies(jnp.concatenate([roots_a, roots_b, roots_c]), ROW)
     got = lax.ppermute(added(1), "core", swap)
     keep = added(0)
     panel = jnp.where(

time: 200 us -> 196 us (0.980)
  Pallas kernels: 112 us -> 108 us
    pallas_call x3 -> x2, Pallas kernels: 71.6 us -> 70 us  [find_roots(): pl.pallas_call(root_kernel, in_specs=[pl.BlockSpec(memory_space=pltpu.SME...]
  transfers between devices with their start and end apart: 25 -> 25, of which waited for: 9 -> 9; matrix products, arithmetic and copies ran while one was open for 7% -> 7% of each run, Pallas kernels for 45% -> 44%
where the time goes in v6:
time: 196 us; the launch traced here: 195 us
  Pallas kernels  108 us (55%)
  starting transfers between devices  49.8 us (25%)
  waiting for transfers between devices  17.2 us (9%)
  local copies, waits for them, and re-layouts  9.98 us (5%)
  other arithmetic  8.81 us (4%)
    pallas_call x2, Pallas kernels, find_roots(): pl.pallas_call(root_kernel, in_specs=[pl.BlockSpec(memory_space=pltpu.SME...  70 us
    pallas_call x1, Pallas kernels, panel_product(): pl.pallas_call(matmul_kernel, in_specs=[pl.BlockSpec(memory_space=pltpu.S...  21.6 us
    all_to_all x3, starting transfers between devices, copies(): lax.all_to_all(jnp.broadcast_to(value[None], (size, *value.shape)), axis,...  19.1 us
    ppermute x6, starting transfers between devices, merge(): lax.ppermute(mine[s], axes[1 - half], ring(s))  10.3 us
    ppermute x6, starting transfers between devices, merge(): eigen[half].append(lax.ppermute(cut[half][shift], axes[half], ring(shift)))  9.48 us
    pallas_call x1, Pallas kernels, panel_roots(): pl.pallas_call(panel_kernel, out_shape=jax.ShapeDtypeStruct((2, LANES), F...  7.03 us
    all_to_all x3, waiting for transfers between devices, copies(): lax.all_to_all(jnp.broadcast_to(value[None], (size, *value.shape)), axis,...  6.79 us
    pallas_call x1, Pallas kernels, turn_blocks(): pl.pallas_call(turn_kernel, in_specs=[pl.BlockSpec(memory_space=pltpu.SME...  6.35 us
  transfers between devices with their start and end apart: 25, of which 9 were waited for; matrix products, arithmetic and copies ran while one was open for 7% of the time, Pallas kernels for 44%

profile of v6, /device:TPU:1, one launch (start us, length us, event | category | flops | bytes accessed | tf_op | source)
XLA Modules:
  0.0 195.0 jit_solution(4523666922395213889)
XLA Ops:
  2.3 8.4 %all-to-all-start = ((f32[16,2,32,128]{3,2,1,0:T(8,128)}), f32[16,2,32,128]{3,2,1,0:T(8,128)S(1)}, u32[]{:S(2)}, u32[]{:S(2)}) async-start(f32[16,2,32,128]{3,2,1,0:T(8,128)} %broadcast_in_dim.43), calls=%async_computation | async-start | bytes 1048576 | tf_op jit(solution)/shard_map/all_to_all | solution.py:354
  11.5 2.1 %select_reduce_fusion.1 = (f32[128]{0:T(128)S(1)}, f32[128]{0:T(128)S(1)}) fusion(f32[8192]{0:T(1024)} %param.9, s32[128]{0:T(128)S(1)} %dynamic-slice_subtract_fusion, f32[8192]{0:T(1024)} %param.10), kind=kLoop, calls=%fused_computation.1 | loop fusion | flops 5242624 | bytes 67072 | tf_op jit(solution)/shard_map/reduce_sum | solution.py:385
  14.4 6.3 %turn_blocks.1 = (bf16[192,2048]{1,0:T(8,128)(2,1)}, bf16[192,2048]{1,0:T(8,128)(2,1)}, bf16[192,2048]{1,0:T(8,128)(2,1)}, bf16[192,2048]{1,0:T(8,128)(2,1)}, bf...) custom-call(s32[2]{0:T(128)} %get-tuple-element.129.place_ref, ...), custom_call_target="tpu_custom_call" | custom-call | flops 50000000 | bytes 1048576 | tf_op jit(solution)/shard_map/turn_blocks/pallas_call | solution.py:236
  23.4 6.0 %all-to-all-start.1 = ((f32[8,2,16]{2,1,0:T(2,128)}), f32[8,2,16]{2,1,0:T(2,128)S(1)}, u32[]{:S(2)}, u32[]{:S(2)}) async-start(f32[8,2,16]{2,1,0:T(2,128)} %copy.23), calls=%async_computation.1 | async-start | bytes 16384 | tf_op jit(solution)/shard_map/all_to_all | solution.py:393
  30.2 2.4 %collective-permute-start.1 = (bf16[192,2048]{1,0:T(8,128)(2,1)}, bf16[192,2048]{1,0:T(8,128)(2,1)}, u32[]{:S(2)}, u32[]{:S(2)}) collective-permute-start(bf16[192,2048]{1,0:T(8,128)(2,1)} %get-tuple-element.60), channel_id=1, source_target_pairs={{0,64},{32,96},{64,0},{96,32},{1,65},{33,97},{65,1},{97,33},{2,66}... | collective-permute-start | bytes 2359304 | tf_op jit(solution)/shard_map/ppermute | solution.py:397
  32.6 1.2 collective-permute-start.2
  33.8 1.2 collective-permute-start.3
  35.0 2.4 %collective-permute-start.4 = (bf16[192,2048]{1,0:T(8,128)(2,1)}, bf16[192,2048]{1,0:T(8,128)(2,1)}, u32[]{:S(2)}, u32[]{:S(2)}) collective-permute-start(bf16[192,2048]{1,0:T(8,128)(2,1)} %get-tuple-element.64), channel_id=1, source_target_pairs={{0,16},{8,24},{16,0},{24,8},{1,17},{9,25},{17,1},{25,9},{2,18},{10... | collective-permute-start | bytes 2359304 | tf_op jit(solution)/shard_map/ppermute | solution.py:397
  37.4 3.3 %pick_columns.1 = f32[8,128]{1,0:T(8,128)} custom-call(s32[4,128]{1,0:T(4,128)} %constant_dynamic-slice_fusion.4.index_ref, f32[2,512,128]{2,1,0:T(8,128)} %bitcast.53), custom_call_target="tpu_custom_call" | custom-call | flops 50000000 | bytes 1048576 | tf_op jit(solution)/shard_map/pick_columns/pallas_call | solution.py:183
  41.3 7.0 %panel_roots.1 = f32[2,128]{1,0:T(2,128)} custom-call(f32[2,512,128]{2,1,0:T(8,128)} %bitcast.54, f32[2,128]{1,0:T(2,128)} %pad.4.root_ref), custom_call_target="tpu_custom_call" | custom-call | flops 52428800 | bytes 1048576 | tf_op jit(solution)/shard_map/panel_roots/pallas_call | solution.py:154
  48.4 1.2 collective-permute-start.5
  51.3 6.7 %all-to-all-start.2 = ((f32[128,11,128]{2,1,0:T(8,128)}), f32[128,11,128]{2,1,0:T(8,128)S(1)}, u32[]{:S(2)}, u32[]{:S(2)}) async-start(f32[128,11,128]{2,1,0:T(8,128)} %broadcast_in_dim.47), calls=%async_computation.2 | async-start | bytes 2097152 | tf_op jit(solution)/shard_map/all_to_all | solution.py:354
  60.1 35.0 %find_roots.2 = f32[2,128]{1,0:T(2,128)} custom-call(s32[1]{0:T(128)} %bitcast.7.rank_ref, f32[2,512,128]{2,1,0:T(8,128)} %bitcast.55, f32[4,2,128]{2,1,0:T(2,128)} %get-tuple-element.128.root_ref), custom_call_target="tpu_custom_call" | custom-call | flops 503316480 | bytes 1048576 | tf_op jit(solution)/shard_map/find_roots/pallas_call | solution.py:101
  96.8 35.0 %find_roots.3 = f32[2,128]{1,0:T(2,128)} custom-call(s32[1]{0:T(128)S(6)} %add.234.rank_ref, f32[2,512,128]{2,1,0:T(8,128)} %bitcast.56, f32[4,2,128]{2,1,0:T(2,128)} %get-tuple-element.127.root_ref), custom_call_target="tpu_custom_call" | custom-call | flops 503316480 | bytes 1048576 | tf_op jit(solution)/shard_map/find_roots/pallas_call | solution.py:101
  134.6 1.1 collective-permute-done.9.refs_7_
  135.7 1.1 collective-permute-done.11.refs_13_
  136.9 1.1 collective-permute-done.12.refs_14_
  138.0 1.1 collective-permute-done.13.refs_15_
  140.1 21.6 %panel_product.1 = (f32[2,48,1024]{2,1,0:T(8,128)}, bf16[2,48,1024]{2,1,0:T(8,128)(2,1)}, bf16[2,48,1024]{2,1,0:T(8,128)(2,1)}, bf16[2,48,1024]{2,1,0:T(8,128)(2...) custom-call(s32[2]{0:T(128)} %get-tuple-element.130.place_ref, ...), custom_call_target="tpu_custom_call" | custom-call | flops 12884901888 | bytes 1048576 | tf_op jit(solution)/shard_map/panel_product/pallas_call | solution.py:336
  162.4 2.4 %collective-permute-start.15 = (bf16[2,48,1024]{2,1,0:T(8,128)(2,1)}, bf16[2,48,1024]{2,1,0:T(8,128)(2,1)S(1)}, u32[]{:S(2)}, u32[]{:S(2)}) collective-permute-start(bf16[2,48,1024]{2,1,0:T(8,128)(2,1)} %get-tuple-element.92), channel_id=1, source_target_pairs={{0,16},{8,24},{16,0},{24,8},{1,17},{9,25},{17,1},{25,9},{2,18},{10... | collective-permute-start | bytes 589832 | tf_op jit(solution)/shard_map/ppermute | solution.py:457
  164.8 1.2 collective-permute-start.16
  166.0 1.3 collective-permute-start.17
  167.4 2.9 %collective-permute-start.18 = (bf16[2,48,1024]{2,1,0:T(8,128)(2,1)}, bf16[2,48,1024]{2,1,0:T(8,128)(2,1)S(1)}, u32[]{:S(2)}, u32[]{:S(2)}) collective-permute-start(bf16[2,48,1024]{2,1,0:T(8,128)(2,1)} %get-tuple-element.96), channel_id=1, source_target_pairs={{0,64},{32,96},{64,0},{96,32},{1,65},{33,97},{65,1},{97,33},{2,66}... | collective-permute-start | bytes 589832 | tf_op jit(solution)/shard_map/ppermute | solution.py:457
  170.3 1.7 collective-permute-start.19
  172.0 2.1 %collective-permute-done.15 = bf16[2,48,1024]{2,1,0:T(8,128)(2,1)S(1)} collective-permute-done((bf16[2,48,1024]{2,1,0:T(8,128)(2,1)}, bf16[2,48,1024]{2,1,0:T(8,128)(2,1)S(1)}, u32[]{:S(2)}, u32[]{:S(2)}) %collective-permute-start.15) | collective-permute-done | bytes 196640 | tf_op jit(solution)/shard_map/ppermute | solution.py:457
  174.1 1.1 convert_add_fusion.3
  175.2 3.5 %collective-permute-done.18 = bf16[2,48,1024]{2,1,0:T(8,128)(2,1)S(1)} collective-permute-done((bf16[2,48,1024]{2,1,0:T(8,128)(2,1)}, bf16[2,48,1024]{2,1,0:T(8,128)(2,1)S(1)}, u32[]{:S(2)}, u32[]{:S(2)}) %collective-permute-start.18) | collective-permute-done | bytes 196640 | tf_op jit(solution)/shard_map/ppermute | solution.py:457
  178.7 1.1 convert_add_fusion.2
  179.8 2.0 %collective-permute-start.20 = (f32[2,48,1024]{2,1,0:T(8,128)S(1)}, f32[2,48,1024]{2,1,0:T(8,128)S(1)}, u32[]{:S(2)}, u32[]{:S(2)}) collective-permute-start(f32[2,48,1024]{2,1,0:T(8,128)S(1)} %pad_maximum_fusion), channel_id=1, source_target_pairs={{0,1},{1,0},{2,3},{3,2},{4,5},{5,4},{6,7},{7,6},{8,9},{9,8},{10,11... | collective-permute-start | bytes 1179656 | tf_op jit(solution)/shard_map/ppermute | solution.py:463
  182.5 3.9 %all-to-all-start.3 = ((f32[16,4,128]{2,1,0:T(4,128)}), f32[16,4,128]{2,1,0:T(4,128)S(1)}, u32[]{:S(2)}, u32[]{:S(2)}) async-start(f32[16,4,128]{2,1,0:T(4,128)} %broadcast_in_dim.49), calls=%async_computation.3 | async-start | bytes 65536 | tf_op jit(solution)/shard_map/all_to_all | solution.py:354
  186.4 6.4 %all-to-all-done.3 = f32[16,4,128]{2,1,0:T(4,128)S(1)} async-done(((f32[16,4,128]{2,1,0:T(4,128)}), f32[16,4,128]{2,1,0:T(4,128)S(1)}, u32[]{:S(2)}, u32[]{:S(2)}) %all-to-all-start.3) | async-done | bytes 32800 | tf_op jit(solution)/shard_map/all_to_all | solution.py:354
  192.9 1.5 copy.27
  (90 shorter events, 18.5 us)
Async XLA Ops:
  0.6 21.6 %copy-start = (s32[2,2048]{1,0:T(2,128)S(1)}, s32[2,2048]{1,0:T(2,128)}, u32[]{:S(2)}) copy-start(s32[2,2048]{1,0:T(2,128)} %param.12) | copy-start | bytes 49156
  2.3 18.8 %all-to-all-start = ((f32[16,2,32,128]{3,2,1,0:T(8,128)}), f32[16,2,32,128]{3,2,1,0:T(8,128)S(1)}, u32[]{:S(2)}, u32[]{:S(2)}) async-start(f32[16,2,32,128]{3,2,1,0:T(8,128)} %broadcast_in_dim.43), calls=%async_computation | async-start | bytes 1048576 | tf_op jit(solution)/shard_map/all_to_all | solution.py:354
  20.7 74.4 %copy-start.3 = (bf16[192,2048]{1,0:T(8,128)(2,1)S(1)}, bf16[192,2048]{1,0:T(8,128)(2,1)}, u32[]{:S(2)}) copy-start(bf16[192,2048]{1,0:T(8,128)(2,1)} %get-tuple-element.80.refs_0_) | copy-start | bytes 2359300
  20.7 75.4 %copy-start.4 = (bf16[192,2048]{1,0:T(8,128)(2,1)S(1)}, bf16[192,2048]{1,0:T(8,128)(2,1)}, u32[]{:S(2)}) copy-start(bf16[192,2048]{1,0:T(8,128)(2,1)} %get-tuple-element.85.refs_8_) | copy-start | bytes 2359300
  21.1 27.2 %collective-permute-start = (bf16[192,2048]{1,0:T(8,128)(2,1)}, bf16[192,2048]{1,0:T(8,128)(2,1)S(1)}, u32[]{:S(2)}, u32[]{:S(2)}) collective-permute-start(bf16[192,2048]{1,0:T(8,128)(2,1)} %get-tuple-element.59), channel_id=1, source_target_pairs={{0,32},{32,64},{64,96},{96,0},{1,33},{33,65},{65,97},{97,1},{2,34}... | collective-permute-start | bytes 2359304 | tf_op jit(solution)/shard_map/ppermute | solution.py:397
  23.4 17.3 %all-to-all-start.1 = ((f32[8,2,16]{2,1,0:T(2,128)}), f32[8,2,16]{2,1,0:T(2,128)S(1)}, u32[]{:S(2)}, u32[]{:S(2)}) async-start(f32[8,2,16]{2,1,0:T(2,128)} %copy.23), calls=%async_computation.1 | async-start | bytes 16384 | tf_op jit(solution)/shard_map/all_to_all | solution.py:393
  30.2 64.9 %collective-permute-start.1 = (bf16[192,2048]{1,0:T(8,128)(2,1)}, bf16[192,2048]{1,0:T(8,128)(2,1)}, u32[]{:S(2)}, u32[]{:S(2)}) collective-permute-start(bf16[192,2048]{1,0:T(8,128)(2,1)} %get-tuple-element.60), channel_id=1, source_target_pairs={{0,64},{32,96},{64,0},{96,32},{1,65},{33,97},{65,1},{97,33},{2,66}... | collective-permute-start | bytes 2359304 | tf_op jit(solution)/shard_map/ppermute | solution.py:397
  32.6 63.5 %collective-permute-start.2 = (bf16[192,2048]{1,0:T(8,128)(2,1)}, bf16[192,2048]{1,0:T(8,128)(2,1)}, u32[]{:S(2)}, u32[]{:S(2)}) collective-permute-start(bf16[192,2048]{1,0:T(8,128)(2,1)} %get-tuple-element.61), channel_id=1, source_target_pairs={{0,96},{32,0},{64,32},{96,64},{1,97},{33,1},{65,33},{97,65},{2,98}... | collective-permute-start | bytes 2359304 | tf_op jit(solution)/shard_map/ppermute | solution.py:397
  33.8 62.5 %collective-permute-start.3 = (bf16[192,2048]{1,0:T(8,128)(2,1)}, bf16[192,2048]{1,0:T(8,128)(2,1)}, u32[]{:S(2)}, u32[]{:S(2)}) collective-permute-start(bf16[192,2048]{1,0:T(8,128)(2,1)} %get-tuple-element.63), channel_id=1, source_target_pairs={{0,8},{8,16},{16,24},{24,0},{1,9},{9,17},{17,25},{25,1},{2,10},{10... | collective-permute-start | bytes 2359304 | tf_op jit(solution)/shard_map/ppermute | solution.py:397
  35.0 61.3 %collective-permute-start.4 = (bf16[192,2048]{1,0:T(8,128)(2,1)}, bf16[192,2048]{1,0:T(8,128)(2,1)}, u32[]{:S(2)}, u32[]{:S(2)}) collective-permute-start(bf16[192,2048]{1,0:T(8,128)(2,1)} %get-tuple-element.64), channel_id=1, source_target_pairs={{0,16},{8,24},{16,0},{24,8},{1,17},{9,25},{17,1},{25,9},{2,18},{10... | collective-permute-start | bytes 2359304 | tf_op jit(solution)/shard_map/ppermute | solution.py:397
  48.4 47.9 %collective-permute-start.5 = (bf16[192,2048]{1,0:T(8,128)(2,1)}, bf16[192,2048]{1,0:T(8,128)(2,1)}, u32[]{:S(2)}, u32[]{:S(2)}) collective-permute-start(bf16[192,2048]{1,0:T(8,128)(2,1)} %get-tuple-element.65), channel_id=1, source_target_pairs={{0,24},{8,0},{16,8},{24,16},{1,25},{9,1},{17,9},{25,17},{2,26},{10... | collective-permute-start | bytes 2359304 | tf_op jit(solution)/shard_map/ppermute | solution.py:397
  51.3 45.0 %all-to-all-start.2 = ((f32[128,11,128]{2,1,0:T(8,128)}), f32[128,11,128]{2,1,0:T(8,128)S(1)}, u32[]{:S(2)}, u32[]{:S(2)}) async-start(f32[128,11,128]{2,1,0:T(8,128)} %broadcast_in_dim.47), calls=%async_computation.2 | async-start | bytes 2097152 | tf_op jit(solution)/shard_map/all_to_all | solution.py:354
  95.1 37.5 %collective-permute-start.6 = (bf16[192,2048]{1,0:T(8,128)(2,1)S(1)}, bf16[192,2048]{1,0:T(8,128)(2,1)}, u32[]{:S(2)}, u32[]{:S(2)}) collective-permute-start(bf16[192,2048]{1,0:T(8,128)(2,1)S(1)} %copy-done.3), channel_id=1, source_target_pairs={{0,1},{1,0},{2,3},{3,2},{4,5},{5,4},{6,7},{7,6},{8,9},{9,8},{10,11... | collective-permute-start | bytes 2359304 | tf_op jit(solution)/shard_map/ppermute | solution.py:398
  96.2 36.6 %collective-permute-start.10 = (bf16[192,2048]{1,0:T(8,128)(2,1)S(1)}, bf16[192,2048]{1,0:T(8,128)(2,1)}, u32[]{:S(2)}, u32[]{:S(2)}) collective-permute-start(bf16[192,2048]{1,0:T(8,128)(2,1)S(1)} %copy-done.4), channel_id=1, source_target_pairs={{0,1},{1,0},{2,3},{3,2},{4,5},{5,4},{6,7},{7,6},{8,9},{9,8},{10,11... | collective-permute-start | bytes 2359304 | tf_op jit(solution)/shard_map/ppermute | solution.py:398
  96.3 36.8 %collective-permute-start.7 = (bf16[192,2048]{1,0:T(8,128)(2,1)}, bf16[192,2048]{1,0:T(8,128)(2,1)}, u32[]{:S(2)}, u32[]{:S(2)}) collective-permute-start(bf16[192,2048]{1,0:T(8,128)(2,1)} %copy-done.5), channel_id=1, source_target_pairs={{0,1},{1,0},{2,3},{3,2},{4,5},{5,4},{6,7},{7,6},{8,9},{9,8},{10,11... | collective-permute-start | bytes 2359304 | tf_op jit(solution)/shard_map/ppermute | solution.py:422
  132.0 2.6 %collective-permute-start.8 = (bf16[192,2048]{1,0:T(8,128)(2,1)}, bf16[192,2048]{1,0:T(8,128)(2,1)S(1)}, u32[]{:S(2)}, u32[]{:S(2)}) collective-permute-start(bf16[192,2048]{1,0:T(8,128)(2,1)} %collective-permute-done.1.refs_2_), channel_id=1, source_target_pairs={{0,1},{1,0},{2,3},{3,2},{4,5},{5,4},{6,7},{7,6},{8,9},{9,8},{10,11... | collective-permute-start | bytes 2359304 | tf_op jit(solution)/shard_map/ppermute | solution.py:422
  132.3 3.4 %collective-permute-start.9 = (bf16[192,2048]{1,0:T(8,128)(2,1)}, bf16[192,2048]{1,0:T(8,128)(2,1)S(1)}, u32[]{:S(2)}, u32[]{:S(2)}) collective-permute-start(bf16[192,2048]{1,0:T(8,128)(2,1)} %collective-permute-done.2.refs_3_), channel_id=1, source_target_pairs={{0,1},{1,0},{2,3},{3,2},{4,5},{5,4},{6,7},{7,6},{8,9},{9,8},{10,11... | collective-permute-start | bytes 2359304 | tf_op jit(solution)/shard_map/ppermute | solution.py:422
  132.6 4.2 %collective-permute-start.11 = (bf16[192,2048]{1,0:T(8,128)(2,1)}, bf16[192,2048]{1,0:T(8,128)(2,1)S(1)}, u32[]{:S(2)}, u32[]{:S(2)}) collective-permute-start(bf16[192,2048]{1,0:T(8,128)(2,1)} %collective-permute-done.3.refs_9_), channel_id=1, source_target_pairs={{0,1},{1,0},{2,3},{3,2},{4,5},{5,4},{6,7},{7,6},{8,9},{9,8},{10,11... | collective-permute-start | bytes 2359304 | tf_op jit(solution)/shard_map/ppermute | solution.py:422
  132.8 5.2 %collective-permute-start.12 = (bf16[192,2048]{1,0:T(8,128)(2,1)}, bf16[192,2048]{1,0:T(8,128)(2,1)S(1)}, u32[]{:S(2)}, u32[]{:S(2)}) collective-permute-start(bf16[192,2048]{1,0:T(8,128)(2,1)} %collective-permute-done.4.refs_10_), channel_id=1, source_target_pairs={{0,1},{1,0},{2,3},{3,2},{4,5},{5,4},{6,7},{7,6},{8,9},{9,8},{10,11... | collective-permute-start | bytes 2359304 | tf_op jit(solution)/shard_map/ppermute | solution.py:422
  133.1 6.0 %collective-permute-start.13 = (bf16[192,2048]{1,0:T(8,128)(2,1)}, bf16[192,2048]{1,0:T(8,128)(2,1)S(1)}, u32[]{:S(2)}, u32[]{:S(2)}) collective-permute-start(bf16[192,2048]{1,0:T(8,128)(2,1)} %collective-permute-done.5.refs_11_), channel_id=1, source_target_pairs={{0,1},{1,0},{2,3},{3,2},{4,5},{5,4},{6,7},{7,6},{8,9},{9,8},{10,11... | collective-permute-start | bytes 2359304 | tf_op jit(solution)/shard_map/ppermute | solution.py:422
  134.6 5.2 %copy-start.6 = (bf16[192,2048]{1,0:T(8,128)(2,1)}, bf16[192,2048]{1,0:T(8,128)(2,1)S(1)}, u32[]{:S(2)}) copy-start(bf16[192,2048]{1,0:T(8,128)(2,1)S(1)} %collective-permute-done.8.refs_6_) | copy-start | bytes 2359300
  135.7 4.1 %copy-start.7 = (bf16[192,2048]{1,0:T(8,128)(2,1)}, bf16[192,2048]{1,0:T(8,128)(2,1)S(1)}, u32[]{:S(2)}) copy-start(bf16[192,2048]{1,0:T(8,128)(2,1)S(1)} %collective-permute-done.9.refs_7_) | copy-start | bytes 2359300
  140.1 41.7 %copy-start.1 = (f32[2,128]{1,0:T(2,128)S(1)}, f32[2,128]{1,0:T(2,128)}, u32[]{:S(2)}) copy-start(f32[2,128]{1,0:T(2,128)} %find_roots.2) | copy-start | bytes 3076
  140.1 41.7 %copy-start.2 = (f32[2,128]{1,0:T(2,128)S(1)}, f32[2,128]{1,0:T(2,128)}, u32[]{:S(2)}) copy-start(f32[2,128]{1,0:T(2,128)} %find_roots.3) | copy-start | bytes 3076
  161.7 8.6 %collective-permute-start.14 = (bf16[2,48,1024]{2,1,0:T(8,128)(2,1)}, bf16[2,48,1024]{2,1,0:T(8,128)(2,1)S(1)}, u32[]{:S(2)}, u32[]{:S(2)}) collective-permute-start(bf16[2,48,1024]{2,1,0:T(8,128)(2,1)} %get-tuple-element.91), channel_id=1, source_target_pairs={{0,8},{8,16},{16,24},{24,0},{1,9},{9,17},{17,25},{25,1},{2,10},{10... | collective-permute-start | bytes 589832 | tf_op jit(solution)/shard_map/ppermute | solution.py:457
  162.4 11.6 %collective-permute-start.15 = (bf16[2,48,1024]{2,1,0:T(8,128)(2,1)}, bf16[2,48,1024]{2,1,0:T(8,128)(2,1)S(1)}, u32[]{:S(2)}, u32[]{:S(2)}) collective-permute-start(bf16[2,48,1024]{2,1,0:T(8,128)(2,1)} %get-tuple-element.92), channel_id=1, source_target_pairs={{0,16},{8,24},{16,0},{24,8},{1,17},{9,25},{17,1},{25,9},{2,18},{10... | collective-permute-start | bytes 589832 | tf_op jit(solution)/shard_map/ppermute | solution.py:457
  164.8 9.2 %collective-permute-start.16 = (bf16[2,48,1024]{2,1,0:T(8,128)(2,1)}, bf16[2,48,1024]{2,1,0:T(8,128)(2,1)S(1)}, u32[]{:S(2)}, u32[]{:S(2)}) collective-permute-start(bf16[2,48,1024]{2,1,0:T(8,128)(2,1)} %get-tuple-element.93), channel_id=1, source_target_pairs={{0,24},{8,0},{16,8},{24,16},{1,25},{9,1},{17,9},{25,17},{2,26},{10... | collective-permute-start | bytes 589832 | tf_op jit(solution)/shard_map/ppermute | solution.py:457
  166.0 9.2 %collective-permute-start.17 = (bf16[2,48,1024]{2,1,0:T(8,128)(2,1)}, bf16[2,48,1024]{2,1,0:T(8,128)(2,1)S(1)}, u32[]{:S(2)}, u32[]{:S(2)}) collective-permute-start(bf16[2,48,1024]{2,1,0:T(8,128)(2,1)} %get-tuple-element.95), channel_id=1, source_target_pairs={{0,32},{32,64},{64,96},{96,0},{1,33},{33,65},{65,97},{97,1},{2,34}... | collective-permute-start | bytes 589832 | tf_op jit(solution)/shard_map/ppermute | solution.py:457
  167.4 11.3 %collective-permute-start.18 = (bf16[2,48,1024]{2,1,0:T(8,128)(2,1)}, bf16[2,48,1024]{2,1,0:T(8,128)(2,1)S(1)}, u32[]{:S(2)}, u32[]{:S(2)}) collective-permute-start(bf16[2,48,1024]{2,1,0:T(8,128)(2,1)} %get-tuple-element.96), channel_id=1, source_target_pairs={{0,64},{32,96},{64,0},{96,32},{1,65},{33,97},{65,1},{97,33},{2,66}... | collective-permute-start | bytes 589832 | tf_op jit(solution)/shard_map/ppermute | solution.py:457
  170.3 8.4 %collective-permute-start.19 = (bf16[2,48,1024]{2,1,0:T(8,128)(2,1)}, bf16[2,48,1024]{2,1,0:T(8,128)(2,1)S(1)}, u32[]{:S(2)}, u32[]{:S(2)}) collective-permute-start(bf16[2,48,1024]{2,1,0:T(8,128)(2,1)} %get-tuple-element.97), channel_id=1, source_target_pairs={{0,96},{32,0},{64,32},{96,64},{1,97},{33,1},{65,33},{97,65},{2,98}... | collective-permute-start | bytes 589832 | tf_op jit(solution)/shard_map/ppermute | solution.py:457
  179.8 13.0 %collective-permute-start.20 = (f32[2,48,1024]{2,1,0:T(8,128)S(1)}, f32[2,48,1024]{2,1,0:T(8,128)S(1)}, u32[]{:S(2)}, u32[]{:S(2)}) collective-permute-start(f32[2,48,1024]{2,1,0:T(8,128)S(1)} %pad_maximum_fusion), channel_id=1, source_target_pairs={{0,1},{1,0},{2,3},{3,2},{4,5},{5,4},{6,7},{7,6},{8,9},{9,8},{10,11... | collective-permute-start | bytes 1179656 | tf_op jit(solution)/shard_map/ppermute | solution.py:463
  182.5 10.4 %all-to-all-start.3 = ((f32[16,4,128]{2,1,0:T(4,128)}), f32[16,4,128]{2,1,0:T(4,128)S(1)}, u32[]{:S(2)}, u32[]{:S(2)}) async-start(f32[16,4,128]{2,1,0:T(4,128)} %broadcast_in_dim.49), calls=%async_computation.3 | async-start | bytes 65536 | tf_op jit(solution)/shard_map/all_to_all | solution.py:354
  (4 other events, 8.8 us)

commit v7 on v6

--- a/solution.py
+++ b/solution.py
@@ -15,7 +15,7 @@
 LANES = 128
 GROUP = 128
 BLOCK = 16
-CUT_A = 2
+CUT_A, CUT_B, CUT_C = 1, 2, 3
 
 
 def cost(flops):
@@ -251,8 +251,8 @@
 
 def matmul_kernel(place_ref, col_ref, root_ref, *refs):
     blocks = refs[:16]
-    outs = refs[16:24]
-    p_ref, w_ref, e_ref, acc_ref, sems = refs[24:]
+    outs = refs[16:20]
+    p_ref, w_ref, e_ref, acc_ref, sems = refs[20:]
     sources = 4
     halves, _, both, depth = e_ref.shape
     rows = both // 2
@@ -315,12 +315,13 @@
 
             @pl.when(half == which)
             def _():
-                for shift in range(4):
-                    part = (place_ref[which] + shift) % 4
-                    for side in range(2):
-                        piece = acc_ref[pl.ds(side * rows + part * quarter, quarter), :]
-                        out = outs[which * 4 + shift]
-                        out[side] = piece.astype(out.dtype)
+                for side in range(2):
+                    mine = pl.ds(side * rows + place_ref[which] * quarter, quarter)
+                    outs[which * 2][side] = acc_ref[mine, :]
+                    for part in range(4):
+                        first = side * rows + part * quarter
+                        piece = acc_ref[first : first + quarter, :]
+                        outs[which * 2 + 1][part, side] = piece.astype(BF16)
 
         return carry
 
@@ -331,12 +332,13 @@
     rows, depth = blocks[0].shape
     n_roots = root.shape[1]
     shape = (2, rows // 4, n_roots)
-    types = [F32, BF16, BF16, BF16] * 2
+    own = jax.ShapeDtypeStruct(shape, F32)
+    send = jax.ShapeDtypeStruct((4, *shape), BF16)
     vmem = pl.BlockSpec(memory_space=pltpu.VMEM)
     return pl.pallas_call(
         matmul_kernel,
         in_specs=[pl.BlockSpec(memory_space=pltpu.SMEM), vmem, vmem] + [pl.BlockSpec(memory_space=pl.ANY)] * 16,
-        out_shape=[jax.ShapeDtypeStruct(shape, t) for t in types],
+        out_shape=[own, send, own, send],
         scratch_shapes=[pltpu.VMEM((4 * depth, LANES), F32)] * 2
         + [
             pltpu.VMEM((2, 4, 2 * rows, depth), BF16),
@@ -420,7 +422,7 @@
 
     for half in range(2):
         peer[half] += [lax.ppermute(block, "core", swap) for block in eigen[half][1:]]
-    roots_b = find_roots(rank + CUT_A * GROUP, pw, state[:, CUT_A:])
+    roots_b = find_roots(rank + CUT_A * GROUP, pw, state[:, CUT_A:CUT_B])
 
     table = notes[:, :8].reshape(4, 4, 2, 4, 2, 4, LANES)
     columns = (
@@ -442,24 +444,28 @@
     panel_root, columns, peer, roots_b = lax.optimization_barrier(
         (panel_root, columns, peer, roots_b)
     )
-    roots = copies(jnp.concatenate([roots_a, roots_b]), ROW)
     sums = panel_product(
         jnp.stack([x, z]).astype(jnp.int32),
         jnp.stack(columns),
         panel_root,
         eigen[0] + peer[0] + eigen[1] + peer[1],
     )
-    pieces = []
+    others = lax.broadcasted_iota(jnp.int32, (4, 1, 1, 1), 0)
+    totals = []
+    roots_cd = []
     for half in range(2):
-        mine = sums[4 * half : 4 * half + 4]
-        pieces.append(
-            [mine[0]]
-            + [lax.ppermute(mine[s], axes[1 - half], ring(s)) for s in (1, 2, 3)]
-        )
+        cuts = (CUT_B, CUT_C, None)[half : half + 2]
+        found = lax.all_to_all(sums[2 * half + 1], axes[1 - half], 0, 0, tiled=True)
+        part = find_roots(rank + cuts[0] * GROUP, pw, state[:, cuts[0] : cuts[1]])
+        found, part, sums = lax.optimization_barrier((found, part, sums))
+        roots_cd.append(part)
+        far = jnp.where(others == places[1 - half], 0.0, found.astype(F32))
+        totals.append(sums[2 * half] + (far[0] + far[1] + far[2] + far[3]))
 
     def added(side):
-        return jnp.stack([p[0][side] + p[1][side] + p[2][side] + p[3][side] for p in pieces])
-
+        return jnp.stack([total[side] for total in totals])
+
+    roots = copies(jnp.concatenate([roots_a, roots_b, *roots_cd]), ROW)
     got = lax.ppermute(added(1), "core", swap)
     keep = added(0)
     panel = jnp.where(

time: 196 us -> 208 us (1.061)
  waiting for transfers between devices: 17.2 us -> 31.1 us
  Pallas kernels: 108 us -> 112 us
  starting transfers between devices: 49.8 us -> 46.5 us
  other arithmetic: 8.81 us -> 5.86 us
    all_to_all x0 -> x2, waiting for transfers between devices: none -> 10.9 us  [merge(): found = lax.all_to_all(sums[2 * half + 1], axes[1 - half], 0, 0, tiled=True)]
    ppermute x6 -> x0, starting transfers between devices: 10.3 us -> none  [merge(): lax.ppermute(mine[s], axes[1 - half], ring(s))]
    all_to_all x3, waiting for transfers between devices: 6.79 us -> 15.3 us  [copies(): lax.all_to_all(jnp.broadcast_to(value[None], (size, *value.shape)), axis,...]
    all_to_all x0 -> x2, starting transfers between devices: none -> 7 us  [merge(): found = lax.all_to_all(sums[2 * half + 1], axes[1 - half], 0, 0, tiled=True)]
    ppermute x6 -> x0, waiting for transfers between devices: 5.54 us -> none  [merge(): lax.ppermute(mine[s], axes[1 - half], ring(s))]
    pallas_call x2 -> x4, Pallas kernels: 70 us -> 73.2 us  [find_roots(): pl.pallas_call(root_kernel, in_specs=[pl.BlockSpec(memory_space=pltpu.SME...]
  transfers between devices with their start and end apart: 25 -> 21, of which waited for: 9 -> 9; matrix products, arithmetic and copies ran while one was open for 7% -> 5% of each run, Pallas kernels for 44% -> 44%
where the time goes in v7:
time: 208 us; the launch traced here: 206 us
  Pallas kernels  112 us (54%)
  starting transfers between devices  46.5 us (22%)
  waiting for transfers between devices  31.1 us (15%)
  local copies, waits for them, and re-layouts  10 us (5%)
  other arithmetic  5.86 us (3%)
    pallas_call x4, Pallas kernels, find_roots(): pl.pallas_call(root_kernel, in_specs=[pl.BlockSpec(memory_space=pltpu.SME...  73.2 us
    pallas_call x1, Pallas kernels, panel_product(): pl.pallas_call(matmul_kernel, in_specs=[pl.BlockSpec(memory_space=pltpu.S...  21.8 us
    all_to_all x3, starting transfers between devices, copies(): lax.all_to_all(jnp.broadcast_to(value[None], (size, *value.shape)), axis,...  20.7 us
    all_to_all x3, waiting for transfers between devices, copies(): lax.all_to_all(jnp.broadcast_to(value[None], (size, *value.shape)), axis,...  15.3 us
    all_to_all x2, waiting for transfers between devices, merge(): found = lax.all_to_all(sums[2 * half + 1], axes[1 - half], 0, 0, tiled=True)  10.9 us
    ppermute x6, starting transfers between devices, merge(): eigen[half].append(lax.ppermute(cut[half][shift], axes[half], ring(shift)))  8.72 us
    pallas_call x1, Pallas kernels, panel_roots(): pl.pallas_call(panel_kernel, out_shape=jax.ShapeDtypeStruct((2, LANES), F...  7.06 us
    all_to_all x2, starting transfers between devices, merge(): found = lax.all_to_all(sums[2 * half + 1], axes[1 - half], 0, 0, tiled=True)  7 us
  transfers between devices with their start and end apart: 21, of which 9 were waited for; matrix products, arithmetic and copies ran while one was open for 5% of the time, Pallas kernels for 44%

profile of v7, /device:TPU:1, one launch (start us, length us, event | category | flops | bytes accessed | tf_op | source)
XLA Modules:
  0.0 206.4 jit_solution(5402160339519991959)
XLA Ops:
  2.3 8.4 %all-to-all-start = ((f32[16,2,32,128]{3,2,1,0:T(8,128)}), f32[16,2,32,128]{3,2,1,0:T(8,128)S(1)}, u32[]{:S(2)}, u32[]{:S(2)}) async-start(f32[16,2,32,128]{3,2,1,0:T(8,128)} %broadcast_in_dim.61), calls=%async_computation | async-start | bytes 1048576 | tf_op jit(solution)/shard_map/all_to_all | solution.py:356
  11.5 1.4 select_reduce_fusion.1
  13.6 6.5 %turn_blocks.1 = (bf16[192,2048]{1,0:T(8,128)(2,1)}, bf16[192,2048]{1,0:T(8,128)(2,1)}, bf16[192,2048]{1,0:T(8,128)(2,1)}, bf16[192,2048]{1,0:T(8,128)(2,1)}, bf...) custom-call(s32[2]{0:T(128)} %get-tuple-element.139.place_ref, ...), custom_call_target="tpu_custom_call" | custom-call | flops 50000000 | bytes 1048576 | tf_op jit(solution)/shard_map/turn_blocks/pallas_call | solution.py:236
  20.1 1.0 all-to-all-done
  22.8 6.1 %all-to-all-start.1 = ((f32[8,2,16]{2,1,0:T(2,128)}), f32[8,2,16]{2,1,0:T(2,128)S(1)}, u32[]{:S(2)}, u32[]{:S(2)}) async-start(f32[8,2,16]{2,1,0:T(2,128)} %copy.23), calls=%async_computation.1 | async-start | bytes 16384 | tf_op jit(solution)/shard_map/all_to_all | solution.py:395
  29.7 2.3 %collective-permute-start.1 = (bf16[192,2048]{1,0:T(8,128)(2,1)}, bf16[192,2048]{1,0:T(8,128)(2,1)}, u32[]{:S(2)}, u32[]{:S(2)}) collective-permute-start(bf16[192,2048]{1,0:T(8,128)(2,1)} %get-tuple-element.64), channel_id=1, source_target_pairs={{0,64},{32,96},{64,0},{96,32},{1,65},{33,97},{65,1},{97,33},{2,66}... | collective-permute-start | bytes 2359304 | tf_op jit(solution)/shard_map/ppermute | solution.py:399
  32.0 1.2 collective-permute-start.2
  33.2 1.2 collective-permute-start.3
  34.4 2.4 %collective-permute-start.4 = (bf16[192,2048]{1,0:T(8,128)(2,1)}, bf16[192,2048]{1,0:T(8,128)(2,1)}, u32[]{:S(2)}, u32[]{:S(2)}) collective-permute-start(bf16[192,2048]{1,0:T(8,128)(2,1)} %get-tuple-element.68), channel_id=1, source_target_pairs={{0,16},{8,24},{16,0},{24,8},{1,17},{9,25},{17,1},{25,9},{2,18},{10... | collective-permute-start | bytes 2359304 | tf_op jit(solution)/shard_map/ppermute | solution.py:399
  36.7 3.3 %pick_columns.1 = f32[8,128]{1,0:T(8,128)} custom-call(s32[4,128]{1,0:T(4,128)} %constant_dynamic-slice_fusion.4.index_ref, f32[2,512,128]{2,1,0:T(8,128)} %bitcast.61), custom_call_target="tpu_custom_call" | custom-call | flops 50000000 | bytes 1048576 | tf_op jit(solution)/shard_map/pick_columns/pallas_call | solution.py:183
  40.6 7.1 %panel_roots.1 = f32[2,128]{1,0:T(2,128)} custom-call(f32[2,512,128]{2,1,0:T(8,128)} %bitcast.62, f32[2,128]{1,0:T(2,128)} %pad.4.root_ref), custom_call_target="tpu_custom_call" | custom-call | flops 52428800 | bytes 1048576 | tf_op jit(solution)/shard_map/panel_roots/pallas_call | solution.py:154
  47.7 1.3 collective-permute-start.5
  49.7 1.0 broadcast_in_dim.65
  50.7 7.4 %all-to-all-start.2 = ((f32[128,11,128]{2,1,0:T(8,128)}), f32[128,11,128]{2,1,0:T(8,128)S(1)}, u32[]{:S(2)}, u32[]{:S(2)}) async-start(f32[128,11,128]{2,1,0:T(8,128)} %broadcast_in_dim.65), calls=%async_computation.2 | async-start | bytes 2097152 | tf_op jit(solution)/shard_map/all_to_all | solution.py:356
  58.8 18.3 %find_roots.4 = f32[1,128]{1,0:T(1,128)} custom-call(s32[1]{0:T(128)} %bitcast.7.rank_ref, f32[2,512,128]{2,1,0:T(8,128)} %bitcast.63, f32[4,1,128]{2,1,0:T(1,128)} %get-tuple-element.138.root_ref), custom_call_target="tpu_custom_call" | custom-call | flops 251658240 | bytes 1048576 | tf_op jit(solution)/shard_map/find_roots/pallas_call | solution.py:101
  77.2 1.1 collective-permute-start.6
  78.3 7.9 %all-to-all-done.2 = f32[128,11,128]{2,1,0:T(8,128)S(1)} async-done(((f32[128,11,128]{2,1,0:T(8,128)}), f32[128,11,128]{2,1,0:T(8,128)S(1)}, u32[]{:S(2)}, u32[]{:S(2)}) %all-to-all-start.2) | async-done | bytes 720928 | tf_op jit(solution)/shard_map/all_to_all | solution.py:356
  86.5 18.3 %find_roots.5 = f32[1,128]{1,0:T(1,128)} custom-call(s32[1]{0:T(128)S(6)} %add.226.rank_ref, f32[2,512,128]{2,1,0:T(8,128)} %bitcast.64, f32[4,1,128]{2,1,0:T(1,128)} %get-tuple-element.137.root_ref), custom_call_target="tpu_custom_call" | custom-call | flops 251658240 | bytes 1048576 | tf_op jit(solution)/shard_map/find_roots/pallas_call | solution.py:101
  107.6 1.1 collective-permute-done.9.refs_7_
  108.8 1.1 collective-permute-done.11.refs_13_
  109.9 1.1 collective-permute-done.12.refs_14_
  111.0 1.1 collective-permute-done.13.refs_15_
  113.1 21.8 %panel_product.1 = (f32[2,48,1024]{2,1,0:T(8,128)}, bf16[4,2,48,1024]{3,2,1,0:T(8,128)(2,1)}, f32[2,48,1024]{2,1,0:T(8,128)}, bf16[4,2,48,1024]{3,2,1,0:T(8,128)(2,1)}) custom-call(s32[2]{0:T(128)} %get-tuple-element.140.place_ref, f32[2,2,4,16,128]{4,3,2,1,0:T(8,128)} %pad_maximum_fusion.1.col_ref, f32[3,1024]{1,0:T(4,128)} %bitcast.76, ...), custom_call_target="tpu_custom_call" | custom-call | flops 12884901888 | bytes 1048576 | tf_op jit(solution)/shard_map/panel_product/pallas_call | solution.py:338
  134.8 3.5 %all-to-all-start.3 = ((bf16[4,2,48,1024]{3,2,1,0:T(8,128)(2,1)}), bf16[4,2,48,1024]{3,2,1,0:T(8,128)(2,1)S(1)}, u32[]{:S(2)}, u32[]{:S(2)}) async-start(bf16[4,2,48,1024]{3,2,1,0:T(8,128)(2,1)} %get-tuple-element.94), calls=%async_computation.3 | async-start | bytes 1572864 | tf_op jit(solution)/shard_map/all_to_all | solution.py:458
  138.4 18.3 %find_roots.7 = f32[1,128]{1,0:T(1,128)} custom-call(s32[1]{0:T(128)S(6)} %add.228.rank_ref, f32[2,512,128]{2,1,0:T(8,128)} %bitcast.65, f32[4,1,128]{2,1,0:T(1,128)} %get-tuple-element.135.root_ref), custom_call_target="tpu_custom_call" | custom-call | flops 251658240 | bytes 1048576 | tf_op jit(solution)/shard_map/find_roots/pallas_call | solution.py:101
  156.7 18.3 %find_roots.6 = f32[1,128]{1,0:T(1,128)} custom-call(s32[1]{0:T(128)S(6)} %add.227.rank_ref, f32[2,512,128]{2,1,0:T(8,128)} %bitcast.66, f32[4,1,128]{2,1,0:T(1,128)} %get-tuple-element.136.root_ref), custom_call_target="tpu_custom_call" | custom-call | flops 251658240 | bytes 1048576 | tf_op jit(solution)/shard_map/find_roots/pallas_call | solution.py:101
  174.9 3.5 %all-to-all-start.4 = ((bf16[4,2,48,1024]{3,2,1,0:T(8,128)(2,1)}), bf16[4,2,48,1024]{3,2,1,0:T(8,128)(2,1)S(1)}, u32[]{:S(2)}, u32[]{:S(2)}) async-start(bf16[4,2,48,1024]{3,2,1,0:T(8,128)(2,1)} %get-tuple-element.99), calls=%async_computation.4 | async-start | bytes 1572864 | tf_op jit(solution)/shard_map/all_to_all | solution.py:458
  179.6 10.9 %all-to-all-done.4 = bf16[4,2,48,1024]{3,2,1,0:T(8,128)(2,1)S(1)} async-done(((bf16[4,2,48,1024]{3,2,1,0:T(8,128)(2,1)}), bf16[4,2,48,1024]{3,2,1,0:T(8,128)(2,1)S(1)}, u32[]{:S(2)}, u32[]{:S(2)}) %all-to-all-start.4) | async-done | bytes 786464 | tf_op jit(solution)/shard_map/all_to_all | solution.py:458
  191.0 1.3 collective-permute-start.14
  192.9 4.9 %all-to-all-start.5 = ((f32[16,4,128]{2,1,0:T(4,128)}), f32[16,4,128]{2,1,0:T(4,128)S(1)}, u32[]{:S(2)}, u32[]{:S(2)}) async-start(f32[16,4,128]{2,1,0:T(4,128)} %broadcast_in_dim.67), calls=%async_computation.5 | async-start | bytes 65536 | tf_op jit(solution)/shard_map/all_to_all | solution.py:356
  197.8 6.4 %all-to-all-done.5 = f32[16,4,128]{2,1,0:T(4,128)S(1)} async-done(((f32[16,4,128]{2,1,0:T(4,128)}), f32[16,4,128]{2,1,0:T(4,128)S(1)}, u32[]{:S(2)}, u32[]{:S(2)}) %all-to-all-start.5) | async-done | bytes 32800 | tf_op jit(solution)/shard_map/all_to_all | solution.py:356
  204.3 1.5 copy.27
  (102 shorter events, 14.5 us)
Async XLA Ops:
  0.6 10.8 %copy-start.2 = (f32[8192]{0:T(1024)S(1)}, f32[8192]{0:T(1024)}, u32[]{:S(2)}) copy-start(f32[8192]{0:T(1024)} %param.10) | copy-start | bytes 98308
  0.6 10.8 %copy-start.3 = (f32[8192]{0:T(1024)S(1)}, f32[8192]{0:T(1024)}, u32[]{:S(2)}) copy-start(f32[8192]{0:T(1024)} %param.9) | copy-start | bytes 98308
  2.3 18.8 %all-to-all-start = ((f32[16,2,32,128]{3,2,1,0:T(8,128)}), f32[16,2,32,128]{3,2,1,0:T(8,128)S(1)}, u32[]{:S(2)}, u32[]{:S(2)}) async-start(f32[16,2,32,128]{3,2,1,0:T(8,128)} %broadcast_in_dim.61), calls=%async_computation | async-start | bytes 1048576 | tf_op jit(solution)/shard_map/all_to_all | solution.py:356
  13.6 7.9 %copy-start.4 = (s32[2,2048]{1,0:T(2,128)S(1)}, s32[2,2048]{1,0:T(2,128)}, u32[]{:S(2)}) copy-start(s32[2,2048]{1,0:T(2,128)} %param.12) | copy-start | bytes 49156
  21.1 26.6 %collective-permute-start = (bf16[192,2048]{1,0:T(8,128)(2,1)}, bf16[192,2048]{1,0:T(8,128)(2,1)S(1)}, u32[]{:S(2)}, u32[]{:S(2)}) collective-permute-start(bf16[192,2048]{1,0:T(8,128)(2,1)} %get-tuple-element.63), channel_id=1, source_target_pairs={{0,32},{32,64},{64,96},{96,0},{1,33},{33,65},{65,97},{97,1},{2,34}... | collective-permute-start | bytes 2359304 | tf_op jit(solution)/shard_map/ppermute | solution.py:399
  22.8 17.3 %all-to-all-start.1 = ((f32[8,2,16]{2,1,0:T(2,128)}), f32[8,2,16]{2,1,0:T(2,128)S(1)}, u32[]{:S(2)}, u32[]{:S(2)}) async-start(f32[8,2,16]{2,1,0:T(2,128)} %copy.23), calls=%async_computation.1 | async-start | bytes 16384 | tf_op jit(solution)/shard_map/all_to_all | solution.py:395
  29.7 47.5 %collective-permute-start.1 = (bf16[192,2048]{1,0:T(8,128)(2,1)}, bf16[192,2048]{1,0:T(8,128)(2,1)}, u32[]{:S(2)}, u32[]{:S(2)}) collective-permute-start(bf16[192,2048]{1,0:T(8,128)(2,1)} %get-tuple-element.64), channel_id=1, source_target_pairs={{0,64},{32,96},{64,0},{96,32},{1,65},{33,97},{65,1},{97,33},{2,66}... | collective-permute-start | bytes 2359304 | tf_op jit(solution)/shard_map/ppermute | solution.py:399
  32.0 46.2 %collective-permute-start.2 = (bf16[192,2048]{1,0:T(8,128)(2,1)}, bf16[192,2048]{1,0:T(8,128)(2,1)}, u32[]{:S(2)}, u32[]{:S(2)}) collective-permute-start(bf16[192,2048]{1,0:T(8,128)(2,1)} %get-tuple-element.65), channel_id=1, source_target_pairs={{0,96},{32,0},{64,32},{96,64},{1,97},{33,1},{65,33},{97,65},{2,98}... | collective-permute-start | bytes 2359304 | tf_op jit(solution)/shard_map/ppermute | solution.py:399
  33.2 53.1 %collective-permute-start.3 = (bf16[192,2048]{1,0:T(8,128)(2,1)}, bf16[192,2048]{1,0:T(8,128)(2,1)}, u32[]{:S(2)}, u32[]{:S(2)}) collective-permute-start(bf16[192,2048]{1,0:T(8,128)(2,1)} %get-tuple-element.67), channel_id=1, source_target_pairs={{0,8},{8,16},{16,24},{24,0},{1,9},{9,17},{17,25},{25,1},{2,10},{10... | collective-permute-start | bytes 2359304 | tf_op jit(solution)/shard_map/ppermute | solution.py:399
  34.4 51.9 %collective-permute-start.4 = (bf16[192,2048]{1,0:T(8,128)(2,1)}, bf16[192,2048]{1,0:T(8,128)(2,1)}, u32[]{:S(2)}, u32[]{:S(2)}) collective-permute-start(bf16[192,2048]{1,0:T(8,128)(2,1)} %get-tuple-element.68), channel_id=1, source_target_pairs={{0,16},{8,24},{16,0},{24,8},{1,17},{9,25},{17,1},{25,9},{2,18},{10... | collective-permute-start | bytes 2359304 | tf_op jit(solution)/shard_map/ppermute | solution.py:399
  47.7 3.0 %copy-start.11 = (bf16[192,2048]{1,0:T(8,128)(2,1)}, bf16[192,2048]{1,0:T(8,128)(2,1)S(1)}, u32[]{:S(2)}) copy-start(bf16[192,2048]{1,0:T(8,128)(2,1)S(1)} %collective-permute-done.refs_1_) | copy-start | bytes 2359300
  47.7 38.6 %collective-permute-start.5 = (bf16[192,2048]{1,0:T(8,128)(2,1)}, bf16[192,2048]{1,0:T(8,128)(2,1)}, u32[]{:S(2)}, u32[]{:S(2)}) collective-permute-start(bf16[192,2048]{1,0:T(8,128)(2,1)} %get-tuple-element.69), channel_id=1, source_target_pairs={{0,24},{8,0},{16,8},{24,16},{1,25},{9,1},{17,9},{25,17},{2,26},{10... | collective-permute-start | bytes 2359304 | tf_op jit(solution)/shard_map/ppermute | solution.py:399
  50.7 26.5 %copy-start.9 = (bf16[192,2048]{1,0:T(8,128)(2,1)S(1)}, bf16[192,2048]{1,0:T(8,128)(2,1)}, u32[]{:S(2)}) copy-start(bf16[192,2048]{1,0:T(8,128)(2,1)} %get-tuple-element.84.refs_0_) | copy-start | bytes 2359300
  50.7 27.5 %copy-start.10 = (bf16[192,2048]{1,0:T(8,128)(2,1)S(1)}, bf16[192,2048]{1,0:T(8,128)(2,1)}, u32[]{:S(2)}) copy-start(bf16[192,2048]{1,0:T(8,128)(2,1)} %get-tuple-element.89.refs_8_) | copy-start | bytes 2359300
  50.7 35.5 %all-to-all-start.2 = ((f32[128,11,128]{2,1,0:T(8,128)}), f32[128,11,128]{2,1,0:T(8,128)S(1)}, u32[]{:S(2)}, u32[]{:S(2)}) async-start(f32[128,11,128]{2,1,0:T(8,128)} %broadcast_in_dim.65), calls=%async_computation.2 | async-start | bytes 2097152 | tf_op jit(solution)/shard_map/all_to_all | solution.py:356
  77.2 28.5 %collective-permute-start.6 = (bf16[192,2048]{1,0:T(8,128)(2,1)S(1)}, bf16[192,2048]{1,0:T(8,128)(2,1)}, u32[]{:S(2)}, u32[]{:S(2)}) collective-permute-start(bf16[192,2048]{1,0:T(8,128)(2,1)S(1)} %copy-done.9), channel_id=1, source_target_pairs={{0,1},{1,0},{2,3},{3,2},{4,5},{5,4},{6,7},{7,6},{8,9},{9,8},{10,11... | collective-permute-start | bytes 2359304 | tf_op jit(solution)/shard_map/ppermute | solution.py:400
  78.2 27.7 %collective-permute-start.10 = (bf16[192,2048]{1,0:T(8,128)(2,1)S(1)}, bf16[192,2048]{1,0:T(8,128)(2,1)}, u32[]{:S(2)}, u32[]{:S(2)}) collective-permute-start(bf16[192,2048]{1,0:T(8,128)(2,1)S(1)} %copy-done.10), channel_id=1, source_target_pairs={{0,1},{1,0},{2,3},{3,2},{4,5},{5,4},{6,7},{7,6},{8,9},{9,8},{10,11... | collective-permute-start | bytes 2359304 | tf_op jit(solution)/shard_map/ppermute | solution.py:400
  86.3 19.9 %collective-permute-start.7 = (bf16[192,2048]{1,0:T(8,128)(2,1)}, bf16[192,2048]{1,0:T(8,128)(2,1)}, u32[]{:S(2)}, u32[]{:S(2)}) collective-permute-start(bf16[192,2048]{1,0:T(8,128)(2,1)} %copy-done.11), channel_id=1, source_target_pairs={{0,1},{1,0},{2,3},{3,2},{4,5},{5,4},{6,7},{7,6},{8,9},{9,8},{10,11... | collective-permute-start | bytes 2359304 | tf_op jit(solution)/shard_map/ppermute | solution.py:424
  105.1 2.6 %collective-permute-start.8 = (bf16[192,2048]{1,0:T(8,128)(2,1)}, bf16[192,2048]{1,0:T(8,128)(2,1)S(1)}, u32[]{:S(2)}, u32[]{:S(2)}) collective-permute-start(bf16[192,2048]{1,0:T(8,128)(2,1)} %collective-permute-done.1.refs_2_), channel_id=1, source_target_pairs={{0,1},{1,0},{2,3},{3,2},{4,5},{5,4},{6,7},{7,6},{8,9},{9,8},{10,11... | collective-permute-start | bytes 2359304 | tf_op jit(solution)/shard_map/ppermute | solution.py:424
  105.5 3.3 %collective-permute-start.9 = (bf16[192,2048]{1,0:T(8,128)(2,1)}, bf16[192,2048]{1,0:T(8,128)(2,1)S(1)}, u32[]{:S(2)}, u32[]{:S(2)}) collective-permute-start(bf16[192,2048]{1,0:T(8,128)(2,1)} %collective-permute-done.2.refs_3_), channel_id=1, source_target_pairs={{0,1},{1,0},{2,3},{3,2},{4,5},{5,4},{6,7},{7,6},{8,9},{9,8},{10,11... | collective-permute-start | bytes 2359304 | tf_op jit(solution)/shard_map/ppermute | solution.py:424
  105.7 4.2 %collective-permute-start.11 = (bf16[192,2048]{1,0:T(8,128)(2,1)}, bf16[192,2048]{1,0:T(8,128)(2,1)S(1)}, u32[]{:S(2)}, u32[]{:S(2)}) collective-permute-start(bf16[192,2048]{1,0:T(8,128)(2,1)} %collective-permute-done.3.refs_9_), channel_id=1, source_target_pairs={{0,1},{1,0},{2,3},{3,2},{4,5},{5,4},{6,7},{7,6},{8,9},{9,8},{10,11... | collective-permute-start | bytes 2359304 | tf_op jit(solution)/shard_map/ppermute | solution.py:424
  106.0 5.0 %collective-permute-start.12 = (bf16[192,2048]{1,0:T(8,128)(2,1)}, bf16[192,2048]{1,0:T(8,128)(2,1)S(1)}, u32[]{:S(2)}, u32[]{:S(2)}) collective-permute-start(bf16[192,2048]{1,0:T(8,128)(2,1)} %collective-permute-done.4.refs_10_), channel_id=1, source_target_pairs={{0,1},{1,0},{2,3},{3,2},{4,5},{5,4},{6,7},{7,6},{8,9},{9,8},{10,11... | collective-permute-start | bytes 2359304 | tf_op jit(solution)/shard_map/ppermute | solution.py:424
  106.2 6.0 %collective-permute-start.13 = (bf16[192,2048]{1,0:T(8,128)(2,1)}, bf16[192,2048]{1,0:T(8,128)(2,1)S(1)}, u32[]{:S(2)}, u32[]{:S(2)}) collective-permute-start(bf16[192,2048]{1,0:T(8,128)(2,1)} %collective-permute-done.5.refs_11_), channel_id=1, source_target_pairs={{0,1},{1,0},{2,3},{3,2},{4,5},{5,4},{6,7},{7,6},{8,9},{9,8},{10,11... | collective-permute-start | bytes 2359304 | tf_op jit(solution)/shard_map/ppermute | solution.py:424
  107.6 5.2 %copy-start.12 = (bf16[192,2048]{1,0:T(8,128)(2,1)}, bf16[192,2048]{1,0:T(8,128)(2,1)S(1)}, u32[]{:S(2)}) copy-start(bf16[192,2048]{1,0:T(8,128)(2,1)S(1)} %collective-permute-done.8.refs_6_) | copy-start | bytes 2359300
  108.8 4.1 %copy-start.13 = (bf16[192,2048]{1,0:T(8,128)(2,1)}, bf16[192,2048]{1,0:T(8,128)(2,1)S(1)}, u32[]{:S(2)}) copy-start(bf16[192,2048]{1,0:T(8,128)(2,1)S(1)} %collective-permute-done.9.refs_7_) | copy-start | bytes 2359300
  109.9 3.0 %copy-start.14 = (bf16[192,2048]{1,0:T(8,128)(2,1)}, bf16[192,2048]{1,0:T(8,128)(2,1)S(1)}, u32[]{:S(2)}) copy-start(bf16[192,2048]{1,0:T(8,128)(2,1)S(1)} %collective-permute-done.11.refs_13_) | copy-start | bytes 2359300
  111.0 1.9 copy-start.15
  134.8 40.1 %all-to-all-start.3 = ((bf16[4,2,48,1024]{3,2,1,0:T(8,128)(2,1)}), bf16[4,2,48,1024]{3,2,1,0:T(8,128)(2,1)S(1)}, u32[]{:S(2)}, u32[]{:S(2)}) async-start(bf16[4,2,48,1024]{3,2,1,0:T(8,128)(2,1)} %get-tuple-element.94), calls=%async_computation.3 | async-start | bytes 1572864 | tf_op jit(solution)/shard_map/all_to_all | solution.py:458
  174.9 15.5 %all-to-all-start.4 = ((bf16[4,2,48,1024]{3,2,1,0:T(8,128)(2,1)}), bf16[4,2,48,1024]{3,2,1,0:T(8,128)(2,1)S(1)}, u32[]{:S(2)}, u32[]{:S(2)}) async-start(bf16[4,2,48,1024]{3,2,1,0:T(8,128)(2,1)} %get-tuple-element.99), calls=%async_computation.4 | async-start | bytes 1572864 | tf_op jit(solution)/shard_map/all_to_all | solution.py:458
  179.6 11.1 %copy-start = (f32[2,48,1024]{2,1,0:T(8,128)S(1)}, f32[2,48,1024]{2,1,0:T(8,128)}, u32[]{:S(2)}) copy-start(f32[2,48,1024]{2,1,0:T(8,128)} %get-tuple-element.104) | copy-start | bytes 1179652
  191.0 13.3 %collective-permute-start.14 = (f32[2,48,1024]{2,1,0:T(8,128)S(1)}, f32[2,48,1024]{2,1,0:T(8,128)S(1)}, u32[]{:S(2)}, u32[]{:S(2)}) collective-permute-start(f32[2,48,1024]{2,1,0:T(8,128)S(1)} %pad_maximum_fusion), channel_id=1, source_target_pairs={{0,1},{1,0},{2,3},{3,2},{4,5},{5,4},{6,7},{7,6},{8,9},{9,8},{10,11... | collective-permute-start | bytes 1179656 | tf_op jit(solution)/shard_map/ppermute | solution.py:469
  192.9 11.4 %all-to-all-start.5 = ((f32[16,4,128]{2,1,0:T(4,128)}), f32[16,4,128]{2,1,0:T(4,128)S(1)}, u32[]{:S(2)}, u32[]{:S(2)}) async-start(f32[16,4,128]{2,1,0:T(4,128)} %broadcast_in_dim.67), calls=%async_computation.5 | async-start | bytes 65536 | tf_op jit(solution)/shard_map/all_to_all | solution.py:356
  (6 other events, 7.9 us)

commit v8 on v7

--- a/solution.py
+++ b/solution.py
@@ -15,7 +15,7 @@
 LANES = 128
 GROUP = 128
 BLOCK = 16
-CUT_A, CUT_B, CUT_C = 1, 2, 3
+CUT_A, CUT_B = 2, 3
 
 
 def cost(flops):
@@ -251,8 +251,8 @@
 
 def matmul_kernel(place_ref, col_ref, root_ref, *refs):
     blocks = refs[:16]
-    outs = refs[16:20]
-    p_ref, w_ref, e_ref, acc_ref, sems = refs[20:]
+    outs = refs[16:22]
+    p_ref, w_ref, e_ref, acc_ref, sems = refs[22:]
     sources = 4
     halves, _, both, depth = e_ref.shape
     rows = both // 2
@@ -317,11 +317,17 @@
             def _():
                 for side in range(2):
                     mine = pl.ds(side * rows + place_ref[which] * quarter, quarter)
-                    outs[which * 2][side] = acc_ref[mine, :]
-                    for part in range(4):
-                        first = side * rows + part * quarter
-                        piece = acc_ref[first : first + quarter, :]
-                        outs[which * 2 + 1][part, side] = piece.astype(BF16)
+                    outs[which * 4][side] = acc_ref[mine, :]
+                    if which == 0:
+                        for shift in (1, 2, 3):
+                            part = (place_ref[which] + shift) % 4
+                            there = pl.ds(side * rows + part * quarter, quarter)
+                            outs[shift][side] = acc_ref[there, :].astype(BF16)
+                    else:
+                        for part in range(4):
+                            first = side * rows + part * quarter
+                            piece = acc_ref[first : first + quarter, :]
+                            outs[5][part, side] = piece.astype(BF16)
 
         return carry
 
@@ -333,12 +339,13 @@
     n_roots = root.shape[1]
     shape = (2, rows // 4, n_roots)
     own = jax.ShapeDtypeStruct(shape, F32)
-    send = jax.ShapeDtypeStruct((4, *shape), BF16)
+    send = jax.ShapeDtypeStruct(shape, BF16)
+    sends = jax.ShapeDtypeStruct((4, *shape), BF16)
     vmem = pl.BlockSpec(memory_space=pltpu.VMEM)
     return pl.pallas_call(
         matmul_kernel,
         in_specs=[pl.BlockSpec(memory_space=pltpu.SMEM), vmem, vmem] + [pl.BlockSpec(memory_space=pl.ANY)] * 16,
-        out_shape=[own, send, own, send],
+        out_shape=[own, send, send, send, own, sends],
         scratch_shapes=[pltpu.VMEM((4 * depth, LANES), F32)] * 2
         + [
             pltpu.VMEM((2, 4, 2 * rows, depth), BF16),
@@ -450,22 +457,20 @@
         panel_root,
         eigen[0] + peer[0] + eigen[1] + peer[1],
     )
+    found = [lax.ppermute(sums[s], "x", ring(s)) for s in (1, 2, 3)]
+    turned = lax.all_to_all(sums[5], "z", 0, 0, tiled=True)
+    roots_c = find_roots(rank + CUT_B * GROUP, pw, state[:, CUT_B:])
     others = lax.broadcasted_iota(jnp.int32, (4, 1, 1, 1), 0)
-    totals = []
-    roots_cd = []
-    for half in range(2):
-        cuts = (CUT_B, CUT_C, None)[half : half + 2]
-        found = lax.all_to_all(sums[2 * half + 1], axes[1 - half], 0, 0, tiled=True)
-        part = find_roots(rank + cuts[0] * GROUP, pw, state[:, cuts[0] : cuts[1]])
-        found, part, sums = lax.optimization_barrier((found, part, sums))
-        roots_cd.append(part)
-        far = jnp.where(others == places[1 - half], 0.0, found.astype(F32))
-        totals.append(sums[2 * half] + (far[0] + far[1] + far[2] + far[3]))
+    far = jnp.where(others == z, 0.0, turned.astype(F32))
+    totals = [
+        sums[0] + found[0] + found[1] + found[2],
+        sums[4] + (far[0] + far[1] + far[2] + far[3]),
+    ]
 
     def added(side):
         return jnp.stack([total[side] for total in totals])
 
-    roots = copies(jnp.concatenate([roots_a, roots_b, *roots_cd]), ROW)
+    roots = copies(jnp.concatenate([roots_a, roots_b, roots_c]), ROW)
     got = lax.ppermute(added(1), "core", swap)
     keep = added(0)
     panel = jnp.where(

time: 208 us -> 201 us (0.966)
  waiting for transfers between devices: 31.1 us -> 21.6 us
  other arithmetic: 5.86 us -> 9.21 us
    all_to_all x3, waiting for transfers between devices: 15.3 us -> 6.74 us  [copies(): lax.all_to_all(jnp.broadcast_to(value[None], (size, *value.shape)), axis,...]
    all_to_all x2 -> x1, waiting for transfers between devices: 10.9 us -> 6.26 us  [merge(): turned = lax.all_to_all(sums[5], 'z', 0, 0, tiled=True)]
    ppermute x0 -> x3, starting transfers between devices: none -> 4.32 us  [merge(): found = [lax.ppermute(sums[s], 'x', ring(s)) for s in (1, 2, 3)]]
    ppermute x0 -> x3, waiting for transfers between devices: none -> 3.66 us  [merge(): found = [lax.ppermute(sums[s], 'x', ring(s)) for s in (1, 2, 3)]]
    all_to_all x2 -> x1, starting transfers between devices: 7 us -> 4.38 us  [merge(): turned = lax.all_to_all(sums[5], 'z', 0, 0, tiled=True)]
    pallas_call x4 -> x3, Pallas kernels: 73.2 us -> 71.6 us  [find_roots(): pl.pallas_call(root_kernel, in_specs=[pl.BlockSpec(memory_space=pltpu.SME...]
  transfers between devices with their start and end apart: 21 -> 23, of which waited for: 9 -> 9; matrix products, arithmetic and copies ran while one was open for 5% -> 7% of each run, Pallas kernels for 44% -> 44%
where the time goes in v8:
time: 201 us; the launch traced here: 200 us
  Pallas kernels  110 us (55%)
  starting transfers between devices  48.1 us (24%)
  waiting for transfers between devices  21.6 us (11%)
  local copies, waits for them, and re-layouts  9.95 us (5%)
  other arithmetic  9.21 us (5%)
    pallas_call x3, Pallas kernels, find_roots(): pl.pallas_call(root_kernel, in_specs=[pl.BlockSpec(memory_space=pltpu.SME...  71.6 us
    pallas_call x1, Pallas kernels, panel_product(): pl.pallas_call(matmul_kernel, in_specs=[pl.BlockSpec(memory_space=pltpu.S...  21.6 us
    all_to_all x3, starting transfers between devices, copies(): lax.all_to_all(jnp.broadcast_to(value[None], (size, *value.shape)), axis,...  18.7 us
    ppermute x6, starting transfers between devices, merge(): eigen[half].append(lax.ppermute(cut[half][shift], axes[half], ring(shift)))  9.47 us
    pallas_call x1, Pallas kernels, panel_roots(): pl.pallas_call(panel_kernel, out_shape=jax.ShapeDtypeStruct((2, LANES), F...  7.08 us
    all_to_all x3, waiting for transfers between devices, copies(): lax.all_to_all(jnp.broadcast_to(value[None], (size, *value.shape)), axis,...  6.74 us
    pallas_call x1, Pallas kernels, turn_blocks(): pl.pallas_call(turn_kernel, in_specs=[pl.BlockSpec(memory_space=pltpu.SME...  6.34 us
    all_to_all x1, waiting for transfers between devices, merge(): turned = lax.all_to_all(sums[5], 'z', 0, 0, tiled=True)  6.26 us
  transfers between devices with their start and end apart: 23, of which 9 were waited for; matrix products, arithmetic and copies ran while one was open for 7% of the time, Pallas kernels for 44%

profile of v8, /device:TPU:1, one launch (start us, length us, event | category | flops | bytes accessed | tf_op | source)
XLA Modules:
  0.0 199.8 jit_solution(5145525722363977867)
XLA Ops:
  2.2 8.4 %all-to-all-start = ((f32[16,2,32,128]{3,2,1,0:T(8,128)}), f32[16,2,32,128]{3,2,1,0:T(8,128)S(1)}, u32[]{:S(2)}, u32[]{:S(2)}) async-start(f32[16,2,32,128]{3,2,1,0:T(8,128)} %broadcast_in_dim.55), calls=%async_computation | async-start | bytes 1048576 | tf_op jit(solution)/shard_map/all_to_all | solution.py:363
  11.4 2.1 %select_reduce_fusion.1 = (f32[128]{0:T(128)S(1)}, f32[128]{0:T(128)S(1)}) fusion(f32[8192]{0:T(1024)} %param.9, s32[128]{0:T(128)S(1)} %dynamic-slice_subtract_fusion, f32[8192]{0:T(1024)} %param.10), kind=kLoop, calls=%fused_computation.1 | loop fusion | flops 5242624 | bytes 67072 | tf_op jit(solution)/shard_map/reduce_sum | solution.py:394
  14.3 6.3 %turn_blocks.1 = (bf16[192,2048]{1,0:T(8,128)(2,1)}, bf16[192,2048]{1,0:T(8,128)(2,1)}, bf16[192,2048]{1,0:T(8,128)(2,1)}, bf16[192,2048]{1,0:T(8,128)(2,1)}, bf...) custom-call(s32[2]{0:T(128)} %get-tuple-element.125.place_ref, ...), custom_call_target="tpu_custom_call" | custom-call | flops 50000000 | bytes 1048576 | tf_op jit(solution)/shard_map/turn_blocks/pallas_call | solution.py:236
  21.1 1.1 collective-permute-start
  23.4 6.0 %all-to-all-start.1 = ((f32[8,2,16]{2,1,0:T(2,128)}), f32[8,2,16]{2,1,0:T(2,128)S(1)}, u32[]{:S(2)}, u32[]{:S(2)}) async-start(f32[8,2,16]{2,1,0:T(2,128)} %copy.23), calls=%async_computation.1 | async-start | bytes 16384 | tf_op jit(solution)/shard_map/all_to_all | solution.py:402
  30.2 2.4 %collective-permute-start.1 = (bf16[192,2048]{1,0:T(8,128)(2,1)}, bf16[192,2048]{1,0:T(8,128)(2,1)}, u32[]{:S(2)}, u32[]{:S(2)}) collective-permute-start(bf16[192,2048]{1,0:T(8,128)(2,1)} %get-tuple-element.58), channel_id=1, source_target_pairs={{0,64},{32,96},{64,0},{96,32},{1,65},{33,97},{65,1},{97,33},{2,66}... | collective-permute-start | bytes 2359304 | tf_op jit(solution)/shard_map/ppermute | solution.py:406
  32.6 1.2 collective-permute-start.2
  33.8 1.2 collective-permute-start.3
  34.9 2.4 %collective-permute-start.4 = (bf16[192,2048]{1,0:T(8,128)(2,1)}, bf16[192,2048]{1,0:T(8,128)(2,1)}, u32[]{:S(2)}, u32[]{:S(2)}) collective-permute-start(bf16[192,2048]{1,0:T(8,128)(2,1)} %get-tuple-element.62), channel_id=1, source_target_pairs={{0,16},{8,24},{16,0},{24,8},{1,17},{9,25},{17,1},{25,9},{2,18},{10... | collective-permute-start | bytes 2359304 | tf_op jit(solution)/shard_map/ppermute | solution.py:406
  37.3 3.3 %pick_columns.1 = f32[8,128]{1,0:T(8,128)} custom-call(s32[4,128]{1,0:T(4,128)} %constant_dynamic-slice_fusion.4.index_ref, f32[2,512,128]{2,1,0:T(8,128)} %bitcast.57), custom_call_target="tpu_custom_call" | custom-call | flops 50000000 | bytes 1048576 | tf_op jit(solution)/shard_map/pick_columns/pallas_call | solution.py:183
  41.2 7.1 %panel_roots.1 = f32[2,128]{1,0:T(2,128)} custom-call(f32[2,512,128]{2,1,0:T(8,128)} %bitcast.58, f32[2,128]{1,0:T(2,128)} %pad.4.root_ref), custom_call_target="tpu_custom_call" | custom-call | flops 52428800 | bytes 1048576 | tf_op jit(solution)/shard_map/panel_roots/pallas_call | solution.py:154
  48.3 1.2 collective-permute-start.5
  51.3 6.7 %all-to-all-start.2 = ((f32[128,11,128]{2,1,0:T(8,128)}), f32[128,11,128]{2,1,0:T(8,128)S(1)}, u32[]{:S(2)}, u32[]{:S(2)}) async-start(f32[128,11,128]{2,1,0:T(8,128)} %broadcast_in_dim.59), calls=%async_computation.2 | async-start | bytes 2097152 | tf_op jit(solution)/shard_map/all_to_all | solution.py:363
  60.1 35.0 %find_roots.3 = f32[2,128]{1,0:T(2,128)} custom-call(s32[1]{0:T(128)} %bitcast.7.rank_ref, f32[2,512,128]{2,1,0:T(8,128)} %bitcast.59, f32[4,2,128]{2,1,0:T(2,128)} %slice.70.root_ref), custom_call_target="tpu_custom_call" | custom-call | flops 503316480 | bytes 1048576 | tf_op jit(solution)/shard_map/find_roots/pallas_call | solution.py:101
  95.1 1.1 collective-permute-start.6
  97.4 18.3 %find_roots.4 = f32[1,128]{1,0:T(1,128)} custom-call(s32[1]{0:T(128)S(6)} %add.215.rank_ref, f32[2,512,128]{2,1,0:T(8,128)} %bitcast.60, f32[4,1,128]{2,1,0:T(1,128)} %get-tuple-element.123.root_ref), custom_call_target="tpu_custom_call" | custom-call | flops 251658240 | bytes 1048576 | tf_op jit(solution)/shard_map/find_roots/pallas_call | solution.py:101
  118.5 1.1 collective-permute-done.9.refs_7_
  119.7 1.1 collective-permute-done.11.refs_13_
  120.8 1.1 collective-permute-done.12.refs_14_
  121.9 1.1 collective-permute-done.13.refs_15_
  124.0 21.6 %panel_product.1 = (f32[2,48,1024]{2,1,0:T(8,128)}, bf16[2,48,1024]{2,1,0:T(8,128)(2,1)}, bf16[2,48,1024]{2,1,0:T(8,128)(2,1)}, bf16[2,48,1024]{2,1,0:T(8,128)(2...) custom-call(s32[2]{0:T(128)} %get-tuple-element.126.place_ref, ...), custom_call_target="tpu_custom_call" | custom-call | flops 12884901888 | bytes 1048576 | tf_op jit(solution)/shard_map/panel_product/pallas_call | solution.py:345
  146.4 2.4 %collective-permute-start.15 = (bf16[2,48,1024]{2,1,0:T(8,128)(2,1)}, bf16[2,48,1024]{2,1,0:T(8,128)(2,1)S(1)}, u32[]{:S(2)}, u32[]{:S(2)}) collective-permute-start(bf16[2,48,1024]{2,1,0:T(8,128)(2,1)} %get-tuple-element.90), channel_id=1, source_target_pairs={{0,16},{8,24},{16,0},{24,8},{1,17},{9,25},{17,1},{25,9},{2,18},{10... | collective-permute-start | bytes 589832 | tf_op jit(solution)/shard_map/ppermute | solution.py:460
  148.8 1.2 collective-permute-start.16
  149.9 4.4 %all-to-all-start.4 = ((bf16[4,2,48,1024]{3,2,1,0:T(8,128)(2,1)}), bf16[4,2,48,1024]{3,2,1,0:T(8,128)(2,1)S(1)}, u32[]{:S(2)}, u32[]{:S(2)}) async-start(bf16[4,2,48,1024]{3,2,1,0:T(8,128)(2,1)} %get-tuple-element.93), calls=%async_computation.4 | async-start | bytes 1572864 | tf_op jit(solution)/shard_map/all_to_all | solution.py:461
  154.3 3.7 %collective-permute-done.15 = bf16[2,48,1024]{2,1,0:T(8,128)(2,1)S(1)} collective-permute-done((bf16[2,48,1024]{2,1,0:T(8,128)(2,1)}, bf16[2,48,1024]{2,1,0:T(8,128)(2,1)S(1)}, u32[]{:S(2)}, u32[]{:S(2)}) %collective-permute-start.15) | collective-permute-done | bytes 196640 | tf_op jit(solution)/shard_map/ppermute | solution.py:460
  158.0 1.1 convert_add_fusion
  159.1 6.3 %all-to-all-done.4 = bf16[4,2,48,1024]{3,2,1,0:T(8,128)(2,1)S(1)} async-done(((bf16[4,2,48,1024]{3,2,1,0:T(8,128)(2,1)}), bf16[4,2,48,1024]{3,2,1,0:T(8,128)(2,1)S(1)}, u32[]{:S(2)}, u32[]{:S(2)}) %all-to-all-start.4) | async-done | bytes 786464 | tf_op jit(solution)/shard_map/all_to_all | solution.py:461
  165.9 2.3 %collective-permute-start.17 = (f32[2,48,1024]{2,1,0:T(8,128)S(1)}, f32[2,48,1024]{2,1,0:T(8,128)S(1)}, u32[]{:S(2)}, u32[]{:S(2)}) collective-permute-start(f32[2,48,1024]{2,1,0:T(8,128)S(1)} %pad_maximum_fusion), channel_id=1, source_target_pairs={{0,1},{1,0},{2,3},{3,2},{4,5},{5,4},{6,7},{7,6},{8,9},{9,8},{10,11... | collective-permute-start | bytes 1179656 | tf_op jit(solution)/shard_map/ppermute | solution.py:474
  168.1 18.3 %find_roots.5 = f32[1,128]{1,0:T(1,128)} custom-call(s32[1]{0:T(128)S(6)} %add.216.rank_ref, f32[2,512,128]{2,1,0:T(8,128)} %bitcast.61, f32[4,1,128]{2,1,0:T(1,128)} %get-tuple-element.124.root_ref), custom_call_target="tpu_custom_call" | custom-call | flops 251658240 | bytes 1048576 | tf_op jit(solution)/shard_map/find_roots/pallas_call | solution.py:101
  187.7 3.5 %all-to-all-start.3 = ((f32[16,4,128]{2,1,0:T(4,128)}), f32[16,4,128]{2,1,0:T(4,128)S(1)}, u32[]{:S(2)}, u32[]{:S(2)}) async-start(f32[16,4,128]{2,1,0:T(4,128)} %broadcast_in_dim.61), calls=%async_computation.3 | async-start | bytes 65536 | tf_op jit(solution)/shard_map/all_to_all | solution.py:363
  191.2 6.4 %all-to-all-done.3 = f32[16,4,128]{2,1,0:T(4,128)S(1)} async-done(((f32[16,4,128]{2,1,0:T(4,128)}), f32[16,4,128]{2,1,0:T(4,128)S(1)}, u32[]{:S(2)}, u32[]{:S(2)}) %all-to-all-start.3) | async-done | bytes 32800 | tf_op jit(solution)/shard_map/all_to_all | solution.py:363
  197.7 1.5 copy.27
  (94 shorter events, 17.9 us)
Async XLA Ops:
  0.6 21.5 %copy-start.1 = (s32[2,2048]{1,0:T(2,128)S(1)}, s32[2,2048]{1,0:T(2,128)}, u32[]{:S(2)}) copy-start(s32[2,2048]{1,0:T(2,128)} %param.12) | copy-start | bytes 49156
  2.2 18.8 %all-to-all-start = ((f32[16,2,32,128]{3,2,1,0:T(8,128)}), f32[16,2,32,128]{3,2,1,0:T(8,128)S(1)}, u32[]{:S(2)}, u32[]{:S(2)}) async-start(f32[16,2,32,128]{3,2,1,0:T(8,128)} %broadcast_in_dim.55), calls=%async_computation | async-start | bytes 1048576 | tf_op jit(solution)/shard_map/all_to_all | solution.py:363
  20.7 74.5 %copy-start.4 = (bf16[192,2048]{1,0:T(8,128)(2,1)S(1)}, bf16[192,2048]{1,0:T(8,128)(2,1)}, u32[]{:S(2)}) copy-start(bf16[192,2048]{1,0:T(8,128)(2,1)} %get-tuple-element.78.refs_0_) | copy-start | bytes 2359300
  20.7 75.5 %copy-start.5 = (bf16[192,2048]{1,0:T(8,128)(2,1)S(1)}, bf16[192,2048]{1,0:T(8,128)(2,1)}, u32[]{:S(2)}) copy-start(bf16[192,2048]{1,0:T(8,128)(2,1)} %get-tuple-element.83.refs_8_) | copy-start | bytes 2359300
  21.1 27.3 %collective-permute-start = (bf16[192,2048]{1,0:T(8,128)(2,1)}, bf16[192,2048]{1,0:T(8,128)(2,1)S(1)}, u32[]{:S(2)}, u32[]{:S(2)}) collective-permute-start(bf16[192,2048]{1,0:T(8,128)(2,1)} %get-tuple-element.57), channel_id=1, source_target_pairs={{0,32},{32,64},{64,96},{96,0},{1,33},{33,65},{65,97},{97,1},{2,34}... | collective-permute-start | bytes 2359304 | tf_op jit(solution)/shard_map/ppermute | solution.py:406
  23.4 17.3 %all-to-all-start.1 = ((f32[8,2,16]{2,1,0:T(2,128)}), f32[8,2,16]{2,1,0:T(2,128)S(1)}, u32[]{:S(2)}, u32[]{:S(2)}) async-start(f32[8,2,16]{2,1,0:T(2,128)} %copy.23), calls=%async_computation.1 | async-start | bytes 16384 | tf_op jit(solution)/shard_map/all_to_all | solution.py:402
  30.2 65.0 %collective-permute-start.1 = (bf16[192,2048]{1,0:T(8,128)(2,1)}, bf16[192,2048]{1,0:T(8,128)(2,1)}, u32[]{:S(2)}, u32[]{:S(2)}) collective-permute-start(bf16[192,2048]{1,0:T(8,128)(2,1)} %get-tuple-element.58), channel_id=1, source_target_pairs={{0,64},{32,96},{64,0},{96,32},{1,65},{33,97},{65,1},{97,33},{2,66}... | collective-permute-start | bytes 2359304 | tf_op jit(solution)/shard_map/ppermute | solution.py:406
  32.6 63.6 %collective-permute-start.2 = (bf16[192,2048]{1,0:T(8,128)(2,1)}, bf16[192,2048]{1,0:T(8,128)(2,1)}, u32[]{:S(2)}, u32[]{:S(2)}) collective-permute-start(bf16[192,2048]{1,0:T(8,128)(2,1)} %get-tuple-element.59), channel_id=1, source_target_pairs={{0,96},{32,0},{64,32},{96,64},{1,97},{33,1},{65,33},{97,65},{2,98}... | collective-permute-start | bytes 2359304 | tf_op jit(solution)/shard_map/ppermute | solution.py:406
  33.8 62.6 %collective-permute-start.3 = (bf16[192,2048]{1,0:T(8,128)(2,1)}, bf16[192,2048]{1,0:T(8,128)(2,1)}, u32[]{:S(2)}, u32[]{:S(2)}) collective-permute-start(bf16[192,2048]{1,0:T(8,128)(2,1)} %get-tuple-element.61), channel_id=1, source_target_pairs={{0,8},{8,16},{16,24},{24,0},{1,9},{9,17},{17,25},{25,1},{2,10},{10... | collective-permute-start | bytes 2359304 | tf_op jit(solution)/shard_map/ppermute | solution.py:406
  34.9 61.4 %collective-permute-start.4 = (bf16[192,2048]{1,0:T(8,128)(2,1)}, bf16[192,2048]{1,0:T(8,128)(2,1)}, u32[]{:S(2)}, u32[]{:S(2)}) collective-permute-start(bf16[192,2048]{1,0:T(8,128)(2,1)} %get-tuple-element.62), channel_id=1, source_target_pairs={{0,16},{8,24},{16,0},{24,8},{1,17},{9,25},{17,1},{25,9},{2,18},{10... | collective-permute-start | bytes 2359304 | tf_op jit(solution)/shard_map/ppermute | solution.py:406
  48.3 3.0 %copy-start.6 = (bf16[192,2048]{1,0:T(8,128)(2,1)}, bf16[192,2048]{1,0:T(8,128)(2,1)S(1)}, u32[]{:S(2)}) copy-start(bf16[192,2048]{1,0:T(8,128)(2,1)S(1)} %collective-permute-done.refs_1_) | copy-start | bytes 2359300
  48.3 48.0 %collective-permute-start.5 = (bf16[192,2048]{1,0:T(8,128)(2,1)}, bf16[192,2048]{1,0:T(8,128)(2,1)}, u32[]{:S(2)}, u32[]{:S(2)}) collective-permute-start(bf16[192,2048]{1,0:T(8,128)(2,1)} %get-tuple-element.63), channel_id=1, source_target_pairs={{0,24},{8,0},{16,8},{24,16},{1,25},{9,1},{17,9},{25,17},{2,26},{10... | collective-permute-start | bytes 2359304 | tf_op jit(solution)/shard_map/ppermute | solution.py:406
  51.3 45.0 %all-to-all-start.2 = ((f32[128,11,128]{2,1,0:T(8,128)}), f32[128,11,128]{2,1,0:T(8,128)S(1)}, u32[]{:S(2)}, u32[]{:S(2)}) async-start(f32[128,11,128]{2,1,0:T(8,128)} %broadcast_in_dim.59), calls=%async_computation.2 | async-start | bytes 2097152 | tf_op jit(solution)/shard_map/all_to_all | solution.py:363
  95.1 21.4 %collective-permute-start.6 = (bf16[192,2048]{1,0:T(8,128)(2,1)S(1)}, bf16[192,2048]{1,0:T(8,128)(2,1)}, u32[]{:S(2)}, u32[]{:S(2)}) collective-permute-start(bf16[192,2048]{1,0:T(8,128)(2,1)S(1)} %copy-done.4), channel_id=1, source_target_pairs={{0,1},{1,0},{2,3},{3,2},{4,5},{5,4},{6,7},{7,6},{8,9},{9,8},{10,11... | collective-permute-start | bytes 2359304 | tf_op jit(solution)/shard_map/ppermute | solution.py:407
  96.2 20.5 %collective-permute-start.10 = (bf16[192,2048]{1,0:T(8,128)(2,1)S(1)}, bf16[192,2048]{1,0:T(8,128)(2,1)}, u32[]{:S(2)}, u32[]{:S(2)}) collective-permute-start(bf16[192,2048]{1,0:T(8,128)(2,1)S(1)} %copy-done.5), channel_id=1, source_target_pairs={{0,1},{1,0},{2,3},{3,2},{4,5},{5,4},{6,7},{7,6},{8,9},{9,8},{10,11... | collective-permute-start | bytes 2359304 | tf_op jit(solution)/shard_map/ppermute | solution.py:407
  96.3 20.7 %collective-permute-start.7 = (bf16[192,2048]{1,0:T(8,128)(2,1)}, bf16[192,2048]{1,0:T(8,128)(2,1)}, u32[]{:S(2)}, u32[]{:S(2)}) collective-permute-start(bf16[192,2048]{1,0:T(8,128)(2,1)} %copy-done.6), channel_id=1, source_target_pairs={{0,1},{1,0},{2,3},{3,2},{4,5},{5,4},{6,7},{7,6},{8,9},{9,8},{10,11... | collective-permute-start | bytes 2359304 | tf_op jit(solution)/shard_map/ppermute | solution.py:431
  116.0 2.6 %collective-permute-start.8 = (bf16[192,2048]{1,0:T(8,128)(2,1)}, bf16[192,2048]{1,0:T(8,128)(2,1)S(1)}, u32[]{:S(2)}, u32[]{:S(2)}) collective-permute-start(bf16[192,2048]{1,0:T(8,128)(2,1)} %collective-permute-done.1.refs_2_), channel_id=1, source_target_pairs={{0,1},{1,0},{2,3},{3,2},{4,5},{5,4},{6,7},{7,6},{8,9},{9,8},{10,11... | collective-permute-start | bytes 2359304 | tf_op jit(solution)/shard_map/ppermute | solution.py:431
  116.2 3.4 %collective-permute-start.9 = (bf16[192,2048]{1,0:T(8,128)(2,1)}, bf16[192,2048]{1,0:T(8,128)(2,1)S(1)}, u32[]{:S(2)}, u32[]{:S(2)}) collective-permute-start(bf16[192,2048]{1,0:T(8,128)(2,1)} %collective-permute-done.2.refs_3_), channel_id=1, source_target_pairs={{0,1},{1,0},{2,3},{3,2},{4,5},{5,4},{6,7},{7,6},{8,9},{9,8},{10,11... | collective-permute-start | bytes 2359304 | tf_op jit(solution)/shard_map/ppermute | solution.py:431
  116.5 4.2 %collective-permute-start.11 = (bf16[192,2048]{1,0:T(8,128)(2,1)}, bf16[192,2048]{1,0:T(8,128)(2,1)S(1)}, u32[]{:S(2)}, u32[]{:S(2)}) collective-permute-start(bf16[192,2048]{1,0:T(8,128)(2,1)} %collective-permute-done.3.refs_9_), channel_id=1, source_target_pairs={{0,1},{1,0},{2,3},{3,2},{4,5},{5,4},{6,7},{7,6},{8,9},{9,8},{10,11... | collective-permute-start | bytes 2359304 | tf_op jit(solution)/shard_map/ppermute | solution.py:431
  116.7 5.2 %collective-permute-start.12 = (bf16[192,2048]{1,0:T(8,128)(2,1)}, bf16[192,2048]{1,0:T(8,128)(2,1)S(1)}, u32[]{:S(2)}, u32[]{:S(2)}) collective-permute-start(bf16[192,2048]{1,0:T(8,128)(2,1)} %collective-permute-done.4.refs_10_), channel_id=1, source_target_pairs={{0,1},{1,0},{2,3},{3,2},{4,5},{5,4},{6,7},{7,6},{8,9},{9,8},{10,11... | collective-permute-start | bytes 2359304 | tf_op jit(solution)/shard_map/ppermute | solution.py:431
  117.1 6.0 %collective-permute-start.13 = (bf16[192,2048]{1,0:T(8,128)(2,1)}, bf16[192,2048]{1,0:T(8,128)(2,1)S(1)}, u32[]{:S(2)}, u32[]{:S(2)}) collective-permute-start(bf16[192,2048]{1,0:T(8,128)(2,1)} %collective-permute-done.5.refs_11_), channel_id=1, source_target_pairs={{0,1},{1,0},{2,3},{3,2},{4,5},{5,4},{6,7},{7,6},{8,9},{9,8},{10,11... | collective-permute-start | bytes 2359304 | tf_op jit(solution)/shard_map/ppermute | solution.py:431
  118.5 5.2 %copy-start.7 = (bf16[192,2048]{1,0:T(8,128)(2,1)}, bf16[192,2048]{1,0:T(8,128)(2,1)S(1)}, u32[]{:S(2)}) copy-start(bf16[192,2048]{1,0:T(8,128)(2,1)S(1)} %collective-permute-done.8.refs_6_) | copy-start | bytes 2359300
  119.7 4.1 %copy-start.8 = (bf16[192,2048]{1,0:T(8,128)(2,1)}, bf16[192,2048]{1,0:T(8,128)(2,1)S(1)}, u32[]{:S(2)}) copy-start(bf16[192,2048]{1,0:T(8,128)(2,1)S(1)} %collective-permute-done.9.refs_7_) | copy-start | bytes 2359300
  145.6 20.0 %copy-start = (f32[2,48,1024]{2,1,0:T(8,128)S(1)}, f32[2,48,1024]{2,1,0:T(8,128)}, u32[]{:S(2)}) copy-start(f32[2,48,1024]{2,1,0:T(8,128)} %get-tuple-element.92) | copy-start | bytes 1179652
  145.6 8.7 %collective-permute-start.14 = (bf16[2,48,1024]{2,1,0:T(8,128)(2,1)}, bf16[2,48,1024]{2,1,0:T(8,128)(2,1)S(1)}, u32[]{:S(2)}, u32[]{:S(2)}) collective-permute-start(bf16[2,48,1024]{2,1,0:T(8,128)(2,1)} %get-tuple-element.89), channel_id=1, source_target_pairs={{0,8},{8,16},{16,24},{24,0},{1,9},{9,17},{17,25},{25,1},{2,10},{10... | collective-permute-start | bytes 589832 | tf_op jit(solution)/shard_map/ppermute | solution.py:460
  146.4 11.6 %collective-permute-start.15 = (bf16[2,48,1024]{2,1,0:T(8,128)(2,1)}, bf16[2,48,1024]{2,1,0:T(8,128)(2,1)S(1)}, u32[]{:S(2)}, u32[]{:S(2)}) collective-permute-start(bf16[2,48,1024]{2,1,0:T(8,128)(2,1)} %get-tuple-element.90), channel_id=1, source_target_pairs={{0,16},{8,24},{16,0},{24,8},{1,17},{9,25},{17,1},{25,9},{2,18},{10... | collective-permute-start | bytes 589832 | tf_op jit(solution)/shard_map/ppermute | solution.py:460
  148.8 9.2 %collective-permute-start.16 = (bf16[2,48,1024]{2,1,0:T(8,128)(2,1)}, bf16[2,48,1024]{2,1,0:T(8,128)(2,1)S(1)}, u32[]{:S(2)}, u32[]{:S(2)}) collective-permute-start(bf16[2,48,1024]{2,1,0:T(8,128)(2,1)} %get-tuple-element.91), channel_id=1, source_target_pairs={{0,24},{8,0},{16,8},{24,16},{1,25},{9,1},{17,9},{25,17},{2,26},{10... | collective-permute-start | bytes 589832 | tf_op jit(solution)/shard_map/ppermute | solution.py:460
  149.9 15.5 %all-to-all-start.4 = ((bf16[4,2,48,1024]{3,2,1,0:T(8,128)(2,1)}), bf16[4,2,48,1024]{3,2,1,0:T(8,128)(2,1)S(1)}, u32[]{:S(2)}, u32[]{:S(2)}) async-start(bf16[4,2,48,1024]{3,2,1,0:T(8,128)(2,1)} %get-tuple-element.93), calls=%async_computation.4 | async-start | bytes 1572864 | tf_op jit(solution)/shard_map/all_to_all | solution.py:461
  159.1 27.3 %copy-start.2 = (f32[2,128]{1,0:T(2,128)S(1)}, f32[2,128]{1,0:T(2,128)}, u32[]{:S(2)}) copy-start(f32[2,128]{1,0:T(2,128)} %find_roots.3) | copy-start | bytes 3076
  159.1 27.3 %copy-start.3 = (f32[1,128]{1,0:T(1,128)S(1)}, f32[1,128]{1,0:T(1,128)}, u32[]{:S(2)}) copy-start(f32[1,128]{1,0:T(1,128)} %find_roots.4) | copy-start | bytes 1540
  165.9 31.7 %collective-permute-start.17 = (f32[2,48,1024]{2,1,0:T(8,128)S(1)}, f32[2,48,1024]{2,1,0:T(8,128)S(1)}, u32[]{:S(2)}, u32[]{:S(2)}) collective-permute-start(f32[2,48,1024]{2,1,0:T(8,128)S(1)} %pad_maximum_fusion), channel_id=1, source_target_pairs={{0,1},{1,0},{2,3},{3,2},{4,5},{5,4},{6,7},{7,6},{8,9},{9,8},{10,11... | collective-permute-start | bytes 1179656 | tf_op jit(solution)/shard_map/ppermute | solution.py:474
  187.7 9.9 %all-to-all-start.3 = ((f32[16,4,128]{2,1,0:T(4,128)}), f32[16,4,128]{2,1,0:T(4,128)S(1)}, u32[]{:S(2)}, u32[]{:S(2)}) async-start(f32[16,4,128]{2,1,0:T(4,128)} %broadcast_in_dim.61), calls=%async_computation.3 | async-start | bytes 65536 | tf_op jit(solution)/shard_map/all_to_all | solution.py:363
  (3 other events, 5.7 us)

commit v9 on v8

--- a/solution.py
+++ b/solution.py
@@ -60,8 +60,8 @@
 
             def far(i, sums):
                 first, second = sums
-                for half in range(2):
-                    block = 2 * i + half
+                for third in range(3):
+                    block = 3 * i + third
                     block = jnp.where(block >= near_block, block + 2, block)
                     some = None
                     for u in range(BLOCK):
@@ -77,7 +77,7 @@
 
             zero = jnp.zeros((GROUP, LANES), F32)
             sums = lax.fori_loop(0, 2, near, (zero, zero))
-            first, second = lax.fori_loop(0, (blocks - 2) // 2, far, sums)
+            first, second = lax.fori_loop(0, (blocks - 2) // 3, far, sums)
             sum_inverse = jnp.sum(first, axis=1, keepdims=True)
             sum_square = jnp.sum(second, axis=1, keepdims=True)
             nearest = jnp.minimum(jnp.abs(lo_ref[here, :] - t), jnp.abs(hi_ref[here, :] - t))
@@ -143,7 +143,16 @@
         sum_inverse, sum_square, nearest = sums_at(t)
         limit = 0.5 * nearest
         t = t - jnp.clip((1.0 + sum_inverse) / sum_square, -limit, limit)
-    norm = lax.rsqrt(sums_at(t)[1])
+
+    def squares(r, total):
+        for u in range(unroll):
+            row = pl.ds(r * unroll + u, 1)
+            inverse = 1.0 / ((pw_ref[0, row, :] - c) - t)
+            total = total + w2_ref[row, :] * inverse * inverse
+        return total
+
+    square = lax.fori_loop(0, w2_ref.shape[0] // unroll, squares, zero)
+    norm = lax.rsqrt(jnp.sum(square, axis=1, keepdims=True))
     pad = jnp.zeros((LANES - count, LANES), F32)
     out_ref[0:1, :] = jnp.concatenate([t, pad], axis=0).T[0:1, :]
     out_ref[1:2, :] = jnp.concatenate([jnp.broadcast_to(norm, (count, LANES)), pad], axis=0).T[0:1, :]

time: 201 us -> 200 us (level)
  no operation moved by 1% of the time
where the time goes in v9:
time: 200 us; the launch traced here: 199 us
  Pallas kernels  109 us (54%)
  starting transfers between devices  48.1 us (24%)
  waiting for transfers between devices  21.6 us (11%)
  local copies, waits for them, and re-layouts  9.95 us (5%)
  other arithmetic  9.21 us (5%)
    pallas_call x3, Pallas kernels, find_roots(): pl.pallas_call(root_kernel, in_specs=[pl.BlockSpec(memory_space=pltpu.SME...  71 us
    pallas_call x1, Pallas kernels, panel_product(): pl.pallas_call(matmul_kernel, in_specs=[pl.BlockSpec(memory_space=pltpu.S...  21.6 us
    all_to_all x3, starting transfers between devices, copies(): lax.all_to_all(jnp.broadcast_to(value[None], (size, *value.shape)), axis,...  18.7 us
    ppermute x6, starting transfers between devices, merge(): eigen[half].append(lax.ppermute(cut[half][shift], axes[half], ring(shift)))  9.47 us
    pallas_call x1, Pallas kernels, panel_roots(): pl.pallas_call(panel_kernel, out_shape=jax.ShapeDtypeStruct((2, LANES), F...  7.08 us
    all_to_all x3, waiting for transfers between devices, copies(): lax.all_to_all(jnp.broadcast_to(value[None], (size, *value.shape)), axis,...  6.74 us
    pallas_call x1, Pallas kernels, turn_blocks(): pl.pallas_call(turn_kernel, in_specs=[pl.BlockSpec(memory_space=pltpu.SME...  6.34 us
    all_to_all x1, waiting for transfers between devices, merge(): turned = lax.all_to_all(sums[5], 'z', 0, 0, tiled=True)  6.26 us
  transfers between devices with their start and end apart: 23, of which 9 were waited for; matrix products, arithmetic and copies ran while one was open for 7% of the time, Pallas kernels for 44%

profile of v9, /device:TPU:1, one launch (start us, length us, event | category | flops | bytes accessed | tf_op | source)
XLA Modules:
  0.0 199.2 jit_solution(12183330190632656034)
XLA Ops:
  2.2 8.4 %all-to-all-start = ((f32[16,2,32,128]{3,2,1,0:T(8,128)}), f32[16,2,32,128]{3,2,1,0:T(8,128)S(1)}, u32[]{:S(2)}, u32[]{:S(2)}) async-start(f32[16,2,32,128]{3,2,1,0:T(8,128)} %broadcast_in_dim.55), calls=%async_computation | async-start | bytes 1048576 | tf_op jit(solution)/shard_map/all_to_all | solution.py:372
  11.4 2.1 %select_reduce_fusion.1 = (f32[128]{0:T(128)S(1)}, f32[128]{0:T(128)S(1)}) fusion(f32[8192]{0:T(1024)} %param.9, s32[128]{0:T(128)S(1)} %dynamic-slice_subtract_fusion, f32[8192]{0:T(1024)} %param.10), kind=kLoop, calls=%fused_computation.1 | loop fusion | flops 5242624 | bytes 67072 | tf_op jit(solution)/shard_map/reduce_sum | solution.py:403
  14.3 6.3 %turn_blocks.1 = (bf16[192,2048]{1,0:T(8,128)(2,1)}, bf16[192,2048]{1,0:T(8,128)(2,1)}, bf16[192,2048]{1,0:T(8,128)(2,1)}, bf16[192,2048]{1,0:T(8,128)(2,1)}, bf...) custom-call(s32[2]{0:T(128)} %get-tuple-element.125.place_ref, ...), custom_call_target="tpu_custom_call" | custom-call | flops 50000000 | bytes 1048576 | tf_op jit(solution)/shard_map/turn_blocks/pallas_call | solution.py:245
  21.1 1.1 collective-permute-start
  23.4 6.0 %all-to-all-start.1 = ((f32[8,2,16]{2,1,0:T(2,128)}), f32[8,2,16]{2,1,0:T(2,128)S(1)}, u32[]{:S(2)}, u32[]{:S(2)}) async-start(f32[8,2,16]{2,1,0:T(2,128)} %copy.23), calls=%async_computation.1 | async-start | bytes 16384 | tf_op jit(solution)/shard_map/all_to_all | solution.py:411
  30.2 2.4 %collective-permute-start.1 = (bf16[192,2048]{1,0:T(8,128)(2,1)}, bf16[192,2048]{1,0:T(8,128)(2,1)}, u32[]{:S(2)}, u32[]{:S(2)}) collective-permute-start(bf16[192,2048]{1,0:T(8,128)(2,1)} %get-tuple-element.58), channel_id=1, source_target_pairs={{0,64},{32,96},{64,0},{96,32},{1,65},{33,97},{65,1},{97,33},{2,66}... | collective-permute-start | bytes 2359304 | tf_op jit(solution)/shard_map/ppermute | solution.py:415
  32.6 1.2 collective-permute-start.2
  33.8 1.2 collective-permute-start.3
  34.9 2.4 %collective-permute-start.4 = (bf16[192,2048]{1,0:T(8,128)(2,1)}, bf16[192,2048]{1,0:T(8,128)(2,1)}, u32[]{:S(2)}, u32[]{:S(2)}) collective-permute-start(bf16[192,2048]{1,0:T(8,128)(2,1)} %get-tuple-element.62), channel_id=1, source_target_pairs={{0,16},{8,24},{16,0},{24,8},{1,17},{9,25},{17,1},{25,9},{2,18},{10... | collective-permute-start | bytes 2359304 | tf_op jit(solution)/shard_map/ppermute | solution.py:415
  37.3 3.3 %pick_columns.1 = f32[8,128]{1,0:T(8,128)} custom-call(s32[4,128]{1,0:T(4,128)} %constant_dynamic-slice_fusion.4.index_ref, f32[2,512,128]{2,1,0:T(8,128)} %bitcast.57), custom_call_target="tpu_custom_call" | custom-call | flops 50000000 | bytes 1048576 | tf_op jit(solution)/shard_map/pick_columns/pallas_call | solution.py:192
  41.2 7.1 %panel_roots.1 = f32[2,128]{1,0:T(2,128)} custom-call(f32[2,512,128]{2,1,0:T(8,128)} %bitcast.58, f32[2,128]{1,0:T(2,128)} %pad.4.root_ref), custom_call_target="tpu_custom_call" | custom-call | flops 52428800 | bytes 1048576 | tf_op jit(solution)/shard_map/panel_roots/pallas_call | solution.py:163
  48.3 1.2 collective-permute-start.5
  51.3 6.7 %all-to-all-start.2 = ((f32[128,11,128]{2,1,0:T(8,128)}), f32[128,11,128]{2,1,0:T(8,128)S(1)}, u32[]{:S(2)}, u32[]{:S(2)}) async-start(f32[128,11,128]{2,1,0:T(8,128)} %broadcast_in_dim.59), calls=%async_computation.2 | async-start | bytes 2097152 | tf_op jit(solution)/shard_map/all_to_all | solution.py:372
  60.1 34.7 %find_roots.3 = f32[2,128]{1,0:T(2,128)} custom-call(s32[1]{0:T(128)} %bitcast.7.rank_ref, f32[2,512,128]{2,1,0:T(8,128)} %bitcast.59, f32[4,2,128]{2,1,0:T(2,128)} %slice.70.root_ref), custom_call_target="tpu_custom_call" | custom-call | flops 503316480 | bytes 1048576 | tf_op jit(solution)/shard_map/find_roots/pallas_call | solution.py:101
  94.9 1.1 collective-permute-start.6
  97.1 18.1 %find_roots.4 = f32[1,128]{1,0:T(1,128)} custom-call(s32[1]{0:T(128)S(6)} %add.215.rank_ref, f32[2,512,128]{2,1,0:T(8,128)} %bitcast.60, f32[4,1,128]{2,1,0:T(1,128)} %get-tuple-element.123.root_ref), custom_call_target="tpu_custom_call" | custom-call | flops 251658240 | bytes 1048576 | tf_op jit(solution)/shard_map/find_roots/pallas_call | solution.py:101
  118.1 1.1 collective-permute-done.9.refs_7_
  119.2 1.1 collective-permute-done.11.refs_13_
  120.4 1.1 collective-permute-done.12.refs_14_
  121.5 1.1 collective-permute-done.13.refs_15_
  123.5 21.6 %panel_product.1 = (f32[2,48,1024]{2,1,0:T(8,128)}, bf16[2,48,1024]{2,1,0:T(8,128)(2,1)}, bf16[2,48,1024]{2,1,0:T(8,128)(2,1)}, bf16[2,48,1024]{2,1,0:T(8,128)(2...) custom-call(s32[2]{0:T(128)} %get-tuple-element.126.place_ref, ...), custom_call_target="tpu_custom_call" | custom-call | flops 12884901888 | bytes 1048576 | tf_op jit(solution)/shard_map/panel_product/pallas_call | solution.py:354
  145.9 2.4 %collective-permute-start.15 = (bf16[2,48,1024]{2,1,0:T(8,128)(2,1)}, bf16[2,48,1024]{2,1,0:T(8,128)(2,1)S(1)}, u32[]{:S(2)}, u32[]{:S(2)}) collective-permute-start(bf16[2,48,1024]{2,1,0:T(8,128)(2,1)} %get-tuple-element.90), channel_id=1, source_target_pairs={{0,16},{8,24},{16,0},{24,8},{1,17},{9,25},{17,1},{25,9},{2,18},{10... | collective-permute-start | bytes 589832 | tf_op jit(solution)/shard_map/ppermute | solution.py:469
  148.3 1.2 collective-permute-start.16
  149.5 4.4 %all-to-all-start.4 = ((bf16[4,2,48,1024]{3,2,1,0:T(8,128)(2,1)}), bf16[4,2,48,1024]{3,2,1,0:T(8,128)(2,1)S(1)}, u32[]{:S(2)}, u32[]{:S(2)}) async-start(bf16[4,2,48,1024]{3,2,1,0:T(8,128)(2,1)} %get-tuple-element.93), calls=%async_computation.4 | async-start | bytes 1572864 | tf_op jit(solution)/shard_map/all_to_all | solution.py:470
  153.9 3.7 %collective-permute-done.15 = bf16[2,48,1024]{2,1,0:T(8,128)(2,1)S(1)} collective-permute-done((bf16[2,48,1024]{2,1,0:T(8,128)(2,1)}, bf16[2,48,1024]{2,1,0:T(8,128)(2,1)S(1)}, u32[]{:S(2)}, u32[]{:S(2)}) %collective-permute-start.15) | collective-permute-done | bytes 196640 | tf_op jit(solution)/shard_map/ppermute | solution.py:469
  157.6 1.1 convert_add_fusion
  158.7 6.3 %all-to-all-done.4 = bf16[4,2,48,1024]{3,2,1,0:T(8,128)(2,1)S(1)} async-done(((bf16[4,2,48,1024]{3,2,1,0:T(8,128)(2,1)}), bf16[4,2,48,1024]{3,2,1,0:T(8,128)(2,1)S(1)}, u32[]{:S(2)}, u32[]{:S(2)}) %all-to-all-start.4) | async-done | bytes 786464 | tf_op jit(solution)/shard_map/all_to_all | solution.py:470
  165.4 2.2 %collective-permute-start.17 = (f32[2,48,1024]{2,1,0:T(8,128)S(1)}, f32[2,48,1024]{2,1,0:T(8,128)S(1)}, u32[]{:S(2)}, u32[]{:S(2)}) collective-permute-start(f32[2,48,1024]{2,1,0:T(8,128)S(1)} %pad_maximum_fusion), channel_id=1, source_target_pairs={{0,1},{1,0},{2,3},{3,2},{4,5},{5,4},{6,7},{7,6},{8,9},{9,8},{10,11... | collective-permute-start | bytes 1179656 | tf_op jit(solution)/shard_map/ppermute | solution.py:483
  167.7 18.1 %find_roots.5 = f32[1,128]{1,0:T(1,128)} custom-call(s32[1]{0:T(128)S(6)} %add.216.rank_ref, f32[2,512,128]{2,1,0:T(8,128)} %bitcast.61, f32[4,1,128]{2,1,0:T(1,128)} %get-tuple-element.124.root_ref), custom_call_target="tpu_custom_call" | custom-call | flops 251658240 | bytes 1048576 | tf_op jit(solution)/shard_map/find_roots/pallas_call | solution.py:101
  187.1 3.5 %all-to-all-start.3 = ((f32[16,4,128]{2,1,0:T(4,128)}), f32[16,4,128]{2,1,0:T(4,128)S(1)}, u32[]{:S(2)}, u32[]{:S(2)}) async-start(f32[16,4,128]{2,1,0:T(4,128)} %broadcast_in_dim.61), calls=%async_computation.3 | async-start | bytes 65536 | tf_op jit(solution)/shard_map/all_to_all | solution.py:372
  190.6 6.4 %all-to-all-done.3 = f32[16,4,128]{2,1,0:T(4,128)S(1)} async-done(((f32[16,4,128]{2,1,0:T(4,128)}), f32[16,4,128]{2,1,0:T(4,128)S(1)}, u32[]{:S(2)}, u32[]{:S(2)}) %all-to-all-start.3) | async-done | bytes 32800 | tf_op jit(solution)/shard_map/all_to_all | solution.py:372
  197.1 1.5 copy.27
  (94 shorter events, 17.9 us)
Async XLA Ops:
  0.6 21.5 %copy-start.1 = (s32[2,2048]{1,0:T(2,128)S(1)}, s32[2,2048]{1,0:T(2,128)}, u32[]{:S(2)}) copy-start(s32[2,2048]{1,0:T(2,128)} %param.12) | copy-start | bytes 49156
  2.2 18.8 %all-to-all-start = ((f32[16,2,32,128]{3,2,1,0:T(8,128)}), f32[16,2,32,128]{3,2,1,0:T(8,128)S(1)}, u32[]{:S(2)}, u32[]{:S(2)}) async-start(f32[16,2,32,128]{3,2,1,0:T(8,128)} %broadcast_in_dim.55), calls=%async_computation | async-start | bytes 1048576 | tf_op jit(solution)/shard_map/all_to_all | solution.py:372
  20.7 74.2 %copy-start.4 = (bf16[192,2048]{1,0:T(8,128)(2,1)S(1)}, bf16[192,2048]{1,0:T(8,128)(2,1)}, u32[]{:S(2)}) copy-start(bf16[192,2048]{1,0:T(8,128)(2,1)} %get-tuple-element.78.refs_0_) | copy-start | bytes 2359300
  20.7 75.2 %copy-start.5 = (bf16[192,2048]{1,0:T(8,128)(2,1)S(1)}, bf16[192,2048]{1,0:T(8,128)(2,1)}, u32[]{:S(2)}) copy-start(bf16[192,2048]{1,0:T(8,128)(2,1)} %get-tuple-element.83.refs_8_) | copy-start | bytes 2359300
  21.1 27.3 %collective-permute-start = (bf16[192,2048]{1,0:T(8,128)(2,1)}, bf16[192,2048]{1,0:T(8,128)(2,1)S(1)}, u32[]{:S(2)}, u32[]{:S(2)}) collective-permute-start(bf16[192,2048]{1,0:T(8,128)(2,1)} %get-tuple-element.57), channel_id=1, source_target_pairs={{0,32},{32,64},{64,96},{96,0},{1,33},{33,65},{65,97},{97,1},{2,34}... | collective-permute-start | bytes 2359304 | tf_op jit(solution)/shard_map/ppermute | solution.py:415
  23.4 17.3 %all-to-all-start.1 = ((f32[8,2,16]{2,1,0:T(2,128)}), f32[8,2,16]{2,1,0:T(2,128)S(1)}, u32[]{:S(2)}, u32[]{:S(2)}) async-start(f32[8,2,16]{2,1,0:T(2,128)} %copy.23), calls=%async_computation.1 | async-start | bytes 16384 | tf_op jit(solution)/shard_map/all_to_all | solution.py:411
  30.2 64.7 %collective-permute-start.1 = (bf16[192,2048]{1,0:T(8,128)(2,1)}, bf16[192,2048]{1,0:T(8,128)(2,1)}, u32[]{:S(2)}, u32[]{:S(2)}) collective-permute-start(bf16[192,2048]{1,0:T(8,128)(2,1)} %get-tuple-element.58), channel_id=1, source_target_pairs={{0,64},{32,96},{64,0},{96,32},{1,65},{33,97},{65,1},{97,33},{2,66}... | collective-permute-start | bytes 2359304 | tf_op jit(solution)/shard_map/ppermute | solution.py:415
  32.6 63.4 %collective-permute-start.2 = (bf16[192,2048]{1,0:T(8,128)(2,1)}, bf16[192,2048]{1,0:T(8,128)(2,1)}, u32[]{:S(2)}, u32[]{:S(2)}) collective-permute-start(bf16[192,2048]{1,0:T(8,128)(2,1)} %get-tuple-element.59), channel_id=1, source_target_pairs={{0,96},{32,0},{64,32},{96,64},{1,97},{33,1},{65,33},{97,65},{2,98}... | collective-permute-start | bytes 2359304 | tf_op jit(solution)/shard_map/ppermute | solution.py:415
  33.8 62.3 %collective-permute-start.3 = (bf16[192,2048]{1,0:T(8,128)(2,1)}, bf16[192,2048]{1,0:T(8,128)(2,1)}, u32[]{:S(2)}, u32[]{:S(2)}) collective-permute-start(bf16[192,2048]{1,0:T(8,128)(2,1)} %get-tuple-element.61), channel_id=1, source_target_pairs={{0,8},{8,16},{16,24},{24,0},{1,9},{9,17},{17,25},{25,1},{2,10},{10... | collective-permute-start | bytes 2359304 | tf_op jit(solution)/shard_map/ppermute | solution.py:415
  34.9 61.1 %collective-permute-start.4 = (bf16[192,2048]{1,0:T(8,128)(2,1)}, bf16[192,2048]{1,0:T(8,128)(2,1)}, u32[]{:S(2)}, u32[]{:S(2)}) collective-permute-start(bf16[192,2048]{1,0:T(8,128)(2,1)} %get-tuple-element.62), channel_id=1, source_target_pairs={{0,16},{8,24},{16,0},{24,8},{1,17},{9,25},{17,1},{25,9},{2,18},{10... | collective-permute-start | bytes 2359304 | tf_op jit(solution)/shard_map/ppermute | solution.py:415
  48.3 3.0 %copy-start.6 = (bf16[192,2048]{1,0:T(8,128)(2,1)}, bf16[192,2048]{1,0:T(8,128)(2,1)S(1)}, u32[]{:S(2)}) copy-start(bf16[192,2048]{1,0:T(8,128)(2,1)S(1)} %collective-permute-done.refs_1_) | copy-start | bytes 2359300
  48.3 47.7 %collective-permute-start.5 = (bf16[192,2048]{1,0:T(8,128)(2,1)}, bf16[192,2048]{1,0:T(8,128)(2,1)}, u32[]{:S(2)}, u32[]{:S(2)}) collective-permute-start(bf16[192,2048]{1,0:T(8,128)(2,1)} %get-tuple-element.63), channel_id=1, source_target_pairs={{0,24},{8,0},{16,8},{24,16},{1,25},{9,1},{17,9},{25,17},{2,26},{10... | collective-permute-start | bytes 2359304 | tf_op jit(solution)/shard_map/ppermute | solution.py:415
  51.3 44.7 %all-to-all-start.2 = ((f32[128,11,128]{2,1,0:T(8,128)}), f32[128,11,128]{2,1,0:T(8,128)S(1)}, u32[]{:S(2)}, u32[]{:S(2)}) async-start(f32[128,11,128]{2,1,0:T(8,128)} %broadcast_in_dim.59), calls=%async_computation.2 | async-start | bytes 2097152 | tf_op jit(solution)/shard_map/all_to_all | solution.py:372
  94.9 21.3 %collective-permute-start.6 = (bf16[192,2048]{1,0:T(8,128)(2,1)S(1)}, bf16[192,2048]{1,0:T(8,128)(2,1)}, u32[]{:S(2)}, u32[]{:S(2)}) collective-permute-start(bf16[192,2048]{1,0:T(8,128)(2,1)S(1)} %copy-done.4), channel_id=1, source_target_pairs={{0,1},{1,0},{2,3},{3,2},{4,5},{5,4},{6,7},{7,6},{8,9},{9,8},{10,11... | collective-permute-start | bytes 2359304 | tf_op jit(solution)/shard_map/ppermute | solution.py:416
  95.9 20.4 %collective-permute-start.10 = (bf16[192,2048]{1,0:T(8,128)(2,1)S(1)}, bf16[192,2048]{1,0:T(8,128)(2,1)}, u32[]{:S(2)}, u32[]{:S(2)}) collective-permute-start(bf16[192,2048]{1,0:T(8,128)(2,1)S(1)} %copy-done.5), channel_id=1, source_target_pairs={{0,1},{1,0},{2,3},{3,2},{4,5},{5,4},{6,7},{7,6},{8,9},{9,8},{10,11... | collective-permute-start | bytes 2359304 | tf_op jit(solution)/shard_map/ppermute | solution.py:416
  96.1 20.6 %collective-permute-start.7 = (bf16[192,2048]{1,0:T(8,128)(2,1)}, bf16[192,2048]{1,0:T(8,128)(2,1)}, u32[]{:S(2)}, u32[]{:S(2)}) collective-permute-start(bf16[192,2048]{1,0:T(8,128)(2,1)} %copy-done.6), channel_id=1, source_target_pairs={{0,1},{1,0},{2,3},{3,2},{4,5},{5,4},{6,7},{7,6},{8,9},{9,8},{10,11... | collective-permute-start | bytes 2359304 | tf_op jit(solution)/shard_map/ppermute | solution.py:440
  115.5 2.6 %collective-permute-start.8 = (bf16[192,2048]{1,0:T(8,128)(2,1)}, bf16[192,2048]{1,0:T(8,128)(2,1)S(1)}, u32[]{:S(2)}, u32[]{:S(2)}) collective-permute-start(bf16[192,2048]{1,0:T(8,128)(2,1)} %collective-permute-done.1.refs_2_), channel_id=1, source_target_pairs={{0,1},{1,0},{2,3},{3,2},{4,5},{5,4},{6,7},{7,6},{8,9},{9,8},{10,11... | collective-permute-start | bytes 2359304 | tf_op jit(solution)/shard_map/ppermute | solution.py:440
  115.8 3.4 %collective-permute-start.9 = (bf16[192,2048]{1,0:T(8,128)(2,1)}, bf16[192,2048]{1,0:T(8,128)(2,1)S(1)}, u32[]{:S(2)}, u32[]{:S(2)}) collective-permute-start(bf16[192,2048]{1,0:T(8,128)(2,1)} %collective-permute-done.2.refs_3_), channel_id=1, source_target_pairs={{0,1},{1,0},{2,3},{3,2},{4,5},{5,4},{6,7},{7,6},{8,9},{9,8},{10,11... | collective-permute-start | bytes 2359304 | tf_op jit(solution)/shard_map/ppermute | solution.py:440
  116.1 4.2 %collective-permute-start.11 = (bf16[192,2048]{1,0:T(8,128)(2,1)}, bf16[192,2048]{1,0:T(8,128)(2,1)S(1)}, u32[]{:S(2)}, u32[]{:S(2)}) collective-permute-start(bf16[192,2048]{1,0:T(8,128)(2,1)} %collective-permute-done.3.refs_9_), channel_id=1, source_target_pairs={{0,1},{1,0},{2,3},{3,2},{4,5},{5,4},{6,7},{7,6},{8,9},{9,8},{10,11... | collective-permute-start | bytes 2359304 | tf_op jit(solution)/shard_map/ppermute | solution.py:440
  116.3 5.2 %collective-permute-start.12 = (bf16[192,2048]{1,0:T(8,128)(2,1)}, bf16[192,2048]{1,0:T(8,128)(2,1)S(1)}, u32[]{:S(2)}, u32[]{:S(2)}) collective-permute-start(bf16[192,2048]{1,0:T(8,128)(2,1)} %collective-permute-done.4.refs_10_), channel_id=1, source_target_pairs={{0,1},{1,0},{2,3},{3,2},{4,5},{5,4},{6,7},{7,6},{8,9},{9,8},{10,11... | collective-permute-start | bytes 2359304 | tf_op jit(solution)/shard_map/ppermute | solution.py:440
  116.6 6.0 %collective-permute-start.13 = (bf16[192,2048]{1,0:T(8,128)(2,1)}, bf16[192,2048]{1,0:T(8,128)(2,1)S(1)}, u32[]{:S(2)}, u32[]{:S(2)}) collective-permute-start(bf16[192,2048]{1,0:T(8,128)(2,1)} %collective-permute-done.5.refs_11_), channel_id=1, source_target_pairs={{0,1},{1,0},{2,3},{3,2},{4,5},{5,4},{6,7},{7,6},{8,9},{9,8},{10,11... | collective-permute-start | bytes 2359304 | tf_op jit(solution)/shard_map/ppermute | solution.py:440
  118.1 5.2 %copy-start.7 = (bf16[192,2048]{1,0:T(8,128)(2,1)}, bf16[192,2048]{1,0:T(8,128)(2,1)S(1)}, u32[]{:S(2)}) copy-start(bf16[192,2048]{1,0:T(8,128)(2,1)S(1)} %collective-permute-done.8.refs_6_) | copy-start | bytes 2359300
  119.2 4.1 %copy-start.8 = (bf16[192,2048]{1,0:T(8,128)(2,1)}, bf16[192,2048]{1,0:T(8,128)(2,1)S(1)}, u32[]{:S(2)}) copy-start(bf16[192,2048]{1,0:T(8,128)(2,1)S(1)} %collective-permute-done.9.refs_7_) | copy-start | bytes 2359300
  145.2 20.0 %copy-start = (f32[2,48,1024]{2,1,0:T(8,128)S(1)}, f32[2,48,1024]{2,1,0:T(8,128)}, u32[]{:S(2)}) copy-start(f32[2,48,1024]{2,1,0:T(8,128)} %get-tuple-element.92) | copy-start | bytes 1179652
  145.2 8.7 %collective-permute-start.14 = (bf16[2,48,1024]{2,1,0:T(8,128)(2,1)}, bf16[2,48,1024]{2,1,0:T(8,128)(2,1)S(1)}, u32[]{:S(2)}, u32[]{:S(2)}) collective-permute-start(bf16[2,48,1024]{2,1,0:T(8,128)(2,1)} %get-tuple-element.89), channel_id=1, source_target_pairs={{0,8},{8,16},{16,24},{24,0},{1,9},{9,17},{17,25},{25,1},{2,10},{10... | collective-permute-start | bytes 589832 | tf_op jit(solution)/shard_map/ppermute | solution.py:469
  145.9 11.6 %collective-permute-start.15 = (bf16[2,48,1024]{2,1,0:T(8,128)(2,1)}, bf16[2,48,1024]{2,1,0:T(8,128)(2,1)S(1)}, u32[]{:S(2)}, u32[]{:S(2)}) collective-permute-start(bf16[2,48,1024]{2,1,0:T(8,128)(2,1)} %get-tuple-element.90), channel_id=1, source_target_pairs={{0,16},{8,24},{16,0},{24,8},{1,17},{9,25},{17,1},{25,9},{2,18},{10... | collective-permute-start | bytes 589832 | tf_op jit(solution)/shard_map/ppermute | solution.py:469
  148.3 9.2 %collective-permute-start.16 = (bf16[2,48,1024]{2,1,0:T(8,128)(2,1)}, bf16[2,48,1024]{2,1,0:T(8,128)(2,1)S(1)}, u32[]{:S(2)}, u32[]{:S(2)}) collective-permute-start(bf16[2,48,1024]{2,1,0:T(8,128)(2,1)} %get-tuple-element.91), channel_id=1, source_target_pairs={{0,24},{8,0},{16,8},{24,16},{1,25},{9,1},{17,9},{25,17},{2,26},{10... | collective-permute-start | bytes 589832 | tf_op jit(solution)/shard_map/ppermute | solution.py:469
  149.5 15.5 %all-to-all-start.4 = ((bf16[4,2,48,1024]{3,2,1,0:T(8,128)(2,1)}), bf16[4,2,48,1024]{3,2,1,0:T(8,128)(2,1)S(1)}, u32[]{:S(2)}, u32[]{:S(2)}) async-start(bf16[4,2,48,1024]{3,2,1,0:T(8,128)(2,1)} %get-tuple-element.93), calls=%async_computation.4 | async-start | bytes 1572864 | tf_op jit(solution)/shard_map/all_to_all | solution.py:470
  158.7 27.2 %copy-start.2 = (f32[2,128]{1,0:T(2,128)S(1)}, f32[2,128]{1,0:T(2,128)}, u32[]{:S(2)}) copy-start(f32[2,128]{1,0:T(2,128)} %find_roots.3) | copy-start | bytes 3076
  158.7 27.2 %copy-start.3 = (f32[1,128]{1,0:T(1,128)S(1)}, f32[1,128]{1,0:T(1,128)}, u32[]{:S(2)}) copy-start(f32[1,128]{1,0:T(1,128)} %find_roots.4) | copy-start | bytes 1540
  165.4 31.6 %collective-permute-start.17 = (f32[2,48,1024]{2,1,0:T(8,128)S(1)}, f32[2,48,1024]{2,1,0:T(8,128)S(1)}, u32[]{:S(2)}, u32[]{:S(2)}) collective-permute-start(f32[2,48,1024]{2,1,0:T(8,128)S(1)} %pad_maximum_fusion), channel_id=1, source_target_pairs={{0,1},{1,0},{2,3},{3,2},{4,5},{5,4},{6,7},{7,6},{8,9},{9,8},{10,11... | collective-permute-start | bytes 1179656 | tf_op jit(solution)/shard_map/ppermute | solution.py:483
  187.1 9.9 %all-to-all-start.3 = ((f32[16,4,128]{2,1,0:T(4,128)}), f32[16,4,128]{2,1,0:T(4,128)S(1)}, u32[]{:S(2)}, u32[]{:S(2)}) async-start(f32[16,4,128]{2,1,0:T(4,128)} %broadcast_in_dim.61), calls=%async_computation.3 | async-start | bytes 65536 | tf_op jit(solution)/shard_map/all_to_all | solution.py:372
  (3 other events, 5.7 us)
